TPU v7x, 32 devices: a whole 2x2x4 slice. The times are simulated.
32 devices in a mesh: image: 8 (over z, x), space: 4 (over y, core).
Axes of the slice: x: 2, y: 2, z: 4, core: 2. Of those that a mesh axis runs over, the one named last changes fastest.
Arguments:
- magnet: float32 [16, 3, 8, 256, 256], P('image', None, None, 'space'), may hold values from -1 to 1, as said below
- anisotropy: float32 [256], P('space'), may hold values from 0.25 to 10
- kernel: float32 [6, 16, 512, 512], P(None, 'space'), as said below
Outputs:
- updated_magnet: float32 [16, 3, 8, 256, 256], P('image', None, None, 'space')
- band_force: float32 [16, 3, 8, 256, 256], P('image', None, None, 'space')
- energy: float32 [16], P('image')
Inputs may be any that keep to these rules, and one draw needn't show every extreme that they name: `magnet`: each cell's three components form a unit vector. `kernel`: each component is even under k -> -k modulo the padded length along every frequency index, except that xy is odd along x and y, xz odd along x and z, and yz odd along y and z.
All inputs are finite; a program needn't handle non-finite values.
Results may differ from a plain program's by a relative error of at most 0.0003.
Values sent between devices are 32-bit elements; how exact they have to be, the bound alone decides.
A program may use at most 256 MiB of HBM per device.

v0:
```python
import functools
import math

import jax
import jax.numpy as jnp
import numpy as np
from jax import lax
from jax.experimental import pallas as pl
from jax.experimental.pallas import tpu as pltpu
from jax.sharding import PartitionSpec as P

exchange_strength = 0.25
chiral_strength = 0.3
spring_strength = 10.0
step_limit = 1.0
rotation_limit = 0.5
epsilon = 1e-06


def extended(cells, sides, width):
    for axis, dim in sides:
        count = lax.axis_size(axis)
        ends = count - 1
        head = lax.slice_in_dim(cells, 0, width, axis=dim)
        tail = lax.slice_in_dim(cells, cells.shape[dim] - width, cells.shape[dim], axis=dim)
        cells = jnp.concatenate(
            [
                lax.ppermute(tail, axis, [(i, (i + 1) % count) for i in range(ends)]),
                cells,
                lax.ppermute(head, axis, [((i + 1) % count, i) for i in range(ends)]),
            ],
            axis=dim,
        )
    return cells


def lift_axes(values):
    return values[:, None, None, None, None]


def total_cells(values):
    return jnp.sum(values, axis=tuple(range(1, values.ndim)))


def project(vector, magnet):
    return vector - jnp.sum(vector * magnet, axis=1, keepdims=True) * magnet


def angle_squared(first, second):
    normal_part = jnp.cross(first, second, axis=1)
    sine_value = jnp.sqrt(jnp.sum(normal_part * normal_part, axis=1))
    cosine = jnp.sum(first * second, axis=1)
    return jnp.arctan2(sine_value, cosine) ** 2


def tangent_weights(energy_total, energy_next, energy_prior):
    rise_next = energy_next - energy_total
    rise_prior = energy_total - energy_prior
    upward = (rise_next > 0) & (rise_prior > 0)
    downward = (rise_next < 0) & (rise_prior < 0)
    larger = jnp.maximum(jnp.abs(rise_next), jnp.abs(rise_prior))
    smaller = jnp.minimum(jnp.abs(rise_next), jnp.abs(rise_prior))
    toward_next = energy_next > energy_prior
    weight_next = jnp.where(
        upward, 1.0, jnp.where(downward, 0.0, jnp.where(toward_next, larger, smaller))
    )
    weight_prior = jnp.where(
        upward, 0.0, jnp.where(downward, 1.0, jnp.where(toward_next, smaller, larger))
    )
    return (weight_next, weight_prior)


def split_limbs(values):
    upper = values.astype(jnp.bfloat16)
    return upper, (values - upper.astype(jnp.float32)).astype(jnp.bfloat16)


def table_limbs(table):
    upper = table.astype(np.float32).astype(jnp.bfloat16)
    lower = (table - upper.astype(np.float64)).astype(np.float32).astype(jnp.bfloat16)
    return np.stack([upper, lower])


def parity_table(count):
    position = np.arange(count)[:, None]
    slot = np.arange(count)[None, :]
    turn = np.pi / count
    even_part = np.cos(turn * (position * slot % (2 * count)))
    odd_part = np.sin(turn * (position * slot % (2 * count)))
    odd_part[:, 0] = np.cos(turn * (position[:, 0] * count % (2 * count)))
    return np.concatenate([even_part, odd_part], axis=1)


def parity_weights(count):
    weights = np.full((2 * count,), 2.0)
    weights[0] = 1.0
    weights[count] = 1.0
    return weights


def times(value, factor):
    re, im = value
    wr, wi = factor
    if wi == 0.0:
        return (re, im) if wr == 1.0 else (wr * re, wr * im)
    if wr == 0.0:
        return (-im, re) if wi == 1.0 else (-wi * im, wi * re)
    return (wr * re - wi * im, wr * im + wi * re)


def unit_root(index, length, sign):
    quarter = {0: (1.0, 0.0), 1: (0.0, 1.0), 2: (-1.0, 0.0), 3: (0.0, -1.0)}
    if 4 * index % length == 0:
        wr, wi = quarter[4 * index // length % 4]
        return (wr, sign * wi)
    phase = 2.0 * math.pi * index / length
    return (math.cos(phase), sign * math.sin(phase))


def add_pair(first, second):
    return (first[0] + second[0], first[1] + second[1])


def sub_pair(first, second):
    return (first[0] - second[0], first[1] - second[1])


def fourier(values, sign):
    length = len(values)
    if length == 1:
        return values
    evens = fourier(values[0::2], sign)
    odds = fourier(values[1::2], sign)
    half = length // 2
    turned = [times(odds[k], unit_root(k, length, sign)) for k in range(half)]
    return [add_pair(evens[k], turned[k]) for k in range(half)] + [
        sub_pair(evens[k], turned[k]) for k in range(half)
    ]


def layers_to_planes(in_ref, out_ref):
    layer_count = in_ref.shape[2]
    row_step = 8

    def chunk(i, carry):
        rows = pl.ds(pl.multiple_of(i * row_step, row_step), row_step)
        layers = [(in_ref[0, 0, z, rows, :], in_ref[1, 0, z, rows, :]) for z in range(layer_count)]
        turned = [times(layers[z], unit_root(z, 2 * layer_count, -1.0)) for z in range(layer_count)]
        evens = fourier(layers, -1.0)
        odds = fourier(turned, -1.0)
        for k in range(layer_count):
            for part in range(2):
                out_ref[2 * k, 0, part, rows, :] = evens[k][part]
                out_ref[2 * k + 1, 0, part, rows, :] = odds[k][part]
        return carry

    lax.fori_loop(0, in_ref.shape[3] // row_step, chunk, 0)


def planes_to_layers(scale, in_ref, out_ref):
    layer_count = out_ref.shape[2]
    row_step = 8

    def chunk(i, carry):
        rows = pl.ds(pl.multiple_of(i * row_step, row_step), row_step)
        planes = [
            (in_ref[k, 0, 0, rows, :], in_ref[k, 0, 1, rows, :]) for k in range(2 * layer_count)
        ]
        evens = fourier(planes[0::2], 1.0)
        odds = fourier(planes[1::2], 1.0)
        for z in range(layer_count):
            total = add_pair(evens[z], times(odds[z], unit_root(z, 2 * layer_count, 1.0)))
            out_ref[0, 0, z, rows, :] = scale * total[0]
            out_ref[1, 0, z, rows, :] = scale * total[1]
        return carry

    lax.fori_loop(0, out_ref.shape[3] // row_step, chunk, 0)


def dot32(left, right):
    return jnp.dot(left, right, preferred_element_type=jnp.float32)


def plane_kernel(
    planes_ref,
    kernel_ref,
    fy_ref,
    fx_ref,
    gx_ref,
    gy_ref,
    out_ref,
    spec_ref,
    held_ref,
    tensor_ref,
    result_ref,
    send_sem,
    recv_sem,
    own_sem,
    tensor_sem,
    out_sem,
):
    groups, local_planes = planes_ref.shape[0], planes_ref.shape[1]
    slab, columns_full = planes_ref.shape[4], planes_ref.shape[5]
    rows_full = groups * slab
    me = lax.axis_index("space")
    peers = [lax.rem(me + d, groups) for d in range(groups)]
    sources = [lax.rem(me + groups - d, groups) for d in range(groups)]

    def tensor_copy(q):
        return pltpu.make_async_copy(
            kernel_ref.at[:, q, pl.ds(0, rows_full + 8), pl.ds(0, columns_full + 128)],
            tensor_ref.at[q],
            tensor_sem.at[q],
        )

    def own_copy(q):
        return pltpu.make_async_copy(planes_ref.at[me, q], held_ref.at[q, me], own_sem.at[q])

    def out_copy(q):
        return pltpu.make_async_copy(result_ref.at[q], out_ref.at[:, q], out_sem.at[q])

    def remote_copy(q, d):
        return pltpu.make_async_remote_copy(
            src_ref=planes_ref.at[peers[d], q],
            dst_ref=held_ref.at[q, me],
            send_sem=send_sem.at[q, d],
            recv_sem=recv_sem.at[q, d],
            device_id={"space": peers[d]},
            device_id_type=pl.DeviceIdType.MESH,
        )

    def arrival(q, d):
        return pltpu.make_async_remote_copy(
            src_ref=planes_ref.at[peers[d], q],
            dst_ref=held_ref.at[q, sources[d]],
            send_sem=send_sem.at[q, d],
            recv_sem=recv_sem.at[q, d],
            device_id={"space": peers[d]},
            device_id_type=pl.DeviceIdType.MESH,
        )

    barrier = pltpu.get_barrier_semaphore()
    for d in range(1, groups):
        pl.semaphore_signal(
            barrier, inc=1, device_id={"space": peers[d]}, device_id_type=pl.DeviceIdType.MESH
        )
    for q in range(local_planes):
        tensor_copy(q).start()
        own_copy(q).start()
    pl.semaphore_wait(barrier, groups - 1)
    for q in range(local_planes):
        for d in range(1, groups):
            remote_copy(q, d).start()

    def plane(q, carry):
        tensor_copy(q).wait()
        own_copy(q).wait()
        for d in range(1, groups):
            arrival(q, d).wait_recv()
        plane_compute(
            held_ref.at[q], tensor_ref.at[q], fy_ref, fx_ref, gx_ref, gy_ref, result_ref.at[q], spec_ref
        )
        out_copy(q).start()
        return carry

    lax.fori_loop(0, local_planes, plane, 0)
    for q in range(local_planes):
        out_copy(q).wait()
        for d in range(1, groups):
            remote_copy(q, d).wait_send()


def plane_compute(in_ref, kernel_ref, fy_ref, fx_ref, gx_ref, gy_ref, out_ref, spec_ref):
    groups, slab, columns_full = in_ref.shape[0], in_ref.shape[3], in_ref.shape[4]
    rows_full = groups * slab
    fy = jnp.concatenate([fy_ref[0], fy_ref[0], fy_ref[1]], axis=0)
    fx = jnp.concatenate([fx_ref[0], fx_ref[0], fx_ref[1]], axis=1)
    gx = jnp.concatenate([gx_ref[0], gx_ref[0], gx_ref[1]], axis=1)
    gy = jnp.concatenate([gy_ref[0], gy_ref[0], gy_ref[1]], axis=0)

    def forward(f, carry):
        c, part = f // 2, f % 2
        cells = jnp.concatenate([in_ref[g, c, part] for g in range(groups)], axis=0)
        upper, lower = split_limbs(cells)
        lines = dot32(jnp.concatenate([upper, lower, upper], axis=1), fy)
        upper, lower = split_limbs(lines)
        spec_ref[f] = dot32(fx, jnp.concatenate([upper, lower, upper], axis=0))
        return carry

    lax.fori_loop(0, 6, forward, 0)

    lane = 128
    sub = 8
    row_pos = lax.broadcasted_iota(jnp.int32, (sub, lane), 0)
    lane_pos = lax.broadcasted_iota(jnp.int32, (sub, lane), 1)

    def tensor(i, carry):
        row_start = pl.multiple_of(i * sub, sub)
        top = (row_pos + row_start) == 0
        for start in range(0, columns_full, lane):

            def pick(component, odd_x, odd_y):
                def at(rows):
                    inner = kernel_ref[component, rows, start : start + lane]
                    if odd_y and start == 0:
                        edge = kernel_ref[component, rows, columns_full : columns_full + lane]
                        inner = jnp.where(lane_pos == 0, edge, inner)
                    return inner

                values = at(pl.ds(row_start, sub))
                if odd_x:
                    values = jnp.where(top, at(pl.ds(rows_full, sub)), values)
                return values

            spec = {}
            for px in range(2):
                for py in range(2):
                    for f in range(6):
                        spec[px, py, f] = spec_ref[
                            f,
                            pl.ds(row_start + px * rows_full, sub),
                            py * columns_full + start : py * columns_full + start + lane,
                        ]
            k_xy = pick(3, 0, 0)
            for px in range(2):
                for py in range(2):
                    sx = 1.0 if px else -1.0
                    sy = 1.0 if py else -1.0
                    k_xx, k_yy, k_zz = [pick(n, px, py) for n in range(3)]
                    k_xz = sx * pick(4, 0, py)
                    k_yz = sy * pick(5, px, 0)
                    xy_both = -(sx * sy) * k_xy
                    for part in range(2):
                        turn = 1.0 if part else -1.0
                        other = 1 - part
                        field_x = (
                            k_xx * spec[px, py, part]
                            + xy_both * spec[1 - px, 1 - py, 2 + part]
                            + turn * (k_xz * spec[1 - px, py, 4 + other])
                        )
                        field_y = (
                            xy_both * spec[1 - px, 1 - py, part]
                            + k_yy * spec[px, py, 2 + part]
                            + turn * (k_yz * spec[px, 1 - py, 4 + other])
                        )
                        field_z = k_zz * spec[px, py, 4 + part] + turn * (
                            k_xz * spec[1 - px, py, other] + k_yz * spec[px, 1 - py, 2 + other]
                        )
                        for c, field in enumerate((field_x, field_y, field_z)):
                            spec_ref[
                                2 * c + part,
                                pl.ds(row_start + px * rows_full, sub),
                                py * columns_full + start : py * columns_full + start + lane,
                            ] = field
        return carry

    lax.fori_loop(0, rows_full // sub, tensor, 0)

    def backward(f, carry):
        c, part = f // 2, f % 2
        upper, lower = split_limbs(spec_ref[f])
        lines = dot32(gx, jnp.concatenate([upper, lower, upper], axis=0))
        upper, lower = split_limbs(lines)
        cells = dot32(jnp.concatenate([upper, lower, upper], axis=1), gy)
        for g in range(groups):
            out_ref[g, c, part] = cells[g * slab : (g + 1) * slab]
        return carry

    lax.fori_loop(0, 6, backward, 0)


def swap_kernel(shifts, combine, tile_ref, out_ref, held_ref, send_sem, recv_sem):
    groups, images = lax.axis_size("space"), lax.axis_size("image")
    me, image = lax.axis_index("space"), lax.axis_index("image")
    routes = [
        (n, shift, d)
        for n, shift in enumerate(shifts)
        for d in range(groups)
        if shift != 0 or d != 0
    ]

    def target(shift, d):
        return {"image": lax.rem(image - shift + images, images), "space": lax.rem(me + d, groups)}

    barrier = pltpu.get_barrier_semaphore()
    for n, shift, d in routes:
        pl.semaphore_signal(
            barrier, inc=1, device_id=target(shift, d), device_id_type=pl.DeviceIdType.MESH
        )
    pl.semaphore_wait(barrier, len(routes))

    def copy_of(n, shift, d, slot):
        return pltpu.make_async_remote_copy(
            src_ref=tile_ref,
            dst_ref=held_ref.at[n, slot],
            send_sem=send_sem.at[n, d],
            recv_sem=recv_sem.at[n, d],
            device_id=target(shift, d),
            device_id_type=pl.DeviceIdType.MESH,
        )

    for n, shift, d in routes:
        copy_of(n, shift, d, me).start()
    held_ref[shifts.index(0), me] = tile_ref[...]
    for n, shift, d in routes:
        copy_of(n, shift, d, lax.rem(me + groups - d, groups)).wait_recv()
    for n in range(len(shifts)):
        total = held_ref[n, 0]
        for g in range(1, groups):
            total = combine(total, held_ref[n, g])
        out_ref[n] = total
    for n, shift, d in routes:
        copy_of(n, shift, d, me).wait_send()


def swapped(values, shifts, combine, collective_id):
    rows, columns = values.shape
    tile = jnp.pad(values, ((0, -rows % 8), (0, -columns % 128)))
    groups = lax.axis_size("space")
    inside = pl.BlockSpec(memory_space=pltpu.VMEM)
    result = pl.pallas_call(
        functools.partial(swap_kernel, shifts, combine),
        in_specs=[inside],
        out_specs=inside,
        out_shape=jax.ShapeDtypeStruct((len(shifts),) + tile.shape, jnp.float32),
        scratch_shapes=[
            pltpu.VMEM((len(shifts), groups) + tile.shape, jnp.float32),
            pltpu.SemaphoreType.DMA((len(shifts), groups)),
            pltpu.SemaphoreType.DMA((len(shifts), groups)),
        ],
        compiler_params=pltpu.CompilerParams(
            collective_id=collective_id, has_side_effects=True
        ),
        name="swap_kernel",
    )(tile)
    return result[:, :rows, :columns]


def demag_pair(magnet, kernel, images, early_work, pair_index):
    layer_count, row_count, column_count = magnet.shape[2:]
    groups = lax.axis_size("space")
    local_planes = 2 * layer_count // groups
    full_rows = row_count * groups
    plane_dims = (2 * layer_count, 3, 2, row_count, column_count)
    layer_spec = pl.BlockSpec((2, 1, layer_count, row_count, column_count), lambda c: (0, c, 0, 0, 0))
    plane_spec = pl.BlockSpec((2 * layer_count, 1, 2, row_count, column_count), lambda c: (0, c, 0, 0, 0))
    planes = pl.pallas_call(
        layers_to_planes,
        grid=(3,),
        in_specs=[layer_spec],
        out_specs=plane_spec,
        out_shape=jax.ShapeDtypeStruct(plane_dims, jnp.float32),
        name="layers_to_planes",
    )(magnet)
    planes = planes.reshape((groups, local_planes) + plane_dims[1:])
    table_y = parity_table(column_count)
    table_x = parity_table(full_rows)
    tables = [
        table_limbs(table_y),
        table_limbs(table_x.T),
        table_limbs(table_x * parity_weights(full_rows)[None, :]),
        table_limbs((table_y * parity_weights(column_count)[None, :]).T),
    ]
    slab_dims = (local_planes, groups, 3, 2, row_count, column_count)
    tensor_dims = (local_planes, 6, full_rows + 8, column_count + 128)
    anywhere = pl.BlockSpec(memory_space=pl.ANY)
    inside = pl.BlockSpec(memory_space=pltpu.VMEM)
    dots = 6 * local_planes * 4 * full_rows * column_count * 3 * (full_rows + column_count // 2)
    planes = pl.pallas_call(
        plane_kernel,
        in_specs=[anywhere, anywhere] + [inside] * len(tables),
        out_specs=anywhere,
        out_shape=jax.ShapeDtypeStruct(planes.shape, jnp.float32),
        scratch_shapes=[
            pltpu.VMEM((6, 2 * full_rows, 2 * column_count), jnp.float32),
            pltpu.VMEM(slab_dims, jnp.float32),
            pltpu.VMEM(tensor_dims, jnp.float32),
            pltpu.VMEM(slab_dims, jnp.float32),
            pltpu.SemaphoreType.DMA((local_planes, groups)),
            pltpu.SemaphoreType.DMA((local_planes, groups)),
            pltpu.SemaphoreType.DMA((local_planes,)),
            pltpu.SemaphoreType.DMA((local_planes,)),
            pltpu.SemaphoreType.DMA((local_planes,)),
        ],
        compiler_params=pltpu.CompilerParams(
            vmem_limit_bytes=56 * 1024 * 1024, collective_id=pair_index, has_side_effects=True
        ),
        cost_estimate=pl.CostEstimate(
            flops=4 * dots, bytes_accessed=4 * planes.size * 4, transcendentals=0
        ),
        name="plane_kernel",
    )(planes, kernel, *[jnp.asarray(t) for t in tables])
    planes = planes.reshape(plane_dims)
    planes, *images = lax.optimization_barrier((planes, *images))
    planes = lax.all_to_all(planes, "space", split_axis=0, concat_axis=0, tiled=True)
    planes, early = lax.optimization_barrier((planes, early_work(images)))
    padded_cells = 8 * layer_count * full_rows * column_count
    field = pl.pallas_call(
        functools.partial(planes_to_layers, -1.0 / padded_cells),
        grid=(3,),
        in_specs=[plane_spec],
        out_specs=layer_spec,
        out_shape=jax.ShapeDtypeStruct(magnet.shape, jnp.float32),
        name="planes_to_layers",
    )(planes)
    return field, images, early


def demag_field(magnet, kernel, images, early_work):
    fields = []
    for index, start in enumerate(range(0, magnet.shape[0], 2)):
        field, images, early = demag_pair(
            magnet[start : start + 2], kernel, images, early_work, index
        )
        fields.append(field)
    return (fields[0] if len(fields) == 1 else jnp.concatenate(fields, axis=0)), images, early


def local_fields(magnet, anisotropy, rimmed):
    layer_count = magnet.shape[2]
    row_count = magnet.shape[3]
    column_count = magnet.shape[4]
    x_plus = rimmed[:, :, :, 2:]
    x_minus = rimmed[:, :, :, :-2]
    padded = jnp.pad(magnet, ((0, 0), (0, 0), (1, 1), (0, 0), (1, 1)))
    z_plus = padded[:, :, 2:, :, 1:-1]
    z_minus = padded[:, :, :-2, :, 1:-1]
    y_plus = padded[:, :, 1:-1, :, 2:]
    y_minus = padded[:, :, 1:-1, :, :-2]
    first_row = lax.axis_index("space") * row_count
    full_rows = row_count * lax.axis_size("space")
    layer_pos = lax.broadcasted_iota(jnp.int32, (layer_count, row_count, column_count), 0)
    row_pos = lax.broadcasted_iota(jnp.int32, (layer_count, row_count, column_count), 1) + first_row
    column_pos = lax.broadcasted_iota(jnp.int32, (layer_count, row_count, column_count), 2)
    boundary = (layer_pos == 0).astype(jnp.float32) + (layer_pos == layer_count - 1).astype(
        jnp.float32
    )
    boundary = (
        boundary
        + (row_pos == 0).astype(jnp.float32)
        + (row_pos == full_rows - 1).astype(jnp.float32)
    )
    boundary = (
        boundary
        + (column_pos == 0).astype(jnp.float32)
        + (column_pos == column_count - 1).astype(jnp.float32)
    )
    present = 6.0 - boundary
    neighbours = x_plus + x_minus + y_plus + y_minus + z_plus + z_minus
    exchange_part = exchange_strength * (neighbours - present * magnet)
    chiral_x = chiral_strength * (x_plus[:, 2] - x_minus[:, 2])
    chiral_y = chiral_strength * (y_plus[:, 2] - y_minus[:, 2])
    chiral_z = -chiral_strength * (x_plus[:, 0] - x_minus[:, 0] + (y_plus[:, 1] - y_minus[:, 1]))
    easy_axis = 2.0 * anisotropy[:, None] * magnet[:, 2]
    local_part = exchange_part + jnp.stack([chiral_x, chiral_y, chiral_z + easy_axis], axis=1)
    return local_part


def body(magnet, anisotropy, kernel):
    image_count = magnet.shape[0]
    cell_count = magnet.shape[2] * magnet.shape[3] * lax.axis_size("space") * magnet.shape[4]
    framed = extended(magnet, (("image", 0),), 1)
    rimmed = extended(magnet, (("space", 3),), 1)

    def early_work(images):
        prior, following = images[0][:-2], images[0][2:]
        ahead = project(following - magnet, magnet)
        behind = project(magnet - prior, magnet)
        return (
            local_fields(magnet, anisotropy, images[1]),
            total_cells(angle_squared(magnet, following)),
            total_cells(ahead * ahead),
            total_cells(ahead * behind),
            total_cells(behind * behind),
        )

    demag, (framed, _), early = demag_field(magnet, kernel, [framed, rimmed], early_work)
    fields = early[0] + demag
    prior_image = framed[:-2]
    next_image = framed[2:]
    true_force = project(fields, magnet)
    tangent_next = project(next_image - magnet, magnet)
    tangent_prior = project(magnet - prior_image, magnet)
    sums = jnp.stack(
        [
            -0.5 * total_cells(magnet * fields),
            *early[1:],
            total_cells(true_force * tangent_next),
            total_cells(true_force * tangent_prior),
        ],
        axis=1,
    )
    band_size = image_count * lax.axis_size("image")
    swaps = swapped(sums, (-1, 0, 1), jnp.add, 64)
    band = jnp.concatenate([swaps[0, -1:], swaps[1], swaps[2, :1]], axis=0)
    energy_band, distance_band = band[:, 0], jnp.sqrt(band[:, 1] / cell_count)
    weight_next, weight_prior = tangent_weights(
        energy_band, jnp.roll(energy_band, -1), jnp.roll(energy_band, 1)
    )
    length_squares = (
        weight_next * weight_next * band[:, 2]
        + 2.0 * weight_next * weight_prior * band[:, 3]
        + weight_prior * weight_prior * band[:, 4]
    )
    drive_total = weight_next * band[:, 5] + weight_prior * band[:, 6]
    tangent_scale = jnp.sqrt(jnp.maximum(length_squares, 0.0) / cell_count + epsilon)
    parallel = drive_total / (cell_count * tangent_scale)
    spring = spring_strength * (distance_band - jnp.roll(distance_band, 1))
    first_image = lax.axis_index("image") * image_count
    image_index = first_image - 1 + jnp.arange(image_count + 2)
    interior = ((image_index > 0) & (image_index < band_size - 1)).astype(jnp.float32)
    pull = (spring - parallel) / tangent_scale
    mine = jnp.stack([energy_band, pull * weight_next, pull * weight_prior, interior], axis=1)[1:-1]
    energy_total = mine[:, 0]
    band_force = jnp.where(
        lift_axes(mine[:, 3]) > 0.0,
        true_force + lift_axes(mine[:, 1]) * tangent_next + lift_axes(mine[:, 2]) * tangent_prior,
        0.0,
    )
    local_largest = jnp.max(jnp.sqrt(jnp.sum(band_force * band_force, axis=1)), axis=(1, 2, 3))
    largest = swapped(local_largest[None, :], (0,), jnp.maximum, 65)[0, 0]
    move_scale = jnp.minimum(step_limit, rotation_limit / (largest + epsilon))
    stepped = magnet + lift_axes(move_scale) * band_force
    updated = stepped / jnp.sqrt(jnp.sum(stepped * stepped, axis=1, keepdims=True))
    return (updated, band_force, energy_total / cell_count)


def solution(mesh):
    in_specs = (P("image", None, None, "space", None), P("space"), P(None, "space", None, None))
    out_specs = (
        P("image", None, None, "space", None),
        P("image", None, None, "space", None),
        P("image"),
    )
    return jax.shard_map(body, mesh=mesh, in_specs=in_specs, out_specs=out_specs, check_vma=False)
```

profile of v0, /device:TPU:0, one launch (start us, length us, event | category | flops | bytes accessed | tf_op | source)
XLA Modules:
  0.0 241.7 jit_solution(2187860699596797588)
XLA Ops:
  0.6 3.9 %fusion.27 = (f32[1,3,8,64,256]{4,3,2,1,0:T(8,128)}, f32[1,3,8,64,256]{4,3,2,1,0:T(8,128)}) fusion(f32[2,3,8,64,256]{4,3,2,1,0:T(8,128)} %in_ref.1), kind=kLoop, calls=%fused_computation.101 | loop fusion | bytes 6291456 | tf_op jit(solution)/shard_map/slice | solution.py:25
  4.5 6.1 %collective-permute-start = (f32[1,3,8,64,256]{4,3,2,1,0:T(8,128)}, f32[1,3,8,64,256]{4,3,2,1,0:T(8,128)}, u32[]{:S(2)}, u32[]{:S(2)}) collective-permute-start(f32[1,3,8,64,256]{4,3,2,1,0:T(8,128)} %get-tuple-element.51), channel_id=1, source_target_pairs={{0,4},{4,8},{8,12},{12,16},{16,20},{20,24},{24,28},{1,5},{5,9},{9,... | collective-permute-start | bytes 4718600 | tf_op jit(solution)/shard_map/ppermute | solution.py:28
  10.6 1.3 collective-permute-start.1
  11.9 1.2 fusion.26
  13.1 1.5 collective-permute-start.2
  14.6 1.3 collective-permute-start.3
  15.9 5.5 %layers_to_planes.1 = f32[16,3,2,64,256]{4,3,2,1,0:T(8,128)} custom-call(f32[2,3,8,64,256]{4,3,2,1,0:T(8,128)} %in_ref.1), custom_call_target="tpu_custom_call" | custom-call | tf_op jit(solution)/shard_map/layers_to_planes/pallas_call | solution.py:447
  21.4 82.7 %plane_kernel.1 = f32[4,4,3,2,64,256]{5,4,3,2,1,0:T(8,128)} custom-call(f32[4,4,3,2,64,256]{5,4,3,2,1,0:T(8,128)} %bitcast.68, f32[6,4,512,512]{3,2,1,0:T(8,128)} %kernel_ref.1, bf16[2,256,512]{2,1,0:T(8,128)(2,1)} %constant.71.clone.fy_ref, bf16[2,512,256]{2,1,0:T(8,128)(2,1)} %constant.72.clone.fx_ref, bf16[2,256,512]{2,1,0:T(8,128)(2,1)} %constant.73.clone.gx_ref, ...), custom_call_target="tpu_custom_call" | custom-call | flops 28991029248 | bytes 25165824 | tf_op jit(solution)/shard_map/plane_kernel/pallas_call | solution.py:469
  104.1 2.3 pad_maximum_fusion.1
  106.5 5.3 %pad_maximum_fusion = f32[4,3,8,64,256]{4,3,2,1,0:T(8,128)} fusion(f32[1,3,8,64,256]{4,3,2,1,0:T(8,128)} %collective-permute-done.1, f32[2,3,8,64,256]{4,3,2,1,0:T(8,128)S(1)} %copy-done, f32[1,3,8,64,256]{4,3,2,1,0:T(8,128)} %collective-permute-done), kind=kLoop, calls=%fused_computation.8 | loop fusion | flops 3145728 | bytes 12582912 | tf_op jit(solution)/shard_map/concatenate | solution.py:26
  111.8 10.6 %all-to-all-start = ((f32[16,3,2,64,256]{4,3,2,1,0:T(8,128)}), f32[16,3,2,64,256]{4,3,2,1,0:T(8,128)}, u32[]{:S(2)}, u32[]{:S(2)}) async-start(f32[16,3,2,64,256]{4,3,2,1,0:T(8,128)} %bitcast.67), calls=%async_computation | async-start | bytes 12582912 | tf_op jit(solution)/shard_map/all_to_all | solution.py:495
  122.3 2.0 copy.76
  124.5 0.9 add_subtract_fusion
  125.5 5.4 %subtract_multiply_fusion = (f32[2,1,8,64,256]{4,3,2,1,0:T(8,128)}, f32[2,1,8,64,256]{4,3,2,1,0:T(8,128)}, f32[2,1,8,64,256]{4,3,2,1,0:T(8,128)}) fusion(f32[2,3,8,66,256]{4,3,2,1,0:T(8,128)} %pad_maximum_fusion.1, f32[2,3,8,64,256]{4,3,2,1,0:T(8,128)S(1)} %copy-done, f32[64]{0:T(128)S(1)} %broadcast_multiply_fusion), kind=kLoop, calls=%fused_computation.58 | loop fusion | flops 2621440 | bytes 11534848 | tf_op jit(solution)/shard_map/mul | solution.py:551
  130.8 10.6 %multiply_reduce_fusion.8 = (f32[2,8,64,256]{3,2,1,0:T(8,128)}, f32[2,8,64,256]{3,2,1,0:T(8,128)}, f32[2,8,64,256]{3,2,1,0:T(8,128)}, f32[2,8,64,256,3]{3,2,1,4,0:T(8,128)}, f32[2,3,8,64,256]{4,3,2,1,0:T(8,128)}) fusion(f32[2,3,8,64,256]{4,3,2,1,0:T(8,128)S(1)} %copy-done, f32[4,3,8,64,256]{4,3,2,1,0:T(8,128)} %pad_maximum_fusion, ...), kind=kLoop, calls=%fused_computation.34 | loop fusion | flops 14155776 | bytes 28835840 | tf_op jit(solution)/shard_map/reduce_sum | solution.py:46
  141.5 2.6 %fusion.15 = f32[1,2,8,64,256]{4,3,2,1,0:T(8,128)S(1)} fusion(f32[2,8,64,256,3]{3,2,1,4,0:T(8,128)} %get-tuple-element.44, f32[2,8,64,256,3]{3,2,1,0,4:T(8,128)} %bitcast.65), kind=kLoop, calls=%fused_computation.51 | loop fusion | flops 786432 | bytes 5242880 | tf_op jit(solution)/shard_map/jit(cross)/sub | solution.py:50
  144.1 0.5 copy-done.5
  144.6 2.8 %subtract_bitcast_fusion = (f32[1,2,8,64,256]{4,3,2,1,0:T(8,128)S(1)}, f32[1,2,8,64,256]{4,3,2,1,0:T(8,128)S(1)}) fusion(f32[2,8,64,256,3]{3,2,1,4,0:T(8,128)S(1)} %copy-done.5, f32[2,8,64,256,3]{3,2,1,0,4:T(8,128)} %bitcast.66), kind=kLoop, calls=%fused_computation.57 | loop fusion | flops 1572864 | bytes 8388608 | tf_op jit(solution)/shard_map/jit(cross)/sub | solution.py:50
  147.5 0.3 fusion.7
  147.8 0.9 copy-done.6
  148.7 1.9 multiply_reduce_fusion.12
  150.7 4.1 %multiply_reduce_fusion.4 = (f32[2]{0:T(128)S(1)}, f32[2]{0:T(128)S(1)}, f32[2]{0:T(128)S(1)}, f32[2,3,8,64,256]{4,3,2,1,0:T(8,128)}, f32[2,3,8,64,256]{4,3,2,1,0:T(8,128)}) fusion(f32[2,3,8,64,256]{4,3,2,1,0:T(8,128)S(1)} %copy-done, f32[2,8,64,256]{3,2,1,0:T(8,128)S(1)} %copy-done.7, f32[4,3,8,64,256]{4,3,2,1,0:T(8,128)S(1)} %bitcast.64, ...), kind=kLoop, calls=%fused_computation.27 | loop fusion | flops 9437178 | bytes 17825816 | tf_op jit(solution)/shard_map/reduce_sum | solution.py:42
  154.8 37.1 %all-to-all-done.in_ref = f32[16,3,2,64,256]{4,3,2,1,0:T(8,128)} async-done(((f32[16,3,2,64,256]{4,3,2,1,0:T(8,128)}), f32[16,3,2,64,256]{4,3,2,1,0:T(8,128)}, u32[]{:S(2)}, u32[]{:S(2)}) %all-to-all-start) | async-done | bytes 6291488 | tf_op jit(solution)/shard_map/all_to_all | solution.py:495
  191.8 6.0 %planes_to_layers.1 = f32[2,3,8,64,256]{4,3,2,1,0:T(8,128)} custom-call(f32[16,3,2,64,256]{4,3,2,1,0:T(8,128)} %all-to-all-done.in_ref), custom_call_target="tpu_custom_call" | custom-call | tf_op jit(solution)/shard_map/planes_to_layers/pallas_call | solution.py:498
  197.9 4.3 %multiply_reduce_fusion.10 = (f32[2]{0:T(128)S(1)}, f32[2,8,64,256]{3,2,1,0:T(8,128)S(1)}, f32[2,3,8,64,256]{4,3,2,1,0:T(8,128)S(1)}) fusion(f32[2,3,8,64,256]{4,3,2,1,0:T(8,128)S(1)} %copy-done, f32[2,3,8,64,256]{4,3,2,1,0:T(8,128)} %get-tuple-element.15, f32[2,3,8,64,256]{4,3,2,1,0:T(8,128)} %planes_to_layers.1), kind=kLoop, calls=%fused_computation.39 | loop fusion | flops 2883582 | bytes 13631496 | tf_op jit(solution)/shard_map/reduce_sum | solution.py:42
  202.2 0.4 copy-done.3
  202.6 3.1 %multiply_reduce_fusion.2 = (f32[2]{0:T(128)S(1)}, f32[2]{0:T(128)S(1)}, f32[2,3,8,64,256]{4,3,2,1,0:T(8,128)}) fusion(f32[2,3,8,64,256]{4,3,2,1,0:T(8,128)S(1)} %copy-done.3, f32[2,3,8,64,256]{4,3,2,1,0:T(8,128)S(1)} %copy-done.2, f32[2,3,8,64,256]{4,3,2,1,0:T(8,128)S(1)} %get-tuple-element.39, f32[2,3,8,64,256]{4,3,2,1,0:T(8,128)S(1)} %copy-done, ...), kind=kLoop, calls=%fused_computation.24 | loop fusion | flops 4718588 | bytes 16777232 | tf_op jit(solution)/shard_map/reduce_sum | solution.py:42
  205.7 0.1 copy.71
  205.9 0.1 copy.66
  206.4 0.1 stack.39
  206.5 0.6 pad.13.tile_ref
  207.1 11.5 %swap_kernel.2 = f32[3,8,128]{2,1,0:T(8,128)} custom-call(f32[8,128]{1,0:T(8,128)} %pad.13.tile_ref), custom_call_target="tpu_custom_call" | custom-call | tf_op jit(solution)/shard_map/swap_kernel/pallas_call | solution.py:421
  218.6 0.7 slice_bitcast_fusion.5
  219.2 0.7 slice_bitcast_fusion.3
  220.0 0.6 multiply_reduce_fusion.13
  220.6 0.1 select_select_fusion.1
  220.7 0.6 slice.229
  221.3 0.8 fusion.23
  222.1 0.1 slice_reduce_fusion
  222.2 0.1 slice_reduce_fusion.1
  222.3 7.0 %multiply_reduce_fusion.1 = (f32[2,8,64,256]{3,2,1,0:T(8,128)S(1)}, f32[2,3,8,64,256]{4,3,2,1,0:T(8,128)}) fusion(f32[2,3,8,64,256]{4,3,2,1,0:T(8,128)} %get-tuple-element.41, f32[2]{0:T(128)S(1)} %slice_reduce_fusion, f32[2,3,8,64,256]{4,3,2,1,0:T(8,128)} %get-tuple-element.38, f32[2,3,8,64,256]{4,3,2,1,0:T(8,128)} %get-tuple-element.40, ...), kind=kLoop, calls=%fused_computation.22 | loop fusion | flops 5242880 | bytes 13631506 | tf_op jit(solution)/shard_map/reduce_sum | solution.py:620
  229.3 0.4 sqrt_reduce_fusion
  229.7 0.6 pad.14.tile_ref
  230.3 5.0 %swap_kernel.3 = f32[1,8,128]{2,1,0:T(8,128)} custom-call(f32[8,128]{1,0:T(8,128)} %pad.14.tile_ref), custom_call_target="tpu_custom_call" | custom-call | tf_op jit(solution)/shard_map/swap_kernel/pallas_call | solution.py:421
  235.3 0.7 minimum_bitcast_fusion
  236.0 3.0 %multiply_reduce_fusion = f32[2,8,64,256]{3,2,1,0:T(8,128)S(1)} fusion(f32[2,3,8,64,256]{4,3,2,1,0:T(8,128)S(1)} %copy-done, f32[2,3,8,64,256]{4,3,2,1,0:T(8,128)} %get-tuple-element.32, f32[2]{0:T(128)S(1)} %minimum_bitcast_fusion), kind=kLoop, calls=%fused_computation.20 | loop fusion | flops 2883584 | bytes 7340040 | tf_op jit(solution)/shard_map/reduce_sum | solution.py:624
  238.9 0.2 sqrt.29
  239.2 2.5 %broadcast_divide_fusion = f32[2,3,8,64,256]{4,3,2,1,0:T(8,128)} fusion(f32[2,8,64,256]{3,2,1,0:T(8,128)S(1)} %sqrt.29, f32[2,3,8,64,256]{4,3,2,1,0:T(8,128)S(1)} %copy-done, f32[2,3,8,64,256]{4,3,2,1,0:T(8,128)S(1)} %copy-done.4, f32[2]{0:T(128)S(1)} %minimum_bitcast_fusion), kind=kLoop, calls=%fused_computation.38 | loop fusion | flops 2359296 | bytes 10485768 | tf_op jit(solution)/shard_map/div | solution.py:624
  (41 shorter events, 0.6 us)
Async XLA Ops:
  4.5 101.9 %collective-permute-start = (f32[1,3,8,64,256]{4,3,2,1,0:T(8,128)}, f32[1,3,8,64,256]{4,3,2,1,0:T(8,128)}, u32[]{:S(2)}, u32[]{:S(2)}) collective-permute-start(f32[1,3,8,64,256]{4,3,2,1,0:T(8,128)} %get-tuple-element.51), channel_id=1, source_target_pairs={{0,4},{4,8},{8,12},{12,16},{16,20},{20,24},{24,28},{1,5},{5,9},{9,... | collective-permute-start | bytes 4718600 | tf_op jit(solution)/shard_map/ppermute | solution.py:28
  10.6 95.9 %collective-permute-start.1 = (f32[1,3,8,64,256]{4,3,2,1,0:T(8,128)}, f32[1,3,8,64,256]{4,3,2,1,0:T(8,128)}, u32[]{:S(2)}, u32[]{:S(2)}) collective-permute-start(f32[1,3,8,64,256]{4,3,2,1,0:T(8,128)} %get-tuple-element.52), channel_id=1, source_target_pairs={{4,0},{8,4},{12,8},{16,12},{20,16},{24,20},{28,24},{5,1},{9,5},{13... | collective-permute-start | bytes 4718600 | tf_op jit(solution)/shard_map/ppermute | solution.py:30
  13.1 91.0 %collective-permute-start.2 = (f32[2,3,8,1,256]{4,3,2,1,0:T(1,128)S(1)}, f32[2,3,8,1,256]{4,3,2,1,0:T(1,128)S(1)}, u32[]{:S(2)}, u32[]{:S(2)}) collective-permute-start(f32[2,3,8,1,256]{4,3,2,1,0:T(1,128)S(1)} %get-tuple-element.49), channel_id=1, source_target_pairs={{0,1},{1,2},{2,3},{4,5},{5,6},{6,7},{8,9},{9,10},{10,11},{12,13},{... | collective-permute-start | bytes 147464 | tf_op jit(solution)/shard_map/ppermute | solution.py:28
  14.6 89.5 %collective-permute-start.3 = (f32[2,3,8,1,256]{4,3,2,1,0:T(1,128)S(1)}, f32[2,3,8,1,256]{4,3,2,1,0:T(1,128)S(1)}, u32[]{:S(2)}, u32[]{:S(2)}) collective-permute-start(f32[2,3,8,1,256]{4,3,2,1,0:T(1,128)S(1)} %get-tuple-element.50), channel_id=1, source_target_pairs={{1,0},{2,1},{3,2},{5,4},{6,5},{7,6},{9,8},{10,9},{11,10},{13,12},{... | collective-permute-start | bytes 147464 | tf_op jit(solution)/shard_map/ppermute | solution.py:30
  21.4 82.7 %copy-start = (f32[2,3,8,64,256]{4,3,2,1,0:T(8,128)S(1)}, f32[2,3,8,64,256]{4,3,2,1,0:T(8,128)}, u32[]{:S(2)}) copy-start(f32[2,3,8,64,256]{4,3,2,1,0:T(8,128)} %in_ref.1) | copy-start | bytes 9437188
  111.8 80.1 %all-to-all-start = ((f32[16,3,2,64,256]{4,3,2,1,0:T(8,128)}), f32[16,3,2,64,256]{4,3,2,1,0:T(8,128)}, u32[]{:S(2)}, u32[]{:S(2)}) async-start(f32[16,3,2,64,256]{4,3,2,1,0:T(8,128)} %bitcast.67), calls=%async_computation | async-start | bytes 12582912 | tf_op jit(solution)/shard_map/all_to_all | solution.py:495
  122.3 2.1 copy-start.9
  125.5 5.4 %copy-start.1 = (f32[2,3,8,66,256]{4,3,2,1,0:T(8,128)S(1)}, f32[2,3,8,66,256]{4,3,2,1,0:T(8,128)}, u32[]{:S(2)}) copy-start(f32[2,3,8,66,256]{4,3,2,1,0:T(8,128)} %pad_maximum_fusion.1) | copy-start | bytes 9732100
  141.5 3.2 %copy-start.5 = (f32[2,8,64,256,3]{3,2,1,4,0:T(8,128)S(1)}, f32[2,8,64,256,3]{3,2,1,4,0:T(8,128)}, u32[]{:S(2)}) copy-start(f32[2,8,64,256,3]{3,2,1,4,0:T(8,128)} %get-tuple-element.44) | copy-start | bytes 9437188
  141.5 9.2 %slice-start = ((s8[6291456]{0:T(1024)(128)(4,1)}), s8[4194304]{0:T(1024)(128)(4,1)S(1)}, s32[]{:S(2)}) async-start(s8[6291456]{0:T(1024)(128)(4,1)} %bitcast.63), calls=%async_computation.1 | async-start | bytes 8388608
  144.6 6.0 %slice-start.1 = ((s8[6291456]{0:T(1024)(128)(4,1)}), s8[2097152]{0:T(1024)(128)(4,1)S(1)}, s32[]{:S(2)}) async-start(s8[6291456]{0:T(1024)(128)(4,1)} %bitcast.63), calls=%async_computation.2 | async-start | bytes 4194304
  147.5 1.2 copy-start.6
  147.5 3.2 %copy-start.7 = (f32[2,8,64,256]{3,2,1,0:T(8,128)S(1)}, f32[2,8,64,256]{3,2,1,0:T(8,128)}, u32[]{:S(2)}) copy-start(f32[2,8,64,256]{3,2,1,0:T(8,128)} %get-tuple-element.21) | copy-start | bytes 3145732
  147.5 3.2 %copy-start.8 = (f32[2,8,64,256]{3,2,1,0:T(8,128)S(1)}, f32[2,8,64,256]{3,2,1,0:T(8,128)}, u32[]{:S(2)}) copy-start(f32[2,8,64,256]{3,2,1,0:T(8,128)} %get-tuple-element.22) | copy-start | bytes 3145732
  197.9 4.3 %copy-start.2 = (f32[2,3,8,64,256]{4,3,2,1,0:T(8,128)S(1)}, f32[2,3,8,64,256]{4,3,2,1,0:T(8,128)}, u32[]{:S(2)}) copy-start(f32[2,3,8,64,256]{4,3,2,1,0:T(8,128)} %get-tuple-element.40) | copy-start | bytes 9437188
  197.9 4.7 %copy-start.3 = (f32[2,3,8,64,256]{4,3,2,1,0:T(8,128)S(1)}, f32[2,3,8,64,256]{4,3,2,1,0:T(8,128)}, u32[]{:S(2)}) copy-start(f32[2,3,8,64,256]{4,3,2,1,0:T(8,128)} %get-tuple-element.41) | copy-start | bytes 9437188
  236.0 3.2 %copy-start.4 = (f32[2,3,8,64,256]{4,3,2,1,0:T(8,128)S(1)}, f32[2,3,8,64,256]{4,3,2,1,0:T(8,128)}, u32[]{:S(2)}) copy-start(f32[2,3,8,64,256]{4,3,2,1,0:T(8,128)} %get-tuple-element.32) | copy-start | bytes 9437188
where the time goes:
time: 242 us
  Pallas kernels  111 us (46%)
  other arithmetic  59.1 us (24%)
  waiting for transfers between devices  37.1 us (15%)
  starting transfers between devices  20.7 us (9%)
  local copies, waits for them, and re-layouts  13.3 us (5%)
    pallas_call x1, Pallas kernels, demag_pair(): pl.pallas_call(plane_kernel, in_specs=[anywhere, anywhere] + [inside] * l...  82.7 us
    all_to_all x1, waiting for transfers between devices, demag_pair(): lax.all_to_all(planes, 'space', split_axis=0, concat_axis=0, tiled=True)  37.1 us
    pallas_call x2, Pallas kernels, swapped(): pl.pallas_call(functools.partial(swap_kernel, shifts, combine), in_specs=...  16.4 us
    reduce_sum x4, other arithmetic, total_cells(): return jnp.sum(values, axis=tuple(range(1, values.ndim)))  13.5 us
    reduce_sum x1, other arithmetic, project(): return vector - jnp.sum(vector * magnet, axis=1, keepdims=True) * magnet  10.6 us
    all_to_all x1, starting transfers between devices, demag_pair(): lax.all_to_all(planes, 'space', split_axis=0, concat_axis=0, tiled=True)  10.6 us
    concatenate x2, other arithmetic, extended(): jnp.concatenate([lax.ppermute(tail, axis, [(i, (i + 1) % count) for i in...  7.65 us
    ppermute x2, starting transfers between devices, extended(): lax.ppermute(tail, axis, [(i, (i + 1) % count) for i in range(ends)])  7.55 us
  transfers between devices with their start and end apart: 5, of which 1 were waited for; matrix products, arithmetic and copies ran while one was open for 14% of the time, Pallas kernels for 36%

commit v1 on v0

v1 whole, which is shorter than its diff:
```python
import functools

import jax
import jax.numpy as jnp
import numpy as np
from jax import lax
from jax.experimental import pallas as pl
from jax.experimental.pallas import tpu as pltpu
from jax.sharding import PartitionSpec as P

exchange_strength = 0.25
chiral_strength = 0.3
spring_strength = 10.0
step_limit = 1.0
rotation_limit = 0.5
epsilon = 1e-06


def extended(cells, sides, width):
    for axis, dim in sides:
        count = lax.axis_size(axis)
        ends = count - 1
        head = lax.slice_in_dim(cells, 0, width, axis=dim)
        tail = lax.slice_in_dim(cells, cells.shape[dim] - width, cells.shape[dim], axis=dim)
        cells = jnp.concatenate(
            [
                lax.ppermute(tail, axis, [(i, (i + 1) % count) for i in range(ends)]),
                cells,
                lax.ppermute(head, axis, [((i + 1) % count, i) for i in range(ends)]),
            ],
            axis=dim,
        )
    return cells


def lift_axes(values):
    return values[:, None, None, None, None]


def total_cells(values):
    return jnp.sum(values, axis=tuple(range(1, values.ndim)))


def project(vector, magnet):
    return vector - jnp.sum(vector * magnet, axis=1, keepdims=True) * magnet


def angle_squared(first, second):
    normal_part = jnp.cross(first, second, axis=1)
    sine_value = jnp.sqrt(jnp.sum(normal_part * normal_part, axis=1))
    cosine = jnp.sum(first * second, axis=1)
    return jnp.arctan2(sine_value, cosine) ** 2


def tangent_weights(energy_total, energy_next, energy_prior):
    rise_next = energy_next - energy_total
    rise_prior = energy_total - energy_prior
    upward = (rise_next > 0) & (rise_prior > 0)
    downward = (rise_next < 0) & (rise_prior < 0)
    larger = jnp.maximum(jnp.abs(rise_next), jnp.abs(rise_prior))
    smaller = jnp.minimum(jnp.abs(rise_next), jnp.abs(rise_prior))
    toward_next = energy_next > energy_prior
    weight_next = jnp.where(
        upward, 1.0, jnp.where(downward, 0.0, jnp.where(toward_next, larger, smaller))
    )
    weight_prior = jnp.where(
        upward, 0.0, jnp.where(downward, 1.0, jnp.where(toward_next, smaller, larger))
    )
    return (weight_next, weight_prior)


def split_limbs(values):
    upper = values.astype(jnp.bfloat16)
    return upper, (values - upper.astype(jnp.float32)).astype(jnp.bfloat16)


def table_limbs(table):
    upper = table.astype(np.float32).astype(jnp.bfloat16)
    lower = (table - upper.astype(np.float64)).astype(np.float32).astype(jnp.bfloat16)
    return np.stack([upper, lower])


def parity_table(count):
    position = np.arange(count)[:, None]
    slot = np.arange(count)[None, :]
    turn = np.pi / count
    even_part = np.cos(turn * (position * slot % (2 * count)))
    odd_part = np.sin(turn * (position * slot % (2 * count)))
    odd_part[:, 0] = np.cos(turn * (position[:, 0] * count % (2 * count)))
    return np.concatenate([even_part, odd_part], axis=1)


def parity_weights(count):
    weights = np.full((2 * count,), 2.0)
    weights[0] = 1.0
    weights[count] = 1.0
    return weights


def half_table(count):
    place = np.arange(count)
    angle = np.pi * (place[:, None] * place[None, :] % (2 * count)) / count
    cosine, sine = np.cos(angle), np.sin(angle)
    cosine[np.abs(cosine) < 1e-12] = 0.0
    sine[np.abs(sine) < 1e-12] = 0.0
    return cosine, sine


def weighted(terms):
    total = None
    for weight, value in terms:
        weight = float(weight)
        if weight == 0.0:
            continue
        if total is None:
            total = value if weight == 1.0 else -value if weight == -1.0 else weight * value
        elif weight == 1.0:
            total = total + value
        elif weight == -1.0:
            total = total - value
        else:
            total = total + weight * value
    return total


def layers_to_spectrum(layers):
    count = len(layers)
    half = count // 2
    cosine, sine = half_table(count)
    sums = {z: layers[z] + layers[count - z] for z in range(1, half)}
    gaps = {z: layers[z] - layers[count - z] for z in range(1, half)}
    spectrum = []
    for k in range(count):
        near, far = (sums, gaps) if k % 2 == 0 else (gaps, sums)
        re = weighted(
            [(1.0, layers[0]), (cosine[half, k], layers[half])]
            + [(cosine[z, k], near[z]) for z in range(1, half)]
        )
        im = weighted(
            [(-sine[half, k], layers[half])] + [(-sine[z, k], far[z]) for z in range(1, half)]
        )
        spectrum.append((re, jnp.zeros_like(re) if im is None else im))
    return spectrum


def spectrum_to_layers(spectrum):
    count = len(spectrum)
    half = count // 2
    cosine, sine = half_table(count)
    layers = [None] * count
    evens, odds = range(2, count, 2), range(1, count, 2)
    layers[0] = weighted([(1.0, spectrum[0][0])] + [(2.0, spectrum[k][0]) for k in range(1, count)])
    layers[half] = weighted(
        [(1.0, spectrum[0][0])]
        + [(2.0 * cosine[half, k], spectrum[k][0]) for k in range(1, count)]
        + [(-2.0 * sine[half, k], spectrum[k][1]) for k in range(1, count)]
    )
    for z in range(1, half):
        even_re = weighted(
            [(1.0, spectrum[0][0])] + [(2.0 * cosine[z, k], spectrum[k][0]) for k in evens]
        )
        odd_re = weighted([(2.0 * cosine[z, k], spectrum[k][0]) for k in odds])
        even_im = weighted([(2.0 * sine[z, k], spectrum[k][1]) for k in evens])
        odd_im = weighted([(2.0 * sine[z, k], spectrum[k][1]) for k in odds])
        layers[z] = (even_re - odd_im) + (odd_re - even_im)
        layers[count - z] = (even_re - odd_im) - (odd_re - even_im)
    return layers


def dot32(left, right):
    return jnp.dot(left, right, preferred_element_type=jnp.float32)


def three_limbs(values, axis):
    upper, lower = split_limbs(values)
    return jnp.concatenate([upper, lower, upper], axis=axis)


def tensor_part(c, spec_ref, kernel_ref, out_ref):
    rows_full, columns_full = out_ref.shape[1] // 2, out_ref.shape[2] // 2
    lane = 128
    sub = 8
    row_pos = lax.broadcasted_iota(jnp.int32, (sub, lane), 0)
    lane_pos = lax.broadcasted_iota(jnp.int32, (sub, lane), 1)

    def step(i, carry):
        row_start = pl.multiple_of(i * sub, sub)
        top = (row_pos + row_start) == 0
        for start in range(0, columns_full, lane):

            def pick(component, odd_x, odd_y):
                def at(rows):
                    inner = kernel_ref[component, rows, start : start + lane]
                    if odd_y and start == 0:
                        edge = kernel_ref[component, rows, columns_full : columns_full + lane]
                        inner = jnp.where(lane_pos == 0, edge, inner)
                    return inner

                values = at(pl.ds(row_start, sub))
                if odd_x:
                    values = jnp.where(top, at(pl.ds(rows_full, sub)), values)
                return values

            def place(px, py):
                return (
                    pl.ds(row_start + px * rows_full, sub),
                    slice(py * columns_full + start, py * columns_full + start + lane),
                )

            def spec(px, py, f):
                rows, columns = place(px, py)
                return spec_ref[f, rows, columns]

            for px in range(2):
                for py in range(2):
                    sx = 1.0 if px else -1.0
                    sy = 1.0 if py else -1.0
                    own = pick(c, px, py)
                    if c < 2:
                        both = -(sx * sy) * pick(3, 0, 0)
                    if c != 1:
                        k_xz = sx * pick(4, 0, py)
                    if c != 0:
                        k_yz = sy * pick(5, px, 0)
                    for part in range(2):
                        turn = 1.0 if part else -1.0
                        other = 1 - part
                        total = own * spec(px, py, 2 * c + part)
                        if c == 0:
                            total = (
                                total
                                + both * spec(1 - px, 1 - py, 2 + part)
                                + turn * (k_xz * spec(1 - px, py, 4 + other))
                            )
                        elif c == 1:
                            total = (
                                both * spec(1 - px, 1 - py, part)
                                + total
                                + turn * (k_yz * spec(px, 1 - py, 4 + other))
                            )
                        else:
                            total = total + turn * (
                                k_xz * spec(1 - px, py, other) + k_yz * spec(px, 1 - py, 2 + other)
                            )
                        rows, columns = place(px, py)
                        out_ref[part, rows, columns] = total
        return carry

    lax.fori_loop(0, rows_full // sub, step, 0)


def demag_kernel(
    scale,
    magnet_ref,
    kernel_ref,
    fy_ref,
    fx_ref,
    gx_ref,
    gy_ref,
    out_ref,
    cells_ref,
    film_ref,
    stage_ref,
    pair_ref,
    extra_ref,
    send_ref,
    back_ref,
    held_ref,
    spec_ref,
    field_ref,
    tensor_ref,
    result_ref,
    own_sem,
    tensor_sem,
    film_send,
    film_recv,
    pair_send,
    pair_recv,
    plane_send,
    plane_recv,
    back_send,
    back_recv,
    extra_send,
    extra_recv,
    last_send,
    last_recv,
):
    groups, local_planes = held_ref.shape[1], held_ref.shape[2]
    slab, columns_full = held_ref.shape[4], held_ref.shape[5]
    layer_count = cells_ref.shape[2]
    rows_full = groups * slab
    parts = groups // 2
    me = lax.axis_index("space")
    half, seat = me // parts, lax.rem(me, parts)
    partner = lax.rem(me + parts, groups)
    flip = (1 - 2 * half).astype(jnp.float32)
    row_step = 8

    def remote(src, dst, send, recv, target):
        return pltpu.make_async_remote_copy(
            src_ref=src,
            dst_ref=dst,
            send_sem=send,
            recv_sem=recv,
            device_id={"space": target},
            device_id_type=pl.DeviceIdType.MESH,
        )

    def row_loop(step):
        def chunk(i, carry):
            step(pl.ds(pl.multiple_of(i * row_step, row_step), row_step))
            return carry

        lax.fori_loop(0, slab // row_step, chunk, 0)

    def own_copy(c):
        return pltpu.make_async_copy(magnet_ref.at[:, c], cells_ref.at[:, c], own_sem.at[c])

    def tensor_copy(q):
        return pltpu.make_async_copy(
            kernel_ref.at[:, q, pl.ds(0, rows_full + 8), pl.ds(0, columns_full + 128)],
            tensor_ref.at[q],
            tensor_sem.at[q],
        )

    def film_copy(c):
        return remote(
            magnet_ref.at[1 - half, c], film_ref.at[c], film_send.at[c], film_recv.at[c], partner
        )

    def pair_copy(side, source):
        return remote(
            stage_ref.at[side],
            pair_ref.at[source],
            pair_send.at[side],
            pair_recv.at[source],
            side * parts,
        )

    def place_of(seat_index, kind):
        return lax.rem((half + kind) * parts + seat_index, groups)

    def plane_copy(c, kind, slot):
        target = lax.rem(seat + 1 + slot, parts)
        return remote(
            send_ref.at[c, kind, slot],
            held_ref.at[c, place_of(seat, kind)],
            plane_send.at[c, kind, slot],
            plane_recv.at[c, kind, parts - 2 - slot],
            half * parts + target,
        )

    def plane_arrival(c, kind, slot):
        source = lax.rem(seat + 1 + slot, parts)
        return remote(
            send_ref.at[c, kind, slot],
            held_ref.at[c, place_of(source, kind)],
            plane_send.at[c, kind, slot],
            plane_recv.at[c, kind, slot],
            half * parts + source,
        )

    def back_copy(c, kind, slot):
        target = lax.rem(seat + 1 + slot, parts)
        return remote(
            held_ref.at[c, place_of(target, kind)],
            back_ref.at[c, kind, parts - 2 - slot],
            back_send.at[c, kind, slot],
            back_recv.at[c, kind, parts - 2 - slot],
            half * parts + target,
        )

    def back_arrival(c, kind, slot):
        source = lax.rem(seat + 1 + slot, parts)
        return remote(
            held_ref.at[c, place_of(source, kind)],
            back_ref.at[c, kind, slot],
            back_send.at[c, kind, slot],
            back_recv.at[c, kind, slot],
            half * parts + source,
        )

    def extra_copy(c, step):
        target = lax.rem(me + step, groups)
        return remote(
            held_ref.at[c, target, 0, 1],
            extra_ref.at[half, c],
            extra_send.at[c, step],
            extra_recv.at[half, c],
            target,
        )

    def extra_arrival(side, c):
        return remote(
            held_ref.at[c, 0, 0, 1],
            extra_ref.at[side, c],
            extra_send.at[c, 0],
            extra_recv.at[side, c],
            side * parts,
        )

    def last_copy(c):
        return remote(
            film_ref.at[c], field_ref.at[half, c], last_send.at[c], last_recv.at[c], partner
        )

    def last_arrival(c):
        return remote(
            film_ref.at[c], field_ref.at[1 - half, c], last_send.at[c], last_recv.at[c], partner
        )

    def transform_layers(c, kind):
        place = place_of(seat, kind)

        def variant(here):
            def step(rows):
                if kind == 0:
                    layers = [cells_ref[half, c, z, rows, :] for z in range(layer_count)]
                else:
                    layers = [film_ref[c, z, rows, :] for z in range(layer_count)]
                layers = [v * flip if z % 2 else v for z, v in enumerate(layers)]
                spectrum = layers_to_spectrum(layers)
                for k in range(layer_count):
                    target, q = k // local_planes, k % local_planes
                    slot = (target - here) % parts - 1
                    for part in range(2):
                        if target == here:
                            held_ref[c, place, q, part, rows, :] = spectrum[k][part]
                        else:
                            send_ref[c, kind, slot, q, part, rows, :] = spectrum[k][part]

            row_loop(step)

        for here in range(parts):
            pl.when(seat == here)(functools.partial(variant, here))
        for slot in range(parts - 1):
            plane_copy(c, kind, slot).start()

    def transform_planes(c, kind):
        place = place_of(seat, kind)

        def variant(here):
            def step(rows):
                spectrum = []
                for k in range(layer_count):
                    source, q = k // local_planes, k % local_planes
                    slot = (source - here) % parts - 1
                    if source == here:
                        spectrum.append(
                            [held_ref[c, place, q, part, rows, :] for part in range(2)]
                        )
                    else:
                        spectrum.append(
                            [back_ref[c, kind, slot, q, part, rows, :] for part in range(2)]
                        )
                for z, value in enumerate(spectrum_to_layers(spectrum)):
                    value = value * (scale * flip if z % 2 else scale)
                    if kind == 0:
                        field_ref[half, c, z, rows, :] = value
                    else:
                        film_ref[c, z, rows, :] = value

            row_loop(step)

        for here in range(parts):
            pl.when(seat == here)(functools.partial(variant, here))

    barrier = pltpu.get_barrier_semaphore()
    for d in range(1, groups):
        pl.semaphore_signal(
            barrier,
            inc=1,
            device_id={"space": lax.rem(me + d, groups)},
            device_id_type=pl.DeviceIdType.MESH,
        )
    for c in range(3):
        own_copy(c).start()
    pl.semaphore_wait(barrier, groups - 1)
    film_copy(0).start()
    for c in range(3):
        own_copy(c).wait()
    for side in range(2):

        def sum_layers(rows):
            for c in range(3):
                layers = [cells_ref[1 - side, c, z, rows, :] for z in range(layer_count)]
                stage_ref[side, c, rows, :] = weighted(
                    [((-1.0) ** (z * side), layers[z]) for z in range(layer_count)]
                )

        row_loop(sum_layers)

        @pl.when(me == side * parts)
        def _():
            pair_ref[me] = stage_ref[side]

        @pl.when(me != side * parts)
        def _():
            pair_copy(side, me).start()

    for c in range(1, 3):
        film_copy(c).start()
    for q in range(local_planes):
        tensor_copy(q).start()

    for c in range(3):
        transform_layers(c, 0)

    for c in range(3):
        film_copy(c).wait_recv()
        transform_layers(c, 1)
        for kind in range(2):
            for slot in range(parts - 1):
                plane_arrival(c, kind, slot).wait_recv()

        def forward(i, carry):
            q = local_planes - 1 - i

            @pl.when((seat == 0) & (q == 0))
            def _():
                if c == 0:
                    for d in range(1, groups):
                        pair_copy(0, lax.rem(me + d, groups)).wait_recv()
                for g in range(groups):
                    held_ref[c, g, 0, 1] = pair_ref[g, c]

            fy = jnp.concatenate([fy_ref[0], fy_ref[0], fy_ref[1]], axis=0)
            fx = jnp.concatenate([fx_ref[0], fx_ref[0], fx_ref[1]], axis=1)
            cells = jnp.concatenate(
                [held_ref[c, g, q, part] for part in range(2) for g in range(groups)], axis=0
            )
            lines = dot32(three_limbs(cells, 1), fy)
            for part in range(2):
                spec_ref[q, 2 * c + part] = dot32(
                    fx, three_limbs(lines[part * rows_full : (part + 1) * rows_full], 0)
                )
            return carry

        lax.fori_loop(0, local_planes, forward, 0)

    for q in range(local_planes):
        tensor_copy(q).wait()

    for c in range(3):

        def backward(q, carry):
            tensor_part(c, spec_ref.at[q], tensor_ref.at[q], result_ref)
            gx = jnp.concatenate([gx_ref[0], gx_ref[0], gx_ref[1]], axis=1)
            gy = jnp.concatenate([gy_ref[0], gy_ref[0], gy_ref[1]], axis=0)
            for part in range(2):
                lines = dot32(gx, three_limbs(result_ref[part], 0))
                cells = dot32(three_limbs(lines, 1), gy)
                for g in range(groups):
                    held_ref[c, g, q, part] = cells[g * slab : (g + 1) * slab]
            return carry

        lax.fori_loop(0, local_planes, backward, 0)
        for kind in (1, 0):
            for slot in range(parts - 1):
                back_copy(c, kind, slot).start()

        @pl.when(seat == 0)
        def _():
            extra_ref[half, c] = held_ref[c, me, 0, 1]
            for step in range(1, groups):
                extra_copy(c, step).start()

        for slot in range(parts - 1):
            back_arrival(c, 1, slot).wait_recv()
        transform_planes(c, 1)
        last_copy(c).start()
        for slot in range(parts - 1):
            back_arrival(c, 0, slot).wait_recv()
        transform_planes(c, 0)

    for c in range(3):
        last_arrival(c).wait_recv()
        for side in range(2):

            @pl.when(me != side * parts)
            def _():
                extra_arrival(side, c).wait_recv()

        for image in range(2):

            def add_extra(rows):
                extra = scale * extra_ref[1 - image, c, rows, :]
                for z in range(layer_count):
                    sign = (-1.0) ** (z * (1 - image))
                    value = field_ref[image, c, z, rows, :]
                    field_ref[image, c, z, rows, :] = value + extra if sign > 0 else value - extra

            row_loop(add_extra)
        pltpu.make_async_copy(field_ref.at[:, c], out_ref.at[:, c], own_sem.at[c]).start()

    for c in range(3):
        pltpu.make_async_copy(field_ref.at[:, c], out_ref.at[:, c], own_sem.at[c]).wait()
        film_copy(c).wait_send()
        last_copy(c).wait_send()
        for kind in range(2):
            for slot in range(parts - 1):
                plane_copy(c, kind, slot).wait_send()
                back_copy(c, kind, slot).wait_send()

    @pl.when(seat == 0)
    def _():
        for c in range(3):
            for step in range(1, groups):
                extra_copy(c, step).wait_send()

    for side in range(2):

        @pl.when(me != side * parts)
        def _():
            pair_copy(side, me).wait_send()


def demag_field(magnet, kernel):
    layer_count, row_count, column_count = magnet.shape[2:]
    groups = lax.axis_size("space")
    local_planes = 2 * layer_count // groups
    full_rows = row_count * groups
    slots = groups // 2 - 1
    table_y = parity_table(column_count)
    table_x = parity_table(full_rows)
    tables = [
        table_limbs(table_y),
        table_limbs(table_x.T),
        table_limbs(table_x * parity_weights(full_rows)[None, :]),
        table_limbs((table_y * parity_weights(column_count)[None, :]).T),
    ]
    slab = (row_count, column_count)
    film = (layer_count,) + slab
    block = (local_planes, 2) + slab
    anywhere = pl.BlockSpec(memory_space=pl.ANY)
    inside = pl.BlockSpec(memory_space=pltpu.VMEM)
    dots = 6 * local_planes * 4 * full_rows * column_count * 3 * (full_rows + column_count // 2)
    padded_cells = 8 * layer_count * full_rows * column_count
    signals = pltpu.SemaphoreType.DMA
    return pl.pallas_call(
        functools.partial(demag_kernel, -1.0 / padded_cells),
        in_specs=[anywhere, anywhere] + [inside] * len(tables),
        out_specs=anywhere,
        out_shape=jax.ShapeDtypeStruct(magnet.shape, jnp.float32),
        scratch_shapes=[
            pltpu.VMEM((2, 3) + film, jnp.float32),
            pltpu.VMEM((3,) + film, jnp.float32),
            pltpu.VMEM((2, 3) + slab, jnp.float32),
            pltpu.VMEM((groups, 3) + slab, jnp.float32),
            pltpu.VMEM((2, 3) + slab, jnp.float32),
            pltpu.VMEM((3, 2, slots) + block, jnp.float32),
            pltpu.VMEM((3, 2, slots) + block, jnp.float32),
            pltpu.VMEM((3, groups) + block, jnp.float32),
            pltpu.VMEM((local_planes, 6, 2 * full_rows, 2 * column_count), jnp.float32),
            pltpu.VMEM((2, 3) + film, jnp.float32),
            pltpu.VMEM((local_planes, 6, full_rows + 8, column_count + 128), jnp.float32),
            pltpu.VMEM((2, 2 * full_rows, 2 * column_count), jnp.float32),
            signals((3,)),
            signals((local_planes,)),
            signals((3,)),
            signals((3,)),
            signals((2,)),
            signals((groups,)),
            signals((3, 2, slots)),
            signals((3, 2, slots)),
            signals((3, 2, slots)),
            signals((3, 2, slots)),
            signals((3, groups)),
            signals((2, 3)),
            signals((3,)),
            signals((3,)),
        ],
        compiler_params=pltpu.CompilerParams(
            vmem_limit_bytes=67043328, collective_id=0, has_side_effects=True
        ),
        cost_estimate=pl.CostEstimate(
            flops=4 * dots, bytes_accessed=4 * magnet.size * 4, transcendentals=0
        ),
        name="demag_kernel",
    )(magnet, kernel, *[jnp.asarray(t) for t in tables])


def swap_kernel(shifts, combine, tile_ref, out_ref, held_ref, send_sem, recv_sem):
    groups, images = lax.axis_size("space"), lax.axis_size("image")
    me, image = lax.axis_index("space"), lax.axis_index("image")
    routes = [
        (n, shift, d)
        for n, shift in enumerate(shifts)
        for d in range(groups)
        if shift != 0 or d != 0
    ]

    def target(shift, d):
        return {"image": lax.rem(image - shift + images, images), "space": lax.rem(me + d, groups)}

    barrier = pltpu.get_barrier_semaphore()
    for n, shift, d in routes:
        pl.semaphore_signal(
            barrier, inc=1, device_id=target(shift, d), device_id_type=pl.DeviceIdType.MESH
        )
    pl.semaphore_wait(barrier, len(routes))

    def copy_of(n, shift, d, slot):
        return pltpu.make_async_remote_copy(
            src_ref=tile_ref,
            dst_ref=held_ref.at[n, slot],
            send_sem=send_sem.at[n, d],
            recv_sem=recv_sem.at[n, d],
            device_id=target(shift, d),
            device_id_type=pl.DeviceIdType.MESH,
        )

    for n, shift, d in routes:
        copy_of(n, shift, d, me).start()
    held_ref[shifts.index(0), me] = tile_ref[...]
    for n, shift, d in routes:
        copy_of(n, shift, d, lax.rem(me + groups - d, groups)).wait_recv()
    for n in range(len(shifts)):
        total = held_ref[n, 0]
        for g in range(1, groups):
            total = combine(total, held_ref[n, g])
        out_ref[n] = total
    for n, shift, d in routes:
        copy_of(n, shift, d, me).wait_send()


def swapped(values, shifts, combine, collective_id):
    rows, columns = values.shape
    tile = jnp.pad(values, ((0, -rows % 8), (0, -columns % 128)))
    groups = lax.axis_size("space")
    inside = pl.BlockSpec(memory_space=pltpu.VMEM)
    result = pl.pallas_call(
        functools.partial(swap_kernel, shifts, combine),
        in_specs=[inside],
        out_specs=inside,
        out_shape=jax.ShapeDtypeStruct((len(shifts),) + tile.shape, jnp.float32),
        scratch_shapes=[
            pltpu.VMEM((len(shifts), groups) + tile.shape, jnp.float32),
            pltpu.SemaphoreType.DMA((len(shifts), groups)),
            pltpu.SemaphoreType.DMA((len(shifts), groups)),
        ],
        compiler_params=pltpu.CompilerParams(
            collective_id=collective_id, has_side_effects=True
        ),
        name="swap_kernel",
    )(tile)
    return result[:, :rows, :columns]


def local_fields(magnet, anisotropy, rimmed):
    layer_count = magnet.shape[2]
    row_count = magnet.shape[3]
    column_count = magnet.shape[4]
    x_plus = rimmed[:, :, :, 2:]
    x_minus = rimmed[:, :, :, :-2]
    padded = jnp.pad(magnet, ((0, 0), (0, 0), (1, 1), (0, 0), (1, 1)))
    z_plus = padded[:, :, 2:, :, 1:-1]
    z_minus = padded[:, :, :-2, :, 1:-1]
    y_plus = padded[:, :, 1:-1, :, 2:]
    y_minus = padded[:, :, 1:-1, :, :-2]
    first_row = lax.axis_index("space") * row_count
    full_rows = row_count * lax.axis_size("space")
    layer_pos = lax.broadcasted_iota(jnp.int32, (layer_count, row_count, column_count), 0)
    row_pos = lax.broadcasted_iota(jnp.int32, (layer_count, row_count, column_count), 1) + first_row
    column_pos = lax.broadcasted_iota(jnp.int32, (layer_count, row_count, column_count), 2)
    boundary = (layer_pos == 0).astype(jnp.float32) + (layer_pos == layer_count - 1).astype(
        jnp.float32
    )
    boundary = (
        boundary
        + (row_pos == 0).astype(jnp.float32)
        + (row_pos == full_rows - 1).astype(jnp.float32)
    )
    boundary = (
        boundary
        + (column_pos == 0).astype(jnp.float32)
        + (column_pos == column_count - 1).astype(jnp.float32)
    )
    present = 6.0 - boundary
    neighbours = x_plus + x_minus + y_plus + y_minus + z_plus + z_minus
    exchange_part = exchange_strength * (neighbours - present * magnet)
    chiral_x = chiral_strength * (x_plus[:, 2] - x_minus[:, 2])
    chiral_y = chiral_strength * (y_plus[:, 2] - y_minus[:, 2])
    chiral_z = -chiral_strength * (x_plus[:, 0] - x_minus[:, 0] + (y_plus[:, 1] - y_minus[:, 1]))
    easy_axis = 2.0 * anisotropy[:, None] * magnet[:, 2]
    local_part = exchange_part + jnp.stack([chiral_x, chiral_y, chiral_z + easy_axis], axis=1)
    return local_part


def body(magnet, anisotropy, kernel):
    image_count = magnet.shape[0]
    cell_count = magnet.shape[2] * magnet.shape[3] * lax.axis_size("space") * magnet.shape[4]
    framed = extended(magnet, (("image", 0),), 1)
    rimmed = extended(magnet, (("space", 3),), 1)

    prior_image = framed[:-2]
    next_image = framed[2:]
    demag = demag_field(magnet, kernel)
    ahead = project(next_image - magnet, magnet)
    behind = project(magnet - prior_image, magnet)
    early = (
        local_fields(magnet, anisotropy, rimmed),
        total_cells(angle_squared(magnet, next_image)),
        total_cells(ahead * ahead),
        total_cells(ahead * behind),
        total_cells(behind * behind),
    )
    fields = early[0] + demag
    true_force = project(fields, magnet)
    tangent_next = project(next_image - magnet, magnet)
    tangent_prior = project(magnet - prior_image, magnet)
    sums = jnp.stack(
        [
            -0.5 * total_cells(magnet * fields),
            *early[1:],
            total_cells(true_force * tangent_next),
            total_cells(true_force * tangent_prior),
        ],
        axis=1,
    )
    band_size = image_count * lax.axis_size("image")
    swaps = swapped(sums, (-1, 0, 1), jnp.add, 64)
    band = jnp.concatenate([swaps[0, -1:], swaps[1], swaps[2, :1]], axis=0)
    energy_band, distance_band = band[:, 0], jnp.sqrt(band[:, 1] / cell_count)
    weight_next, weight_prior = tangent_weights(
        energy_band, jnp.roll(energy_band, -1), jnp.roll(energy_band, 1)
    )
    length_squares = (
        weight_next * weight_next * band[:, 2]
        + 2.0 * weight_next * weight_prior * band[:, 3]
        + weight_prior * weight_prior * band[:, 4]
    )
    drive_total = weight_next * band[:, 5] + weight_prior * band[:, 6]
    tangent_scale = jnp.sqrt(jnp.maximum(length_squares, 0.0) / cell_count + epsilon)
    parallel = drive_total / (cell_count * tangent_scale)
    spring = spring_strength * (distance_band - jnp.roll(distance_band, 1))
    first_image = lax.axis_index("image") * image_count
    image_index = first_image - 1 + jnp.arange(image_count + 2)
    interior = ((image_index > 0) & (image_index < band_size - 1)).astype(jnp.float32)
    pull = (spring - parallel) / tangent_scale
    mine = jnp.stack([energy_band, pull * weight_next, pull * weight_prior, interior], axis=1)[1:-1]
    energy_total = mine[:, 0]
    band_force = jnp.where(
        lift_axes(mine[:, 3]) > 0.0,
        true_force + lift_axes(mine[:, 1]) * tangent_next + lift_axes(mine[:, 2]) * tangent_prior,
        0.0,
    )
    local_largest = jnp.max(jnp.sqrt(jnp.sum(band_force * band_force, axis=1)), axis=(1, 2, 3))
    largest = swapped(local_largest[None, :], (0,), jnp.maximum, 65)[0, 0]
    move_scale = jnp.minimum(step_limit, rotation_limit / (largest + epsilon))
    stepped = magnet + lift_axes(move_scale) * band_force
    updated = stepped / jnp.sqrt(jnp.sum(stepped * stepped, axis=1, keepdims=True))
    return (updated, band_force, energy_total / cell_count)


def solution(mesh):
    in_specs = (P("image", None, None, "space", None), P("space"), P(None, "space", None, None))
    out_specs = (
        P("image", None, None, "space", None),
        P("image", None, None, "space", None),
        P("image"),
    )
    return jax.shard_map(body, mesh=mesh, in_specs=in_specs, out_specs=out_specs, check_vma=False)
```

time: 242 us -> 198 us (0.82)
  waiting for transfers between devices: 37.1 us -> 0.01 us
  other arithmetic: 59.1 us -> 45.9 us
  starting transfers between devices: 20.7 us -> 12.9 us
  Pallas kernels: 111 us -> 118 us
  local copies, waits for them, and re-layouts: 13.3 us -> 19.9 us
    all_to_all x1 -> x0, waiting for transfers between devices: 37.1 us -> none  [demag_pair(): lax.all_to_all(planes, 'space', split_axis=0, concat_axis=0, tiled=True)]
    all_to_all x1 -> x0, starting transfers between devices: 10.6 us -> none  [demag_pair(): lax.all_to_all(planes, 'space', split_axis=0, concat_axis=0, tiled=True)]
    pallas_call x3 -> x1, Pallas kernels: 94.2 us -> 104 us  [demag_field(): pl.pallas_call(functools.partial(demag_kernel, -1.0 / padded_cells), in_s...]
    concatenate x2 -> x0, other arithmetic: 7.65 us -> none  [extended(): jnp.concatenate([lax.ppermute(tail, axis, [(i, (i + 1) % count) for i in...]
    unnamed x25 -> x12, local copies, waits for them, and re-layouts: 3.81 us -> 7.96 us
    reduce_sum x4 -> x2, other arithmetic: 13.5 us -> 9.81 us  [total_cells(): return jnp.sum(values, axis=tuple(range(1, values.ndim)))]
    ppermute x2, starting transfers between devices: 7.55 us -> 10.3 us  [extended(): lax.ppermute(tail, axis, [(i, (i + 1) % count) for i in range(ends)])]
    slice x2 -> x1, local copies, waits for them, and re-layouts: 5.09 us -> 3.89 us  [extended(): lax.slice_in_dim(cells, cells.shape[dim] - width, cells.shape[dim], axis=...]
  transfers between devices with their start and end apart: 5 -> 4, of which waited for: 1 -> 0; matrix products, arithmetic and copies ran while one was open for 14% -> 9% of each run, Pallas kernels for 36% -> 53%
where the time goes in v1:
time: 198 us
  Pallas kernels  118 us (60%)
  other arithmetic  45.9 us (23%)
  local copies, waits for them, and re-layouts  19.9 us (10%)
  starting transfers between devices  12.9 us (7%)
    pallas_call x1, Pallas kernels, demag_field(): pl.pallas_call(functools.partial(demag_kernel, -1.0 / padded_cells), in_s...  104 us
    pallas_call x2, Pallas kernels, swapped(): pl.pallas_call(functools.partial(swap_kernel, shifts, combine), in_specs=...  14.1 us
    reduce_sum x1, other arithmetic, angle_squared(): cosine = jnp.sum(first * second, axis=1)  10.9 us
    ppermute x2, starting transfers between devices, extended(): lax.ppermute(tail, axis, [(i, (i + 1) % count) for i in range(ends)])  10.3 us
    reduce_sum x2, other arithmetic, total_cells(): return jnp.sum(values, axis=tuple(range(1, values.ndim)))  9.81 us
    unnamed x12, local copies, waits for them, and re-layouts  7.96 us
    reduce_sum x1, other arithmetic, body(): jnp.sum(band_force * band_force, axis=1)  7.01 us
    mul x1, other arithmetic, local_fields(): chiral_x = chiral_strength * (x_plus[:, 2] - x_minus[:, 2])  4.45 us
  transfers between devices with their start and end apart: 4, of which 0 were waited for; matrix products, arithmetic and copies ran while one was open for 9% of the time, Pallas kernels for 53%

profile of v1, /device:TPU:0, one launch (start us, length us, event | category | flops | bytes accessed | tf_op | source)
XLA Modules:
  0.0 197.6 jit_solution(12861192567172739634)
XLA Ops:
  0.6 1.8 fusion.47
  2.5 1.3 collective-permute-start
  3.7 3.7 %collective-permute-start.1 = (f32[2,3,8,1,256]{4,3,2,1,0:T(1,128)}, f32[2,3,8,1,256]{4,3,2,1,0:T(1,128)}, u32[]{:S(2)}, u32[]{:S(2)}) collective-permute-start(f32[2,3,8,1,256]{4,3,2,1,0:T(1,128)} %get-tuple-element.33), channel_id=1, source_target_pairs={{0,1},{1,2},{2,3},{4,5},{5,6},{6,7},{8,9},{9,10},{10,11},{12,13},{... | collective-permute-start | bytes 147464 | tf_op jit(solution)/shard_map/ppermute | solution.py:27
  7.4 3.9 %fusion.48 = (f32[1,3,8,64,256]{4,3,2,1,0:T(8,128)}, f32[1,3,8,64,256]{4,3,2,1,0:T(8,128)}) fusion(f32[2,3,8,64,256]{4,3,2,1,0:T(8,128)} %magnet_ref.1), kind=kLoop, calls=%fused_computation.116 | loop fusion | bytes 6291456 | tf_op jit(solution)/shard_map/slice | solution.py:24
  11.3 1.3 collective-permute-start.2
  12.6 6.7 %collective-permute-start.3 = (f32[1,3,8,64,256]{4,3,2,1,0:T(8,128)}, f32[1,3,8,64,256]{4,3,2,1,0:T(8,128)}, u32[]{:S(2)}, u32[]{:S(2)}) collective-permute-start(f32[1,3,8,64,256]{4,3,2,1,0:T(8,128)} %get-tuple-element.34), channel_id=1, source_target_pairs={{0,4},{4,8},{8,12},{12,16},{16,20},{20,24},{24,28},{1,5},{5,9},{9,... | collective-permute-start | bytes 4718600 | tf_op jit(solution)/shard_map/ppermute | solution.py:27
  19.3 104.0 %demag_kernel.1 = f32[2,3,8,64,256]{4,3,2,1,0:T(8,128)} custom-call(f32[2,3,8,64,256]{4,3,2,1,0:T(8,128)} %magnet_ref.1, f32[6,4,512,512]{3,2,1,0:T(8,128)} %kernel_ref.1, bf16[2,256,512]{2,1,0:T(8,128)(2,1)} %constant.71.clone.fy_ref, bf16[2,512,256]{2,1,0:T(8,128)(2,1)} %constant.72.clone.fx_ref, bf16[2,256,512]{2,1,0:T(8,128)(2,1)} %constant.73.clone.gx_ref, ...), custom_call_target="tpu_custom_call" | custom-call | flops 28991029248 | bytes 12582912 | tf_op jit(solution)/shard_map/demag_kernel/pallas_call | solution.py:640
  123.3 0.7 broadcast_multiply_fusion
  124.1 0.9 add_subtract_fusion
  125.0 4.0 %constant_dynamic-update-slice_fusion = f32[2,3,8,65,256]{4,3,2,1,0:T(8,128)} fusion(f32[2,3,8,64,256]{4,3,2,1,0:T(8,128)} %magnet_ref.1), kind=kLoop, calls=%fused_computation.74 | loop fusion | bytes 6291456
  129.0 1.9 copy.76
  130.9 1.9 dynamic-update-slice.1
  132.9 4.5 %fusion.24 = (f32[2,1,8,64,256]{4,3,2,1,0:T(8,128)}, f32[2,1,8,64,256]{4,3,2,1,0:T(8,128)}, f32[2,1,8,64,256]{4,3,2,1,0:T(8,128)}) fusion(f32[2,3,8,64,256]{4,3,2,1,0:T(8,128)S(1)} %copy-done, f32[2,3,8,1,256]{4,3,2,1,0:T(1,128)} %collective-permute-done.1, f32[2,3,8,65,256]{4,3,2,1,0:T(8,128)} %dynamic-update-slice.1, f32[64]{0:T(128)S(1)} %broadcast_multiply_fusion), kind=kLoop, calls=%fused_computation.53 | loop fusion | flops 3145728 | bytes 9486848 | tf_op jit(solution)/shard_map/mul | solution.py:782
  137.3 10.9 %fusion.20 = (f32[2,8,64,256]{3,2,1,0:T(8,128)}, f32[2,8,64,256]{3,2,1,0:T(8,128)}, f32[2,8,64,256]{3,2,1,0:T(8,128)}, f32[2,8,64,256]{3,2,1,0:T(8,128)}, f32[2]...) fusion(f32[2,3,8,64,256]{4,3,2,1,0:T(8,128)S(1)} %copy-done, ...), kind=kLoop, calls=%fused_computation.34 | loop fusion | flops 19398654 | bytes 26787848 | tf_op jit(solution)/shard_map/reduce_sum | solution.py:51
  148.2 3.5 %subtract_bitcast_fusion = (f32[1,2,8,64,256]{4,3,2,1,0:T(8,128)S(1)}, f32[1,2,8,64,256]{4,3,2,1,0:T(8,128)S(1)}) fusion(f32[2,8,64,256,3]{3,2,1,4,0:T(8,128)} %get-tuple-element.30, f32[2,8,64,256,3]{3,2,1,0,4:T(8,128)} %bitcast.61), kind=kLoop, calls=%fused_computation.72 | loop fusion | flops 1572864 | bytes 8388608 | tf_op jit(solution)/shard_map/jit(cross)/sub | solution.py:49
  151.7 0.2 copy-done.2
  152.0 1.0 copy-done.3
  152.9 0.3 fusion.33
  153.2 0.4 fusion.21
  153.6 0.8 copy-done.4
  154.4 1.9 multiply_reduce_fusion.9
  156.4 0.1 copy.67
  156.5 7.9 %multiply_reduce_fusion.2 = (f32[2]{0:T(128)S(1)}, f32[2]{0:T(128)S(1)}, f32[2]{0:T(128)S(1)}, f32[2]{0:T(128)S(1)}, f32[2]{0:T(128)S(1)}, /*index=5*/f32[2,3,8,...) fusion(f32[2,3,8,64,256]{4,3,2,1,0:T(8,128)S(1)} %copy-done, ...), kind=kLoop, calls=%fused_computation.42 | loop fusion | flops 15728630 | bytes 22020136 | tf_op jit(solution)/shard_map/reduce_sum | solution.py:41
  164.3 0.1 copy.68
  164.4 0.1 copy.69
  164.5 0.1 copy.70
  164.6 0.1 copy.71
  164.7 0.1 copy.72
  164.8 0.1 copy.66
  164.9 0.1 stack.39
  165.0 0.6 pad.13.tile_ref
  165.6 9.1 %swap_kernel.2 = f32[3,8,128]{2,1,0:T(8,128)} custom-call(f32[8,128]{1,0:T(8,128)} %pad.13.tile_ref), custom_call_target="tpu_custom_call" | custom-call | tf_op jit(solution)/shard_map/swap_kernel/pallas_call | solution.py:732
  174.7 0.7 slice_bitcast_fusion.4
  175.4 0.7 slice_bitcast_fusion.2
  176.1 0.6 multiply_reduce_fusion.10
  176.7 0.1 select_select_fusion.1
  176.9 0.5 slice.231
  177.3 0.6 fusion.41
  178.0 0.1 slice_reduce_fusion
  178.1 0.1 slice_reduce_fusion.1
  178.2 7.0 %multiply_reduce_fusion.1 = (f32[2,8,64,256]{3,2,1,0:T(8,128)S(1)}, f32[2,3,8,64,256]{4,3,2,1,0:T(8,128)}) fusion(f32[2,3,8,64,256]{4,3,2,1,0:T(8,128)} %get-tuple-element.24, f32[2]{0:T(128)S(1)} %slice_reduce_fusion, f32[2,3,8,64,256]{4,3,2,1,0:T(8,128)} %get-tuple-element.23, f32[2,3,8,64,256]{4,3,2,1,0:T(8,128)} %get-tuple-element.22, ...), kind=kLoop, calls=%fused_computation.40 | loop fusion | flops 5242880 | bytes 13631506 | tf_op jit(solution)/shard_map/reduce_sum | solution.py:848
  185.2 0.4 sqrt_reduce_fusion
  185.6 0.6 pad.14.tile_ref
  186.2 5.0 %swap_kernel.3 = f32[1,8,128]{2,1,0:T(8,128)} custom-call(f32[8,128]{1,0:T(8,128)} %pad.14.tile_ref), custom_call_target="tpu_custom_call" | custom-call | tf_op jit(solution)/shard_map/swap_kernel/pallas_call | solution.py:732
  191.2 0.7 minimum_bitcast_fusion
  191.9 3.0 %multiply_reduce_fusion = f32[2,8,64,256]{3,2,1,0:T(8,128)S(1)} fusion(f32[2,3,8,64,256]{4,3,2,1,0:T(8,128)S(1)} %copy-done, f32[2,3,8,64,256]{4,3,2,1,0:T(8,128)} %get-tuple-element.16, f32[2]{0:T(128)S(1)} %minimum_bitcast_fusion), kind=kLoop, calls=%fused_computation.38 | loop fusion | flops 2883584 | bytes 7340040 | tf_op jit(solution)/shard_map/reduce_sum | solution.py:852
  194.8 0.2 sqrt.29
  195.1 2.5 %broadcast_divide_fusion = f32[2,3,8,64,256]{4,3,2,1,0:T(8,128)} fusion(f32[2,8,64,256]{3,2,1,0:T(8,128)S(1)} %sqrt.29, f32[2,3,8,64,256]{4,3,2,1,0:T(8,128)S(1)} %copy-done, f32[2,3,8,64,256]{4,3,2,1,0:T(8,128)S(1)} %copy-done.1, f32[2]{0:T(128)S(1)} %minimum_bitcast_fusion), kind=kLoop, calls=%fused_computation.48 | loop fusion | flops 2359296 | bytes 10485768 | tf_op jit(solution)/shard_map/div | solution.py:852
  (20 shorter events, 0.2 us)
Async XLA Ops:
  2.5 128.5 %collective-permute-start = (f32[2,3,8,1,256]{4,3,2,1,0:T(1,128)}, f32[2,3,8,1,256]{4,3,2,1,0:T(1,128)}, u32[]{:S(2)}, u32[]{:S(2)}) collective-permute-start(f32[2,3,8,1,256]{4,3,2,1,0:T(1,128)} %get-tuple-element.32), channel_id=1, source_target_pairs={{1,0},{2,1},{3,2},{5,4},{6,5},{7,6},{9,8},{10,9},{11,10},{13,12},{... | collective-permute-start | bytes 147464 | tf_op jit(solution)/shard_map/ppermute | solution.py:29
  3.7 129.1 %collective-permute-start.1 = (f32[2,3,8,1,256]{4,3,2,1,0:T(1,128)}, f32[2,3,8,1,256]{4,3,2,1,0:T(1,128)}, u32[]{:S(2)}, u32[]{:S(2)}) collective-permute-start(f32[2,3,8,1,256]{4,3,2,1,0:T(1,128)} %get-tuple-element.33), channel_id=1, source_target_pairs={{0,1},{1,2},{2,3},{4,5},{5,6},{6,7},{8,9},{9,10},{10,11},{12,13},{... | collective-permute-start | bytes 147464 | tf_op jit(solution)/shard_map/ppermute | solution.py:27
  11.3 126.0 %collective-permute-start.2 = (f32[1,3,8,64,256]{4,3,2,1,0:T(8,128)}, f32[1,3,8,64,256]{4,3,2,1,0:T(8,128)}, u32[]{:S(2)}, u32[]{:S(2)}) collective-permute-start(f32[1,3,8,64,256]{4,3,2,1,0:T(8,128)} %get-tuple-element.35), channel_id=1, source_target_pairs={{4,0},{8,4},{12,8},{16,12},{20,16},{24,20},{28,24},{5,1},{9,5},{13... | collective-permute-start | bytes 4718600 | tf_op jit(solution)/shard_map/ppermute | solution.py:29
  12.6 124.8 %collective-permute-start.3 = (f32[1,3,8,64,256]{4,3,2,1,0:T(8,128)}, f32[1,3,8,64,256]{4,3,2,1,0:T(8,128)}, u32[]{:S(2)}, u32[]{:S(2)}) collective-permute-start(f32[1,3,8,64,256]{4,3,2,1,0:T(8,128)} %get-tuple-element.34), channel_id=1, source_target_pairs={{0,4},{4,8},{8,12},{12,16},{16,20},{20,24},{24,28},{1,5},{5,9},{9,... | collective-permute-start | bytes 4718600 | tf_op jit(solution)/shard_map/ppermute | solution.py:27
  125.0 4.0 %copy-start = (f32[2,3,8,64,256]{4,3,2,1,0:T(8,128)S(1)}, f32[2,3,8,64,256]{4,3,2,1,0:T(8,128)}, u32[]{:S(2)}) copy-start(f32[2,3,8,64,256]{4,3,2,1,0:T(8,128)} %magnet_ref.1) | copy-start | bytes 9437188
  148.2 3.8 %copy-start.2 = (f32[2,8,64,256,3]{3,2,1,4,0:T(8,128)S(1)}, f32[2,8,64,256,3]{3,2,1,4,0:T(8,128)}, u32[]{:S(2)}) copy-start(f32[2,8,64,256,3]{3,2,1,4,0:T(8,128)} %get-tuple-element.30) | copy-start | bytes 9437188
  148.2 4.7 %copy-start.3 = (f32[2,3,8,64,256]{4,3,2,0,1:T(8,128)S(1)}, f32[2,3,8,64,256]{4,3,2,0,1:T(8,128)}, u32[]{:S(2)}) copy-start(f32[2,3,8,64,256]{4,3,2,0,1:T(8,128)} %copy.76) | copy-start | bytes 9437188
  153.2 1.2 copy-start.4
  191.9 3.2 %copy-start.1 = (f32[2,3,8,64,256]{4,3,2,1,0:T(8,128)S(1)}, f32[2,3,8,64,256]{4,3,2,1,0:T(8,128)}, u32[]{:S(2)}) copy-start(f32[2,3,8,64,256]{4,3,2,1,0:T(8,128)} %get-tuple-element.16) | copy-start | bytes 9437188

commit v2 on v1

--- a/solution.py
+++ b/solution.py
@@ -1,4 +1,5 @@
 import functools
+import math
 
 import jax
 import jax.numpy as jnp
@@ -16,40 +17,8 @@
 epsilon = 1e-06
 
 
-def extended(cells, sides, width):
-    for axis, dim in sides:
-        count = lax.axis_size(axis)
-        ends = count - 1
-        head = lax.slice_in_dim(cells, 0, width, axis=dim)
-        tail = lax.slice_in_dim(cells, cells.shape[dim] - width, cells.shape[dim], axis=dim)
-        cells = jnp.concatenate(
-            [
-                lax.ppermute(tail, axis, [(i, (i + 1) % count) for i in range(ends)]),
-                cells,
-                lax.ppermute(head, axis, [((i + 1) % count, i) for i in range(ends)]),
-            ],
-            axis=dim,
-        )
-    return cells
-
-
 def lift_axes(values):
     return values[:, None, None, None, None]
-
-
-def total_cells(values):
-    return jnp.sum(values, axis=tuple(range(1, values.ndim)))
-
-
-def project(vector, magnet):
-    return vector - jnp.sum(vector * magnet, axis=1, keepdims=True) * magnet
-
-
-def angle_squared(first, second):
-    normal_part = jnp.cross(first, second, axis=1)
-    sine_value = jnp.sqrt(jnp.sum(normal_part * normal_part, axis=1))
-    cosine = jnp.sum(first * second, axis=1)
-    return jnp.arctan2(sine_value, cosine) ** 2
 
 
 def tangent_weights(energy_total, energy_next, energy_prior):
@@ -88,13 +57,6 @@
     odd_part = np.sin(turn * (position * slot % (2 * count)))
     odd_part[:, 0] = np.cos(turn * (position[:, 0] * count % (2 * count)))
     return np.concatenate([even_part, odd_part], axis=1)
-
-
-def parity_weights(count):
-    weights = np.full((2 * count,), 2.0)
-    weights[0] = 1.0
-    weights[count] = 1.0
-    return weights
 
 
 def half_table(count):
@@ -242,6 +204,9 @@
                             total = total + turn * (
                                 k_xz * spec(1 - px, py, other) + k_yz * spec(px, 1 - py, 2 + other)
                             )
+                        total = jnp.where(top, 0.5 * total, total)
+                        if start == 0:
+                            total = jnp.where(lane_pos == 0, 0.5 * total, total)
                         rows, columns = place(px, py)
                         out_ref[part, rows, columns] = total
         return carry
@@ -249,15 +214,35 @@
     lax.fori_loop(0, rows_full // sub, step, 0)
 
 
-def demag_kernel(
+def arc_angle(sine, cosine):
+    size = jnp.abs(cosine)
+    low, high = jnp.minimum(sine, size), jnp.maximum(sine, size)
+    ratio = low / jnp.maximum(high, 1e-37)
+    wide = ratio > 0.41421356
+    ratio = jnp.where(wide, (ratio - 1.0) / (ratio + 1.0), ratio)
+    square = ratio * ratio
+    series = ((8.05374449538e-2 * square - 1.38776856032e-1) * square + 1.99777106478e-1) * square
+    angle = (series - 3.33329491539e-1) * square * ratio + ratio
+    angle = jnp.where(wide, angle + 0.25 * math.pi, angle)
+    angle = jnp.where(sine > size, 0.5 * math.pi - angle, angle)
+    return jnp.where(cosine < 0.0, math.pi - angle, angle)
+
+
+def dot3(first, second):
+    return first[0] * second[0] + first[1] * second[1] + first[2] * second[2]
+
+
+def band_kernel(
     scale,
     magnet_ref,
     kernel_ref,
+    ease_ref,
     fy_ref,
     fx_ref,
     gx_ref,
     gy_ref,
-    out_ref,
+    force_ref,
+    small_ref,
     cells_ref,
     film_ref,
     stage_ref,
@@ -268,6 +253,16 @@
     held_ref,
     spec_ref,
     field_ref,
+    arrive_ref,
+    next_ref,
+    prior_ref,
+    rim_out_ref,
+    rim_ref,
+    present_ref,
+    sums_ref,
+    tile_ref,
+    swap_ref,
+    peak_ref,
     tensor_ref,
     result_ref,
     own_sem,
@@ -284,6 +279,15 @@
     extra_recv,
     last_send,
     last_recv,
+    image_send,
+    image_recv,
+    rim_send,
+    rim_recv,
+    swap_send,
+    swap_recv,
+    peak_send,
+    peak_recv,
+    force_sem,
 ):
     groups, local_planes = held_ref.shape[1], held_ref.shape[2]
     slab, columns_full = held_ref.shape[4], held_ref.shape[5]
@@ -295,6 +299,18 @@
     partner = lax.rem(me + parts, groups)
     flip = (1 - 2 * half).astype(jnp.float32)
     row_step = 8
+    images, image = lax.axis_size("image"), lax.axis_index("image")
+    first, last = image == 0, image == images - 1
+    shifts = (-1, 0, 1)
+    routes = [
+        (n, shift, d)
+        for n, shift in enumerate(shifts)
+        for d in range(groups)
+        if shift != 0 or d != 0
+    ]
+
+    def target_of(shift, d):
+        return {"image": lax.rem(image - shift + images, images), "space": lax.rem(me + d, groups)}
 
     def remote(src, dst, send, recv, target):
         return pltpu.make_async_remote_copy(
@@ -302,7 +318,7 @@
             dst_ref=dst,
             send_sem=send,
             recv_sem=recv,
-            device_id={"space": target},
+            device_id=target if isinstance(target, dict) else {"space": target},
             device_id_type=pl.DeviceIdType.MESH,
         )
 
@@ -401,13 +417,52 @@
 
     def last_copy(c):
         return remote(
-            film_ref.at[c], field_ref.at[half, c], last_send.at[c], last_recv.at[c], partner
-        )
-
-    def last_arrival(c):
-        return remote(
-            film_ref.at[c], field_ref.at[1 - half, c], last_send.at[c], last_recv.at[c], partner
-        )
+            film_ref.at[c], arrive_ref.at[c], last_send.at[c], last_recv.at[c], partner
+        )
+
+    def ahead_copy():
+        return remote(
+            magnet_ref.at[1],
+            prior_ref,
+            image_send.at[0],
+            image_recv.at[0],
+            {"image": lax.rem(image + 1, images)},
+        )
+
+    def behind_copy():
+        return remote(
+            magnet_ref.at[0],
+            next_ref,
+            image_send.at[1],
+            image_recv.at[1],
+            {"image": lax.rem(image + images - 1, images)},
+        )
+
+    def rim_copy(side):
+        return remote(
+            rim_out_ref.at[side],
+            rim_ref.at[side],
+            rim_send.at[side],
+            rim_recv.at[side],
+            lax.rem(me + (1 if side == 0 else groups - 1), groups),
+        )
+
+    def swap_copy(n, shift, d, slot):
+        return remote(
+            tile_ref, swap_ref.at[n, slot], swap_send.at[n, d], swap_recv.at[n, d], target_of(shift, d)
+        )
+
+    def peak_copy(d, slot):
+        return remote(
+            tile_ref.at[pl.ds(0, 8)],
+            peak_ref.at[slot],
+            peak_send.at[d],
+            peak_recv.at[d],
+            lax.rem(me + d, groups),
+        )
+
+    def force_copy(i):
+        return pltpu.make_async_copy(field_ref.at[i], force_ref.at[i], force_sem.at[i])
 
     def transform_layers(c, kind):
         place = place_of(seat, kind)
@@ -456,7 +511,7 @@
                 for z, value in enumerate(spectrum_to_layers(spectrum)):
                     value = value * (scale * flip if z % 2 else scale)
                     if kind == 0:
-                        field_ref[half, c, z, rows, :] = value
+                        field_ref[half, c, z, rows, :] = field_ref[half, c, z, rows, :] + value
                     else:
                         film_ref[c, z, rows, :] = value
 
@@ -465,20 +520,207 @@
         for here in range(parts):
             pl.when(seat == here)(functools.partial(variant, here))
 
+    def fill_rims():
+        def step(f, carry):
+            i, c = f // 3, lax.rem(f, 3)
+            for side in range(2):
+                row = slab - 1 if side == 0 else 0
+                rim_out_ref[side, i, c] = jnp.concatenate(
+                    [cells_ref[i, c, z, row : row + 1, :] for z in range(layer_count)], axis=0
+                )
+            return carry
+
+        lax.fori_loop(0, 6, step, 0)
+        row_pos = lax.broadcasted_iota(jnp.int32, (slab, columns_full), 0) + me * slab
+        column_pos = lax.broadcasted_iota(jnp.int32, (slab, columns_full), 1)
+        faces = [row_pos == 0, row_pos == rows_full - 1]
+        faces += [column_pos == 0, column_pos == columns_full - 1]
+        present_ref[...] = 6.0 - sum(jnp.where(face, 1.0, 0.0) for face in faces)
+        for side in range(2):
+            open_side = me != groups - 1 if side == 0 else me != 0
+
+            @pl.when(open_side)
+            def _():
+                rim_copy(side).start()
+
+            no_source = me == 0 if side == 0 else me == groups - 1
+
+            @pl.when(no_source)
+            def _():
+                rim_ref[side] = jnp.zeros(rim_ref.shape[1:], jnp.float32)
+
+    def local_fields():
+        for side in range(2):
+            has_source = me != 0 if side == 0 else me != groups - 1
+
+            @pl.when(has_source)
+            def _():
+                rim_copy(side).wait_recv()
+
+        row_pos = lax.broadcasted_iota(jnp.int32, (slab, columns_full), 0)
+        column_pos = lax.broadcasted_iota(jnp.int32, (slab, columns_full), 1)
+
+        def step(index, carry):
+            i, z = index // layer_count, lax.rem(index, layer_count)
+            below, above = jnp.maximum(z - 1, 0), jnp.minimum(z + 1, layer_count - 1)
+            has_below = (z > 0).astype(jnp.float32)
+            has_above = (z < layer_count - 1).astype(jnp.float32)
+            present = present_ref[...] - (2.0 - has_below - has_above)
+            tilt = []
+            for c in range(3):
+                cells = cells_ref[i, c, z]
+                x_plus = jnp.where(
+                    row_pos == slab - 1,
+                    rim_ref[1, i, c, pl.ds(z, 1), :],
+                    pltpu.roll(cells, slab - 1, 0),
+                )
+                x_minus = jnp.where(
+                    row_pos == 0, rim_ref[0, i, c, pl.ds(z, 1), :], pltpu.roll(cells, 1, 0)
+                )
+                y_plus = jnp.where(
+                    column_pos == columns_full - 1, 0.0, pltpu.roll(cells, columns_full - 1, 1)
+                )
+                y_minus = jnp.where(column_pos == 0, 0.0, pltpu.roll(cells, 1, 1))
+                around = x_plus + x_minus + y_plus + y_minus
+                around = around + has_above * cells_ref[i, c, above] + has_below * cells_ref[i, c, below]
+                part = exchange_strength * (around - present * cells)
+                if c == 0:
+                    tilt.append(x_plus - x_minus)
+                    field_ref[i, 0, z] = part
+                elif c == 1:
+                    tilt.append(y_plus - y_minus)
+                    field_ref[i, 1, z] = part
+                else:
+                    ease = 2.0 * ease_ref[...] * cells
+                    field_ref[i, 2, z] = part + (ease - chiral_strength * (tilt[0] + tilt[1]))
+                    field_ref[i, 0, z] = field_ref[i, 0, z] + chiral_strength * (x_plus - x_minus)
+                    field_ref[i, 1, z] = field_ref[i, 1, z] + chiral_strength * (y_plus - y_minus)
+            return carry
+
+        lax.fori_loop(0, 2 * layer_count, step, 0)
+
+    lane = columns_full
+
+    def cell_loop(step, carry):
+        steps = slab // row_step
+
+        def chunk(index, carry):
+            z = index // steps
+            start = pl.multiple_of(lax.rem(index, steps) * row_step, row_step)
+            return step(z, start, carry)
+
+        return lax.fori_loop(0, layer_count * steps, chunk, carry)
+
+    def zeros(count):
+        return tuple(jnp.zeros((row_step, lane), jnp.float32) for _ in range(count))
+
+    def tangent_rows(z, start):
+        return pl.ds(pl.multiple_of(z * slab + start, row_step), row_step)
+
+    def neighbour_sums():
+        @pl.when(jnp.logical_not(first))
+        def _():
+            ahead_copy().wait_recv()
+
+        @pl.when(first)
+        def _():
+            for c in range(3):
+                prior_ref[c] = cells_ref[0, c]
+
+        @pl.when(jnp.logical_not(last))
+        def _():
+            behind_copy().wait_recv()
+
+        @pl.when(last)
+        def _():
+            for c in range(3):
+                next_ref[c] = cells_ref[1, c]
+
+        for i in range(2):
+
+            def step(z, start, carry):
+                rows = pl.ds(start, row_step)
+                here = [cells_ref[i, c, z, rows, :] for c in range(3)]
+                if i == 0:
+                    ahead = [cells_ref[1, c, z, rows, :] for c in range(3)]
+                    behind = [prior_ref[c, z, rows, :] for c in range(3)]
+                else:
+                    ahead = [next_ref[c, z, rows, :] for c in range(3)]
+                    behind = [cells_ref[0, c, z, rows, :] for c in range(3)]
+                normal = [
+                    here[1] * ahead[2] - here[2] * ahead[1],
+                    here[2] * ahead[0] - here[0] * ahead[2],
+                    here[0] * ahead[1] - here[1] * ahead[0],
+                ]
+                angle = arc_angle(jnp.sqrt(dot3(normal, normal)), dot3(here, ahead))
+                ahead = [ahead[c] - here[c] for c in range(3)]
+                behind = [here[c] - behind[c] for c in range(3)]
+                ahead_on, behind_on = dot3(ahead, here), dot3(behind, here)
+                ahead = [ahead[c] - ahead_on * here[c] for c in range(3)]
+                behind = [behind[c] - behind_on * here[c] for c in range(3)]
+                for c in range(3):
+                    place = tangent_rows(z, start)
+                    spec_ref[0, 3 * i + c, place, 0:columns_full] = ahead[c]
+                    spec_ref[0, 3 * i + c, place, columns_full : 2 * columns_full] = behind[c]
+                values = (
+                    angle * angle,
+                    dot3(ahead, ahead),
+                    dot3(ahead, behind),
+                    dot3(behind, behind),
+                )
+                return tuple(total + value for total, value in zip(carry, values))
+
+            totals = cell_loop(step, zeros(4))
+            for k in range(4):
+                sums_ref[i, k + 1] = totals[k]
+
+    def field_sums(i, arrived):
+        turn = (2 * i - 1).astype(jnp.float32)
+
+        def step(z, start, carry):
+            rows = pl.ds(start, row_step)
+            place = tangent_rows(z, start)
+            sign = scale * jnp.where(lax.rem(z, 2) == 1, turn, 1.0)
+            here = [cells_ref[i, c, z, rows, :] for c in range(3)]
+            ahead = [spec_ref[0, 3 * i + c, place, 0:columns_full] for c in range(3)]
+            behind = [
+                spec_ref[0, 3 * i + c, place, columns_full : 2 * columns_full] for c in range(3)
+            ]
+            field = []
+            for c in range(3):
+                value = field_ref[i, c, z, rows, :] + sign * extra_ref[1 - i, c, rows, :]
+                if arrived:
+                    value = value + arrive_ref[c, z, rows, :]
+                field_ref[i, c, z, rows, :] = value
+                field.append(value)
+            values = (dot3(here, field), dot3(field, ahead), dot3(field, behind))
+            return tuple(total + value for total, value in zip(carry, values))
+
+        totals = cell_loop(step, zeros(3))
+        for k, slot in enumerate((0, 5, 6)):
+            sums_ref[i, slot] = totals[k]
+
     barrier = pltpu.get_barrier_semaphore()
-    for d in range(1, groups):
+    for n, shift, d in routes:
         pl.semaphore_signal(
-            barrier,
-            inc=1,
-            device_id={"space": lax.rem(me + d, groups)},
-            device_id_type=pl.DeviceIdType.MESH,
+            barrier, inc=1, device_id=target_of(shift, d), device_id_type=pl.DeviceIdType.MESH
         )
     for c in range(3):
         own_copy(c).start()
-    pl.semaphore_wait(barrier, groups - 1)
+    pl.semaphore_wait(barrier, len(routes))
     film_copy(0).start()
+
+    @pl.when(jnp.logical_not(last))
+    def _():
+        ahead_copy().start()
+
+    @pl.when(jnp.logical_not(first))
+    def _():
+        behind_copy().start()
+
     for c in range(3):
         own_copy(c).wait()
+    fill_rims()
     for side in range(2):
 
         def sum_layers(rows):
@@ -505,6 +747,7 @@
 
     for c in range(3):
         transform_layers(c, 0)
+    local_fields()
 
     for c in range(3):
         film_copy(c).wait_recv()
@@ -573,28 +816,103 @@
             back_arrival(c, 0, slot).wait_recv()
         transform_planes(c, 0)
 
+    neighbour_sums()
     for c in range(3):
-        last_arrival(c).wait_recv()
         for side in range(2):
 
             @pl.when(me != side * parts)
             def _():
                 extra_arrival(side, c).wait_recv()
 
-        for image in range(2):
-
-            def add_extra(rows):
-                extra = scale * extra_ref[1 - image, c, rows, :]
-                for z in range(layer_count):
-                    sign = (-1.0) ** (z * (1 - image))
-                    value = field_ref[image, c, z, rows, :]
-                    field_ref[image, c, z, rows, :] = value + extra if sign > 0 else value - extra
-
-            row_loop(add_extra)
-        pltpu.make_async_copy(field_ref.at[:, c], out_ref.at[:, c], own_sem.at[c]).start()
-
+    field_sums(half, False)
     for c in range(3):
-        pltpu.make_async_copy(field_ref.at[:, c], out_ref.at[:, c], own_sem.at[c]).wait()
+        last_copy(c).wait_recv()
+    field_sums(1 - half, True)
+
+    rows = [
+        jnp.sum(sums_ref[i, k], axis=0, keepdims=True) for i in range(2) for k in range(7)
+    ] + [jnp.zeros((1, lane), jnp.float32)] * 2
+    tile = jnp.sum(jnp.concatenate(rows, axis=0), axis=1, keepdims=True)
+    tile_ref[...] = jnp.broadcast_to(tile, tile_ref.shape)
+    for n, shift, d in routes:
+        swap_copy(n, shift, d, me).start()
+    swap_ref[1, me] = tile_ref[...]
+    for n, shift, d in routes:
+        swap_copy(n, shift, d, lax.rem(me + groups - d, groups)).wait_recv()
+    totals = []
+    for n in range(3):
+        total = swap_ref[n, 0]
+        for g in range(1, groups):
+            total = total + swap_ref[n, g]
+        totals.append(total)
+
+    def entry(n, i, k):
+        return totals[n][7 * i + k : 7 * i + k + 1]
+
+    cell_count = float(layer_count * rows_full * columns_full)
+    energies = [-0.5 * entry(*at, 0) for at in ((0, 1), (1, 0), (1, 1), (2, 0))]
+    distances = [jnp.sqrt(entry(*at, 1) / cell_count) for at in ((0, 1), (1, 0), (1, 1))]
+    pulls = []
+    for i in range(2):
+        weight_next, weight_prior = tangent_weights(energies[i + 1], energies[i + 2], energies[i])
+        length_square = (
+            weight_next * weight_next * entry(1, i, 2)
+            + 2.0 * weight_next * weight_prior * entry(1, i, 3)
+            + weight_prior * weight_prior * entry(1, i, 4)
+        )
+        drive = weight_next * entry(1, i, 5) + weight_prior * entry(1, i, 6)
+        size = jnp.sqrt(jnp.maximum(length_square, 0.0) / cell_count + epsilon)
+        spring = spring_strength * (distances[i + 1] - distances[i])
+        pull = (spring - drive / (cell_count * size)) / size
+        pulls.append((pull * weight_next, pull * weight_prior))
+    for n, shift, d in routes:
+        swap_copy(n, shift, d, me).wait_send()
+    peaks = []
+    for i in range(2):
+        end = first if i == 0 else last
+        ahead_pull, behind_pull = [
+            jnp.concatenate([jnp.broadcast_to(pull, (row_step, 128))] * (lane // 128), axis=1)
+            for pull in pulls[i]
+        ]
+
+        def step(z, start, peak):
+            rows = pl.ds(start, row_step)
+            place = tangent_rows(z, start)
+            here = [cells_ref[i, c, z, rows, :] for c in range(3)]
+            force = []
+            for c in range(3):
+                ahead = spec_ref[0, 3 * i + c, place, 0:columns_full]
+                behind = spec_ref[0, 3 * i + c, place, columns_full : 2 * columns_full]
+                field = field_ref[i, c, z, rows, :]
+                force.append(field + ahead_pull * ahead + behind_pull * behind)
+            along = dot3(force, here)
+            force = [jnp.where(end, 0.0, force[c] - along * here[c]) for c in range(3)]
+            for c in range(3):
+                field_ref[i, c, z, rows, :] = force[c]
+            return (jnp.maximum(peak[0], dot3(force, force)),)
+
+        (peak,) = cell_loop(step, zeros(1))
+        peaks.append(jnp.max(peak, axis=0, keepdims=True))
+        force_copy(i).start()
+    peak = jnp.concatenate(peaks + [jnp.zeros((6, lane), jnp.float32)], axis=0)
+    peak = jnp.broadcast_to(jnp.max(peak, axis=1, keepdims=True), (8, 128))
+    tile_ref[0:8] = peak
+    for d in range(1, groups):
+        peak_copy(d, me).start()
+    peak_ref[me] = peak
+    for d in range(1, groups):
+        peak_copy(d, lax.rem(me + groups - d, groups)).wait_recv()
+    largest = peak_ref[0]
+    for g in range(1, groups):
+        largest = jnp.maximum(largest, peak_ref[g])
+    small_ref[0:8] = jnp.minimum(step_limit, rotation_limit / (jnp.sqrt(largest) + epsilon))
+    small_ref[8:16] = jnp.concatenate(energies[1:3] + [jnp.zeros((6, 128), jnp.float32)], axis=0)
+
+    for i in range(2):
+        force_copy(i).wait()
+    for d in range(1, groups):
+        peak_copy(d, me).wait_send()
+    for c in range(3):
         film_copy(c).wait_send()
         last_copy(c).wait_send()
         for kind in range(2):
@@ -609,13 +927,26 @@
                 extra_copy(c, step).wait_send()
 
     for side in range(2):
+        open_side = me != groups - 1 if side == 0 else me != 0
+
+        @pl.when(open_side)
+        def _():
+            rim_copy(side).wait_send()
 
         @pl.when(me != side * parts)
         def _():
             pair_copy(side, me).wait_send()
 
-
-def demag_field(magnet, kernel):
+    @pl.when(jnp.logical_not(last))
+    def _():
+        ahead_copy().wait_send()
+
+    @pl.when(jnp.logical_not(first))
+    def _():
+        behind_copy().wait_send()
+
+
+def band_step(magnet, anisotropy, kernel):
     layer_count, row_count, column_count = magnet.shape[2:]
     groups = lax.axis_size("space")
     local_planes = 2 * layer_count // groups
@@ -623,12 +954,14 @@
     slots = groups // 2 - 1
     table_y = parity_table(column_count)
     table_x = parity_table(full_rows)
-    tables = [
-        table_limbs(table_y),
-        table_limbs(table_x.T),
-        table_limbs(table_x * parity_weights(full_rows)[None, :]),
-        table_limbs((table_y * parity_weights(column_count)[None, :]).T),
-    ]
+    square = full_rows == column_count
+    tables = [table_limbs(t) for t in (table_y, table_x.T, table_x, table_y.T)][: 2 if square else 4]
+
+    def entry(magnet_ref, kernel_ref, ease_ref, fy_ref, fx_ref, *refs):
+        shared = (fy_ref, fx_ref) if square else ()
+        scale = -4.0 / padded_cells
+        band_kernel(scale, magnet_ref, kernel_ref, ease_ref, fy_ref, fx_ref, *shared, *refs)
+
     slab = (row_count, column_count)
     film = (layer_count,) + slab
     block = (local_planes, 2) + slab
@@ -636,218 +969,81 @@
     inside = pl.BlockSpec(memory_space=pltpu.VMEM)
     dots = 6 * local_planes * 4 * full_rows * column_count * 3 * (full_rows + column_count // 2)
     padded_cells = 8 * layer_count * full_rows * column_count
+    ease = jnp.broadcast_to(anisotropy[:, None], slab)
     signals = pltpu.SemaphoreType.DMA
+    scratch = [
+        (2, 3) + film,
+        (3,) + film,
+        (2, 3) + slab,
+        (groups, 3) + slab,
+        (2, 3) + slab,
+        (3, 2, slots) + block,
+        (3, 2, slots) + block,
+        (3, groups) + block,
+        (local_planes, 6, 2 * full_rows, 2 * column_count),
+        (2, 3) + film,
+        (3,) + film,
+        (3,) + film,
+        (3,) + film,
+        (2, 2, 3, layer_count, column_count),
+        (2, 2, 3, layer_count, column_count),
+        slab,
+        (2, 7, 8, column_count),
+        (16, 128),
+        (3, groups, 16, 128),
+        (groups, 8, 128),
+        (local_planes, 6, full_rows + 8, column_count + 128),
+        (2, 2 * full_rows, 2 * column_count),
+    ]
+    semaphores = [
+        (3,),
+        (local_planes,),
+        (3,),
+        (3,),
+        (2,),
+        (groups,),
+        (3, 2, slots),
+        (3, 2, slots),
+        (3, 2, slots),
+        (3, 2, slots),
+        (3, groups),
+        (2, 3),
+        (3,),
+        (3,),
+        (2,),
+        (2,),
+        (2,),
+        (2,),
+        (3, groups),
+        (3, groups),
+        (groups,),
+        (groups,),
+        (2,),
+    ]
     return pl.pallas_call(
-        functools.partial(demag_kernel, -1.0 / padded_cells),
-        in_specs=[anywhere, anywhere] + [inside] * len(tables),
-        out_specs=anywhere,
-        out_shape=jax.ShapeDtypeStruct(magnet.shape, jnp.float32),
-        scratch_shapes=[
-            pltpu.VMEM((2, 3) + film, jnp.float32),
-            pltpu.VMEM((3,) + film, jnp.float32),
-            pltpu.VMEM((2, 3) + slab, jnp.float32),
-            pltpu.VMEM((groups, 3) + slab, jnp.float32),
-            pltpu.VMEM((2, 3) + slab, jnp.float32),
-            pltpu.VMEM((3, 2, slots) + block, jnp.float32),
-            pltpu.VMEM((3, 2, slots) + block, jnp.float32),
-            pltpu.VMEM((3, groups) + block, jnp.float32),
-            pltpu.VMEM((local_planes, 6, 2 * full_rows, 2 * column_count), jnp.float32),
-            pltpu.VMEM((2, 3) + film, jnp.float32),
-            pltpu.VMEM((local_planes, 6, full_rows + 8, column_count + 128), jnp.float32),
-            pltpu.VMEM((2, 2 * full_rows, 2 * column_count), jnp.float32),
-            signals((3,)),
-            signals((local_planes,)),
-            signals((3,)),
-            signals((3,)),
-            signals((2,)),
-            signals((groups,)),
-            signals((3, 2, slots)),
-            signals((3, 2, slots)),
-            signals((3, 2, slots)),
-            signals((3, 2, slots)),
-            signals((3, groups)),
-            signals((2, 3)),
-            signals((3,)),
-            signals((3,)),
+        entry,
+        in_specs=[anywhere, anywhere] + [inside] * (1 + len(tables)),
+        out_specs=[anywhere, inside],
+        out_shape=[
+            jax.ShapeDtypeStruct(magnet.shape, jnp.float32),
+            jax.ShapeDtypeStruct((16, 128), jnp.float32),
         ],
+        scratch_shapes=[pltpu.VMEM(dims, jnp.float32) for dims in scratch]
+        + [signals(dims) for dims in semaphores],
         compiler_params=pltpu.CompilerParams(
             vmem_limit_bytes=67043328, collective_id=0, has_side_effects=True
         ),
         cost_estimate=pl.CostEstimate(
             flops=4 * dots, bytes_accessed=4 * magnet.size * 4, transcendentals=0
         ),
-        name="demag_kernel",
-    )(magnet, kernel, *[jnp.asarray(t) for t in tables])
-
-
-def swap_kernel(shifts, combine, tile_ref, out_ref, held_ref, send_sem, recv_sem):
-    groups, images = lax.axis_size("space"), lax.axis_size("image")
-    me, image = lax.axis_index("space"), lax.axis_index("image")
-    routes = [
-        (n, shift, d)
-        for n, shift in enumerate(shifts)
-        for d in range(groups)
-        if shift != 0 or d != 0
-    ]
-
-    def target(shift, d):
-        return {"image": lax.rem(image - shift + images, images), "space": lax.rem(me + d, groups)}
-
-    barrier = pltpu.get_barrier_semaphore()
-    for n, shift, d in routes:
-        pl.semaphore_signal(
-            barrier, inc=1, device_id=target(shift, d), device_id_type=pl.DeviceIdType.MESH
-        )
-    pl.semaphore_wait(barrier, len(routes))
-
-    def copy_of(n, shift, d, slot):
-        return pltpu.make_async_remote_copy(
-            src_ref=tile_ref,
-            dst_ref=held_ref.at[n, slot],
-            send_sem=send_sem.at[n, d],
-            recv_sem=recv_sem.at[n, d],
-            device_id=target(shift, d),
-            device_id_type=pl.DeviceIdType.MESH,
-        )
-
-    for n, shift, d in routes:
-        copy_of(n, shift, d, me).start()
-    held_ref[shifts.index(0), me] = tile_ref[...]
-    for n, shift, d in routes:
-        copy_of(n, shift, d, lax.rem(me + groups - d, groups)).wait_recv()
-    for n in range(len(shifts)):
-        total = held_ref[n, 0]
-        for g in range(1, groups):
-            total = combine(total, held_ref[n, g])
-        out_ref[n] = total
-    for n, shift, d in routes:
-        copy_of(n, shift, d, me).wait_send()
-
-
-def swapped(values, shifts, combine, collective_id):
-    rows, columns = values.shape
-    tile = jnp.pad(values, ((0, -rows % 8), (0, -columns % 128)))
-    groups = lax.axis_size("space")
-    inside = pl.BlockSpec(memory_space=pltpu.VMEM)
-    result = pl.pallas_call(
-        functools.partial(swap_kernel, shifts, combine),
-        in_specs=[inside],
-        out_specs=inside,
-        out_shape=jax.ShapeDtypeStruct((len(shifts),) + tile.shape, jnp.float32),
-        scratch_shapes=[
-            pltpu.VMEM((len(shifts), groups) + tile.shape, jnp.float32),
-            pltpu.SemaphoreType.DMA((len(shifts), groups)),
-            pltpu.SemaphoreType.DMA((len(shifts), groups)),
-        ],
-        compiler_params=pltpu.CompilerParams(
-            collective_id=collective_id, has_side_effects=True
-        ),
-        name="swap_kernel",
-    )(tile)
-    return result[:, :rows, :columns]
-
-
-def local_fields(magnet, anisotropy, rimmed):
-    layer_count = magnet.shape[2]
-    row_count = magnet.shape[3]
-    column_count = magnet.shape[4]
-    x_plus = rimmed[:, :, :, 2:]
-    x_minus = rimmed[:, :, :, :-2]
-    padded = jnp.pad(magnet, ((0, 0), (0, 0), (1, 1), (0, 0), (1, 1)))
-    z_plus = padded[:, :, 2:, :, 1:-1]
-    z_minus = padded[:, :, :-2, :, 1:-1]
-    y_plus = padded[:, :, 1:-1, :, 2:]
-    y_minus = padded[:, :, 1:-1, :, :-2]
-    first_row = lax.axis_index("space") * row_count
-    full_rows = row_count * lax.axis_size("space")
-    layer_pos = lax.broadcasted_iota(jnp.int32, (layer_count, row_count, column_count), 0)
-    row_pos = lax.broadcasted_iota(jnp.int32, (layer_count, row_count, column_count), 1) + first_row
-    column_pos = lax.broadcasted_iota(jnp.int32, (layer_count, row_count, column_count), 2)
-    boundary = (layer_pos == 0).astype(jnp.float32) + (layer_pos == layer_count - 1).astype(
-        jnp.float32
-    )
-    boundary = (
-        boundary
-        + (row_pos == 0).astype(jnp.float32)
-        + (row_pos == full_rows - 1).astype(jnp.float32)
-    )
-    boundary = (
-        boundary
-        + (column_pos == 0).astype(jnp.float32)
-        + (column_pos == column_count - 1).astype(jnp.float32)
-    )
-    present = 6.0 - boundary
-    neighbours = x_plus + x_minus + y_plus + y_minus + z_plus + z_minus
-    exchange_part = exchange_strength * (neighbours - present * magnet)
-    chiral_x = chiral_strength * (x_plus[:, 2] - x_minus[:, 2])
-    chiral_y = chiral_strength * (y_plus[:, 2] - y_minus[:, 2])
-    chiral_z = -chiral_strength * (x_plus[:, 0] - x_minus[:, 0] + (y_plus[:, 1] - y_minus[:, 1]))
-    easy_axis = 2.0 * anisotropy[:, None] * magnet[:, 2]
-    local_part = exchange_part + jnp.stack([chiral_x, chiral_y, chiral_z + easy_axis], axis=1)
-    return local_part
+        name="band_kernel",
+    )(magnet, kernel, ease, *[jnp.asarray(t) for t in tables])
 
 
 def body(magnet, anisotropy, kernel):
-    image_count = magnet.shape[0]
     cell_count = magnet.shape[2] * magnet.shape[3] * lax.axis_size("space") * magnet.shape[4]
-    framed = extended(magnet, (("image", 0),), 1)
-    rimmed = extended(magnet, (("space", 3),), 1)
-
-    prior_image = framed[:-2]
-    next_image = framed[2:]
-    demag = demag_field(magnet, kernel)
-    ahead = project(next_image - magnet, magnet)
-    behind = project(magnet - prior_image, magnet)
-    early = (
-        local_fields(magnet, anisotropy, rimmed),
-        total_cells(angle_squared(magnet, next_image)),
-        total_cells(ahead * ahead),
-        total_cells(ahead * behind),
-        total_cells(behind * behind),
-    )
-    fields = early[0] + demag
-    true_force = project(fields, magnet)
-    tangent_next = project(next_image - magnet, magnet)
-    tangent_prior = project(magnet - prior_image, magnet)
-    sums = jnp.stack(
-        [
-            -0.5 * total_cells(magnet * fields),
-            *early[1:],
-            total_cells(true_force * tangent_next),
-            total_cells(true_force * tangent_prior),
-        ],
-        axis=1,
-    )
-    band_size = image_count * lax.axis_size("image")
-    swaps = swapped(sums, (-1, 0, 1), jnp.add, 64)
-    band = jnp.concatenate([swaps[0, -1:], swaps[1], swaps[2, :1]], axis=0)
-    energy_band, distance_band = band[:, 0], jnp.sqrt(band[:, 1] / cell_count)
-    weight_next, weight_prior = tangent_weights(
-        energy_band, jnp.roll(energy_band, -1), jnp.roll(energy_band, 1)
-    )
-    length_squares = (
-        weight_next * weight_next * band[:, 2]
-        + 2.0 * weight_next * weight_prior * band[:, 3]
-        + weight_prior * weight_prior * band[:, 4]
-    )
-    drive_total = weight_next * band[:, 5] + weight_prior * band[:, 6]
-    tangent_scale = jnp.sqrt(jnp.maximum(length_squares, 0.0) / cell_count + epsilon)
-    parallel = drive_total / (cell_count * tangent_scale)
-    spring = spring_strength * (distance_band - jnp.roll(distance_band, 1))
-    first_image = lax.axis_index("image") * image_count
-    image_index = first_image - 1 + jnp.arange(image_count + 2)
-    interior = ((image_index > 0) & (image_index < band_size - 1)).astype(jnp.float32)
-    pull = (spring - parallel) / tangent_scale
-    mine = jnp.stack([energy_band, pull * weight_next, pull * weight_prior, interior], axis=1)[1:-1]
-    energy_total = mine[:, 0]
-    band_force = jnp.where(
-        lift_axes(mine[:, 3]) > 0.0,
-        true_force + lift_axes(mine[:, 1]) * tangent_next + lift_axes(mine[:, 2]) * tangent_prior,
-        0.0,
-    )
-    local_largest = jnp.max(jnp.sqrt(jnp.sum(band_force * band_force, axis=1)), axis=(1, 2, 3))
-    largest = swapped(local_largest[None, :], (0,), jnp.maximum, 65)[0, 0]
-    move_scale = jnp.minimum(step_limit, rotation_limit / (largest + epsilon))
+    band_force, small = band_step(magnet, anisotropy, kernel)
+    move_scale, energy_total = small[0:2, 0], small[8:10, 0]
     stepped = magnet + lift_axes(move_scale) * band_force
     updated = stepped / jnp.sqrt(jnp.sum(stepped * stepped, axis=1, keepdims=True))
     return (updated, band_force, energy_total / cell_count)

time: 198 us -> 135 us (0.68)
  other arithmetic: 45.9 us -> 7.68 us
  local copies, waits for them, and re-layouts: 19.9 us -> 3.79 us
  starting transfers between devices: 12.9 us -> 0 us
  Pallas kernels: 118 us -> 123 us
    reduce_sum x5 -> x0, other arithmetic: 28.1 us -> none  [the longest x1 10.9 us: angle_squared(): cosine = jnp.sum(first * second, axis=1)]
    ppermute x4 -> x0, starting transfers between devices: 12.9 us -> none  [the longest x2 10.3 us: extended(): lax.ppermute(tail, axis, [(i, (i + 1) % count) for i in range(ends)])]
    slice x5 -> x0, local copies, waits for them, and re-layouts: 6.44 us -> none  [the longest x1 3.89 us: extended(): lax.slice_in_dim(cells, cells.shape[dim] - width, cells.shape[dim], axis=...]
    unnamed x12 -> x5, local copies, waits for them, and re-layouts: 7.96 us -> 2.19 us
    mul x5 -> x0, other arithmetic: 5.76 us -> none  [the longest x1 4.45 us: local_fields(): chiral_x = chiral_strength * (x_plus[:, 2] - x_minus[:, 2])]
    sub x3 -> x0, other arithmetic: 4.75 us -> none  [the longest x2 3.81 us: angle_squared(): normal_part = jnp.cross(first, second, axis=1)]
    pallas_call x3 -> x1, Pallas kernels: 118 us -> 123 us  [band_step(): pl.pallas_call(entry, in_specs=[anywhere, anywhere] + [inside] * (1 + len...]
  transfers between devices with their start and end apart: 4 -> 0, of which waited for: 0 -> 0; matrix products, arithmetic and copies ran while one was open for 9% -> 0% of each run, Pallas kernels for 53% -> 0%
where the time goes in v2:
time: 135 us
  Pallas kernels  123 us (91%)
  other arithmetic  7.68 us (6%)
  local copies, waits for them, and re-layouts  3.79 us (3%)
    pallas_call x1, Pallas kernels, band_step(): pl.pallas_call(entry, in_specs=[anywhere, anywhere] + [inside] * (1 + len...  123 us
    reduce_sum x1, other arithmetic, body(): jnp.sum(stepped * stepped, axis=1, keepdims=True)  3.91 us

profile of v2, /device:TPU:0, one launch (start us, length us, event | category | flops | bytes accessed | tf_op | source)
XLA Modules:
  0.0 134.7 jit_solution(160200414110951959)
XLA Ops:
  0.6 1.4 %broadcast_in_dim.2.ease_ref = f32[64,256]{1,0:T(8,128)} broadcast(f32[64]{0:T(128)} %param.6), dimensions={0} | broadcast | bytes 65792 | tf_op jit(solution)/shard_map/broadcast_in_dim | solution.py:972
  2.0 122.6 %band_kernel.1 = (f32[2,3,8,64,256]{4,3,2,1,0:T(8,128)}, f32[16,128]{1,0:T(8,128)}) custom-call(f32[2,3,8,64,256]{4,3,2,1,0:T(8,128)} %magnet_ref.1, f32[6,4,512,512]{3,2,1,0:T(8,128)} %kernel_ref.1, f32[64,256]{1,0:T(8,128)} %broadcast_in_dim.2.ease_ref, bf16[2,256,512]{2,1,0:T(8,128)(2,1)} %constant.9.clone.fy_ref, bf16[2,512,256]{2,1,0:T(8,128)(2,1)} %constant.10.clone.fx_ref), custom_call_target="tpu_custom_call" | custom-call | flops 28991029248 | bytes 12582912 | tf_op jit(solution)/shard_map/band_kernel/pallas_call | solution.py:1023
  124.6 1.3 multiply_reduce_fusion.1
  125.9 0.0 copy-start
  125.9 0.0 copy-start.1
  125.9 3.9 %multiply_reduce_fusion = f32[2,8,64,256]{3,2,1,0:T(8,128)S(1)} fusion(f32[2,3,8,64,256]{4,3,2,1,0:T(8,128)} %magnet_ref.1, f32[2,3,8,64,256]{4,3,2,1,0:T(8,128)} %get-tuple-element.13, f32[2]{0:T(128)S(1)} %get-tuple-element.8), kind=kLoop, calls=%fused_computation | loop fusion | flops 2883584 | bytes 7340040 | tf_op jit(solution)/shard_map/reduce_sum | solution.py:1048
  129.8 0.2 sqrt.8
  130.1 0.0 copy-done
  130.1 0.5 copy-done.1
  130.6 2.5 %broadcast_divide_fusion = f32[2,3,8,64,256]{4,3,2,1,0:T(8,128)} fusion(f32[2,8,64,256]{3,2,1,0:T(8,128)S(1)} %sqrt.8, f32[2,3,8,64,256]{4,3,2,1,0:T(8,128)S(1)} %copy-done.1, f32[2,3,8,64,256]{4,3,2,1,0:T(8,128)S(1)} %copy-done, f32[2]{0:T(128)S(1)} %get-tuple-element.8), kind=kLoop, calls=%fused_computation.2 | loop fusion | flops 2359296 | bytes 10485768 | tf_op jit(solution)/shard_map/div | solution.py:1048
  133.1 1.7 %copy.9 = f32[2,3,8,64,256]{4,3,2,1,0:T(8,128)} copy(f32[2,3,8,64,256]{4,3,2,1,0:T(8,128)S(1)} %copy-done) | data formatting | bytes 6291456
Async XLA Ops:
  125.9 4.2 %copy-start = (f32[2,3,8,64,256]{4,3,2,1,0:T(8,128)S(1)}, f32[2,3,8,64,256]{4,3,2,1,0:T(8,128)}, u32[]{:S(2)}) copy-start(f32[2,3,8,64,256]{4,3,2,1,0:T(8,128)} %get-tuple-element.13) | copy-start | bytes 9437188
  125.9 4.7 %copy-start.1 = (f32[2,3,8,64,256]{4,3,2,1,0:T(8,128)S(1)}, f32[2,3,8,64,256]{4,3,2,1,0:T(8,128)}, u32[]{:S(2)}) copy-start(f32[2,3,8,64,256]{4,3,2,1,0:T(8,128)} %magnet_ref.1) | copy-start | bytes 9437188

commit v3 on v2

--- a/solution.py
+++ b/solution.py
@@ -15,10 +15,6 @@
 step_limit = 1.0
 rotation_limit = 0.5
 epsilon = 1e-06
-
-
-def lift_axes(values):
-    return values[:, None, None, None, None]
 
 
 def tangent_weights(energy_total, energy_next, energy_prior):
@@ -139,79 +135,95 @@
 
 
 def tensor_part(c, spec_ref, kernel_ref, out_ref):
-    rows_full, columns_full = out_ref.shape[1] // 2, out_ref.shape[2] // 2
+    rows_full, columns_full = out_ref.shape[2] // 2, out_ref.shape[3] // 2
     lane = 128
-    sub = 8
-    row_pos = lax.broadcasted_iota(jnp.int32, (sub, lane), 0)
-    lane_pos = lax.broadcasted_iota(jnp.int32, (sub, lane), 1)
+    sub = 16
+    top = lax.broadcasted_iota(jnp.int32, (sub, lane), 0) == 0
+    left = lax.broadcasted_iota(jnp.int32, (sub, lane), 1) == 0
+
+    def tile(row_start, first_row, start):
+        rows = pl.ds(row_start, sub)
+        columns = slice(start, start + lane)
+        edge_columns = slice(columns_full, columns_full + lane)
+        first_column = start == 0
+
+        def loaded(component):
+            body = kernel_ref[component, rows, columns]
+            side = kernel_ref[component, rows, edge_columns] if first_column else None
+            if not first_row:
+                return body, side, None, None
+            far = pl.ds(rows_full, 1)
+            body_far = kernel_ref[component, far, columns]
+            side_far = kernel_ref[component, far, edge_columns] if first_column else None
+            return body, side, body_far, side_far
+
+        def pick(parts, odd_x, odd_y):
+            body, side, body_far, side_far = parts
+            mixed = jnp.where(left, side, body) if odd_y and first_column else body
+            if odd_x and first_row:
+                far = body_far
+                if odd_y and first_column:
+                    far = jnp.where(left[:1], side_far, far)
+                mixed = jnp.where(top, far, mixed)
+            return mixed
+
+        own = loaded(c)
+        k_xy = pick(loaded(3), 0, 0) if c < 2 else None
+        k_xz = loaded(4) if c != 1 else None
+        k_yz = loaded(5) if c != 0 else None
+
+        def place(px, py):
+            offset = py * columns_full + start
+            return pl.ds(row_start + px * rows_full, sub), slice(offset, offset + lane)
+
+        def spec(px, py, f):
+            at_rows, at_columns = place(px, py)
+            return spec_ref[f, at_rows, at_columns]
+
+        for px in range(2):
+            for py in range(2):
+                own_here = pick(own, px, py)
+                xz_here = pick(k_xz, 0, py) if c != 1 else None
+                yz_here = pick(k_yz, px, 0) if c != 0 else None
+                for part in range(2):
+                    turn = 1.0 if part else -1.0
+                    sx = turn if px else -turn
+                    sy = turn if py else -turn
+                    other = 1 - part
+                    total = own_here * spec(px, py, 2 * c + part)
+                    if c < 2:
+                        across = k_xy * spec(1 - px, 1 - py, 2 * (1 - c) + part)
+                        total = total - across if px == py else total + across
+                    if c == 0:
+                        third = xz_here * spec(1 - px, py, 4 + other)
+                        total = total + third if sx > 0 else total - third
+                    elif c == 1:
+                        third = yz_here * spec(px, 1 - py, 4 + other)
+                        total = total + third if sy > 0 else total - third
+                    else:
+                        third = xz_here * spec(1 - px, py, other)
+                        total = total + third if sx > 0 else total - third
+                        third = yz_here * spec(px, 1 - py, 2 + other)
+                        total = total + third if sy > 0 else total - third
+                    if first_row:
+                        total = jnp.where(top, 0.5 * total, total)
+                    if first_column:
+                        total = jnp.where(left, 0.5 * total, total)
+                    upper, lower = split_limbs(total)
+                    at_rows, at_columns = place(px, py)
+                    out_ref[part, 0, at_rows, at_columns] = upper
+                    out_ref[part, 1, at_rows, at_columns] = lower
+
+    for start in range(0, columns_full, lane):
+        tile(0, True, start)
 
     def step(i, carry):
         row_start = pl.multiple_of(i * sub, sub)
-        top = (row_pos + row_start) == 0
         for start in range(0, columns_full, lane):
-
-            def pick(component, odd_x, odd_y):
-                def at(rows):
-                    inner = kernel_ref[component, rows, start : start + lane]
-                    if odd_y and start == 0:
-                        edge = kernel_ref[component, rows, columns_full : columns_full + lane]
-                        inner = jnp.where(lane_pos == 0, edge, inner)
-                    return inner
-
-                values = at(pl.ds(row_start, sub))
-                if odd_x:
-                    values = jnp.where(top, at(pl.ds(rows_full, sub)), values)
-                return values
-
-            def place(px, py):
-                return (
-                    pl.ds(row_start + px * rows_full, sub),
-                    slice(py * columns_full + start, py * columns_full + start + lane),
-                )
-
-            def spec(px, py, f):
-                rows, columns = place(px, py)
-                return spec_ref[f, rows, columns]
-
-            for px in range(2):
-                for py in range(2):
-                    sx = 1.0 if px else -1.0
-                    sy = 1.0 if py else -1.0
-                    own = pick(c, px, py)
-                    if c < 2:
-                        both = -(sx * sy) * pick(3, 0, 0)
-                    if c != 1:
-                        k_xz = sx * pick(4, 0, py)
-                    if c != 0:
-                        k_yz = sy * pick(5, px, 0)
-                    for part in range(2):
-                        turn = 1.0 if part else -1.0
-                        other = 1 - part
-                        total = own * spec(px, py, 2 * c + part)
-                        if c == 0:
-                            total = (
-                                total
-                                + both * spec(1 - px, 1 - py, 2 + part)
-                                + turn * (k_xz * spec(1 - px, py, 4 + other))
-                            )
-                        elif c == 1:
-                            total = (
-                                both * spec(1 - px, 1 - py, part)
-                                + total
-                                + turn * (k_yz * spec(px, 1 - py, 4 + other))
-                            )
-                        else:
-                            total = total + turn * (
-                                k_xz * spec(1 - px, py, other) + k_yz * spec(px, 1 - py, 2 + other)
-                            )
-                        total = jnp.where(top, 0.5 * total, total)
-                        if start == 0:
-                            total = jnp.where(lane_pos == 0, 0.5 * total, total)
-                        rows, columns = place(px, py)
-                        out_ref[part, rows, columns] = total
+            tile(row_start, False, start)
         return carry
 
-    lax.fori_loop(0, rows_full // sub, step, 0)
+    lax.fori_loop(1, rows_full // sub, step, 0)
 
 
 def arc_angle(sine, cosine):
@@ -236,13 +248,12 @@
     scale,
     magnet_ref,
     kernel_ref,
-    ease_ref,
-    fy_ref,
-    fx_ref,
-    gx_ref,
-    gy_ref,
+    anisotropy_ref,
+    source_tables,
+    updated_ref,
     force_ref,
     small_ref,
+    tables,
     cells_ref,
     film_ref,
     stage_ref,
@@ -259,6 +270,7 @@
     rim_out_ref,
     rim_ref,
     present_ref,
+    ease_ref,
     sums_ref,
     tile_ref,
     swap_ref,
@@ -288,7 +300,11 @@
     peak_send,
     peak_recv,
     force_sem,
+    update_sem,
+    table_sem,
 ):
+    fy_ref, fx_ref = tables[:2]
+    gx_ref, gy_ref = tables[:2] if len(tables) == 2 else tables[2:]
     groups, local_planes = held_ref.shape[1], held_ref.shape[2]
     slab, columns_full = held_ref.shape[4], held_ref.shape[5]
     layer_count = cells_ref.shape[2]
@@ -309,6 +325,18 @@
         if shift != 0 or d != 0
     ]
 
+    def gate(exists, action):
+        if exists is None:
+            action()
+        else:
+            pl.when(exists)(action)
+
+    def receiver(shift):
+        return None if shift == 0 else jnp.logical_not(last if shift < 0 else first)
+
+    def sender(shift):
+        return None if shift == 0 else jnp.logical_not(first if shift < 0 else last)
+
     def target_of(shift, d):
         return {"image": lax.rem(image - shift + images, images), "space": lax.rem(me + d, groups)}
 
@@ -376,23 +404,23 @@
             half * parts + source,
         )
 
-    def back_copy(c, kind, slot):
+    def back_copy(c, q, kind, slot):
         target = lax.rem(seat + 1 + slot, parts)
         return remote(
-            held_ref.at[c, place_of(target, kind)],
-            back_ref.at[c, kind, parts - 2 - slot],
-            back_send.at[c, kind, slot],
-            back_recv.at[c, kind, parts - 2 - slot],
+            held_ref.at[c, place_of(target, kind), q],
+            back_ref.at[c, kind, parts - 2 - slot, q],
+            back_send.at[c, q, kind, slot],
+            back_recv.at[c, q, kind, parts - 2 - slot],
             half * parts + target,
         )
 
-    def back_arrival(c, kind, slot):
+    def back_arrival(c, q, kind, slot):
         source = lax.rem(seat + 1 + slot, parts)
         return remote(
-            held_ref.at[c, place_of(source, kind)],
-            back_ref.at[c, kind, slot],
-            back_send.at[c, kind, slot],
-            back_recv.at[c, kind, slot],
+            held_ref.at[c, place_of(source, kind), q],
+            back_ref.at[c, kind, slot, q],
+            back_send.at[c, q, kind, slot],
+            back_recv.at[c, q, kind, slot],
             half * parts + source,
         )
 
@@ -460,6 +488,12 @@
             peak_recv.at[d],
             lax.rem(me + d, groups),
         )
+
+    def table_copy(n):
+        return pltpu.make_async_copy(source_tables[n], tables[n], table_sem.at[n])
+
+    def update_copy(i):
+        return pltpu.make_async_copy(cells_ref.at[i], updated_ref.at[i], update_sem.at[i])
 
     def force_copy(i):
         return pltpu.make_async_copy(field_ref.at[i], force_ref.at[i], force_sem.at[i])
@@ -549,7 +583,7 @@
             def _():
                 rim_ref[side] = jnp.zeros(rim_ref.shape[1:], jnp.float32)
 
-    def local_fields():
+    def wait_rims():
         for side in range(2):
             has_source = me != 0 if side == 0 else me != groups - 1
 
@@ -557,11 +591,11 @@
             def _():
                 rim_copy(side).wait_recv()
 
+    def local_fields(i):
         row_pos = lax.broadcasted_iota(jnp.int32, (slab, columns_full), 0)
         column_pos = lax.broadcasted_iota(jnp.int32, (slab, columns_full), 1)
 
-        def step(index, carry):
-            i, z = index // layer_count, lax.rem(index, layer_count)
+        def step(z, carry):
             below, above = jnp.maximum(z - 1, 0), jnp.minimum(z + 1, layer_count - 1)
             has_below = (z > 0).astype(jnp.float32)
             has_above = (z < layer_count - 1).astype(jnp.float32)
@@ -591,23 +625,25 @@
                     tilt.append(y_plus - y_minus)
                     field_ref[i, 1, z] = part
                 else:
-                    ease = 2.0 * ease_ref[...] * cells
+                    ease = ease_ref[...] * cells
                     field_ref[i, 2, z] = part + (ease - chiral_strength * (tilt[0] + tilt[1]))
                     field_ref[i, 0, z] = field_ref[i, 0, z] + chiral_strength * (x_plus - x_minus)
                     field_ref[i, 1, z] = field_ref[i, 1, z] + chiral_strength * (y_plus - y_minus)
             return carry
 
-        lax.fori_loop(0, 2 * layer_count, step, 0)
+        lax.fori_loop(0, layer_count, step, 0)
 
     lane = columns_full
 
     def cell_loop(step, carry):
-        steps = slab // row_step
+        steps = slab // (2 * row_step)
 
         def chunk(index, carry):
             z = index // steps
-            start = pl.multiple_of(lax.rem(index, steps) * row_step, row_step)
-            return step(z, start, carry)
+            start = pl.multiple_of(lax.rem(index, steps) * 2 * row_step, 2 * row_step)
+            for offset in (0, row_step):
+                carry = step(z, pl.multiple_of(start + offset, row_step), carry)
+            return carry
 
         return lax.fori_loop(0, layer_count * steps, chunk, carry)
 
@@ -674,40 +710,50 @@
             for k in range(4):
                 sums_ref[i, k + 1] = totals[k]
 
-    def field_sums(i, arrived):
+    def field_sums(i, c, arrived):
         turn = (2 * i - 1).astype(jnp.float32)
 
         def step(z, start, carry):
             rows = pl.ds(start, row_step)
             place = tangent_rows(z, start)
             sign = scale * jnp.where(lax.rem(z, 2) == 1, turn, 1.0)
-            here = [cells_ref[i, c, z, rows, :] for c in range(3)]
-            ahead = [spec_ref[0, 3 * i + c, place, 0:columns_full] for c in range(3)]
-            behind = [
-                spec_ref[0, 3 * i + c, place, columns_full : 2 * columns_full] for c in range(3)
-            ]
-            field = []
-            for c in range(3):
-                value = field_ref[i, c, z, rows, :] + sign * extra_ref[1 - i, c, rows, :]
-                if arrived:
-                    value = value + arrive_ref[c, z, rows, :]
-                field_ref[i, c, z, rows, :] = value
-                field.append(value)
-            values = (dot3(here, field), dot3(field, ahead), dot3(field, behind))
+            field = field_ref[i, c, z, rows, :] + sign * extra_ref[1 - i, c, rows, :]
+            if arrived:
+                field = field + arrive_ref[c, z, rows, :]
+            field_ref[i, c, z, rows, :] = field
+            values = (
+                cells_ref[i, c, z, rows, :] * field,
+                field * spec_ref[0, 3 * i + c, place, 0:columns_full],
+                field * spec_ref[0, 3 * i + c, place, columns_full : 2 * columns_full],
+            )
             return tuple(total + value for total, value in zip(carry, values))
 
         totals = cell_loop(step, zeros(3))
         for k, slot in enumerate((0, 5, 6)):
-            sums_ref[i, slot] = totals[k]
+            sums_ref[i, slot] = totals[k] if c == 0 else sums_ref[i, slot] + totals[k]
 
     barrier = pltpu.get_barrier_semaphore()
     for n, shift, d in routes:
-        pl.semaphore_signal(
-            barrier, inc=1, device_id=target_of(shift, d), device_id_type=pl.DeviceIdType.MESH
-        )
+        signal = functools.partial(
+            pl.semaphore_signal,
+            barrier,
+            inc=1,
+            device_id=target_of(shift, d),
+            device_id_type=pl.DeviceIdType.MESH,
+        )
+        gate(receiver(shift), signal)
     for c in range(3):
         own_copy(c).start()
-    pl.semaphore_wait(barrier, len(routes))
+    for n in range(len(tables)):
+        table_copy(n).start()
+
+    def spread(r, carry):
+        ease_ref[pl.ds(r, 1), :] = jnp.full((1, columns_full), 2.0 * anisotropy_ref[r])
+        return carry
+
+    lax.fori_loop(0, slab, spread, 0)
+    ends = first.astype(jnp.int32) + last.astype(jnp.int32)
+    pl.semaphore_wait(barrier, len(routes) - groups * ends)
     film_copy(0).start()
 
     @pl.when(jnp.logical_not(last))
@@ -747,8 +793,8 @@
 
     for c in range(3):
         transform_layers(c, 0)
-    local_fields()
-
+    for n in range(len(tables)):
+        table_copy(n).wait()
     for c in range(3):
         film_copy(c).wait_recv()
         transform_layers(c, 1)
@@ -780,6 +826,10 @@
             return carry
 
         lax.fori_loop(0, local_planes, forward, 0)
+        if c == 0:
+            wait_rims()
+        if c < 2:
+            local_fields(c)
 
     for q in range(local_planes):
         tensor_copy(q).wait()
@@ -791,30 +841,31 @@
             gx = jnp.concatenate([gx_ref[0], gx_ref[0], gx_ref[1]], axis=1)
             gy = jnp.concatenate([gy_ref[0], gy_ref[0], gy_ref[1]], axis=0)
             for part in range(2):
-                lines = dot32(gx, three_limbs(result_ref[part], 0))
+                upper, lower = result_ref[part, 0], result_ref[part, 1]
+                lines = dot32(gx, jnp.concatenate([upper, lower, upper], axis=0))
                 cells = dot32(three_limbs(lines, 1), gy)
                 for g in range(groups):
                     held_ref[c, g, q, part] = cells[g * slab : (g + 1) * slab]
+            for kind in (1, 0):
+                for slot in range(parts - 1):
+                    back_copy(c, q, kind, slot).start()
+
+            @pl.when((seat == 0) & (q == 0))
+            def _():
+                extra_ref[half, c] = held_ref[c, me, 0, 1]
+                for step in range(1, groups):
+                    extra_copy(c, step).start()
+
             return carry
 
         lax.fori_loop(0, local_planes, backward, 0)
         for kind in (1, 0):
-            for slot in range(parts - 1):
-                back_copy(c, kind, slot).start()
-
-        @pl.when(seat == 0)
-        def _():
-            extra_ref[half, c] = held_ref[c, me, 0, 1]
-            for step in range(1, groups):
-                extra_copy(c, step).start()
-
-        for slot in range(parts - 1):
-            back_arrival(c, 1, slot).wait_recv()
-        transform_planes(c, 1)
-        last_copy(c).start()
-        for slot in range(parts - 1):
-            back_arrival(c, 0, slot).wait_recv()
-        transform_planes(c, 0)
+            for q in range(local_planes):
+                for slot in range(parts - 1):
+                    back_arrival(c, q, kind, slot).wait_recv()
+            transform_planes(c, kind)
+            if kind == 1:
+                last_copy(c).start()
 
     neighbour_sums()
     for c in range(3):
@@ -824,10 +875,10 @@
             def _():
                 extra_arrival(side, c).wait_recv()
 
-    field_sums(half, False)
+        field_sums(half, c, False)
     for c in range(3):
         last_copy(c).wait_recv()
-    field_sums(1 - half, True)
+        field_sums(1 - half, c, True)
 
     rows = [
         jnp.sum(sums_ref[i, k], axis=0, keepdims=True) for i in range(2) for k in range(7)
@@ -835,10 +886,16 @@
     tile = jnp.sum(jnp.concatenate(rows, axis=0), axis=1, keepdims=True)
     tile_ref[...] = jnp.broadcast_to(tile, tile_ref.shape)
     for n, shift, d in routes:
-        swap_copy(n, shift, d, me).start()
+        gate(receiver(shift), swap_copy(n, shift, d, me).start)
     swap_ref[1, me] = tile_ref[...]
+    for n, end in ((0, first), (2, last)):
+
+        @pl.when(end)
+        def _():
+            swap_ref[n] = jnp.zeros(swap_ref.shape[1:], jnp.float32)
+
     for n, shift, d in routes:
-        swap_copy(n, shift, d, lax.rem(me + groups - d, groups)).wait_recv()
+        gate(sender(shift), swap_copy(n, shift, d, lax.rem(me + groups - d, groups)).wait_recv)
     totals = []
     for n in range(3):
         total = swap_ref[n, 0]
@@ -866,7 +923,7 @@
         pull = (spring - drive / (cell_count * size)) / size
         pulls.append((pull * weight_next, pull * weight_prior))
     for n, shift, d in routes:
-        swap_copy(n, shift, d, me).wait_send()
+        gate(receiver(shift), swap_copy(n, shift, d, me).wait_send)
     peaks = []
     for i in range(2):
         end = first if i == 0 else last
@@ -905,11 +962,28 @@
     largest = peak_ref[0]
     for g in range(1, groups):
         largest = jnp.maximum(largest, peak_ref[g])
-    small_ref[0:8] = jnp.minimum(step_limit, rotation_limit / (jnp.sqrt(largest) + epsilon))
-    small_ref[8:16] = jnp.concatenate(energies[1:3] + [jnp.zeros((6, 128), jnp.float32)], axis=0)
-
+    moves = jnp.minimum(step_limit, rotation_limit / (jnp.sqrt(largest) + epsilon))
+    for i in range(2):
+        move = jnp.broadcast_to(moves[i : i + 1], (row_step, 128))
+        move = jnp.concatenate([move] * (lane // 128), axis=1)
+
+        def step(z, start, carry):
+            rows = pl.ds(start, row_step)
+            moved = [
+                cells_ref[i, c, z, rows, :] + move * field_ref[i, c, z, rows, :] for c in range(3)
+            ]
+            inverse = 1.0 / jnp.sqrt(dot3(moved, moved))
+            for c in range(3):
+                cells_ref[i, c, z, rows, :] = inverse * moved[c]
+            return carry
+
+        cell_loop(step, 0)
+        update_copy(i).start()
+    energy = jnp.concatenate(energies[1:3] + [jnp.zeros((6, 128), jnp.float32)], axis=0)
+    small_ref[...] = energy / cell_count
     for i in range(2):
         force_copy(i).wait()
+        update_copy(i).wait()
     for d in range(1, groups):
         peak_copy(d, me).wait_send()
     for c in range(3):
@@ -918,7 +992,8 @@
         for kind in range(2):
             for slot in range(parts - 1):
                 plane_copy(c, kind, slot).wait_send()
-                back_copy(c, kind, slot).wait_send()
+                for q in range(local_planes):
+                    back_copy(c, q, kind, slot).wait_send()
 
     @pl.when(seat == 0)
     def _():
@@ -957,10 +1032,14 @@
     square = full_rows == column_count
     tables = [table_limbs(t) for t in (table_y, table_x.T, table_x, table_y.T)][: 2 if square else 4]
 
-    def entry(magnet_ref, kernel_ref, ease_ref, fy_ref, fx_ref, *refs):
-        shared = (fy_ref, fx_ref) if square else ()
+    def entry(magnet_ref, kernel_ref, anisotropy_ref, *refs):
+        count = len(tables)
+        sources, outs = refs[:count], refs[count : count + 3]
+        held, rest = refs[count + 3 : 2 * count + 3], refs[2 * count + 3 :]
         scale = -4.0 / padded_cells
-        band_kernel(scale, magnet_ref, kernel_ref, ease_ref, fy_ref, fx_ref, *shared, *refs)
+        band_kernel(
+            scale, magnet_ref, kernel_ref, anisotropy_ref, sources, *outs, held, *rest
+        )
 
     slab = (row_count, column_count)
     film = (layer_count,) + slab
@@ -969,7 +1048,6 @@
     inside = pl.BlockSpec(memory_space=pltpu.VMEM)
     dots = 6 * local_planes * 4 * full_rows * column_count * 3 * (full_rows + column_count // 2)
     padded_cells = 8 * layer_count * full_rows * column_count
-    ease = jnp.broadcast_to(anisotropy[:, None], slab)
     signals = pltpu.SemaphoreType.DMA
     scratch = [
         (2, 3) + film,
@@ -988,12 +1066,12 @@
         (2, 2, 3, layer_count, column_count),
         (2, 2, 3, layer_count, column_count),
         slab,
+        slab,
         (2, 7, 8, column_count),
         (16, 128),
         (3, groups, 16, 128),
         (groups, 8, 128),
         (local_planes, 6, full_rows + 8, column_count + 128),
-        (2, 2 * full_rows, 2 * column_count),
     ]
     semaphores = [
         (3,),
@@ -1004,8 +1082,8 @@
         (groups,),
         (3, 2, slots),
         (3, 2, slots),
-        (3, 2, slots),
-        (3, 2, slots),
+        (3, local_planes, 2, slots),
+        (3, local_planes, 2, slots),
         (3, groups),
         (2, 3),
         (3,),
@@ -1019,16 +1097,22 @@
         (groups,),
         (groups,),
         (2,),
+        (2,),
+        (len(tables),),
     ]
     return pl.pallas_call(
         entry,
-        in_specs=[anywhere, anywhere] + [inside] * (1 + len(tables)),
-        out_specs=[anywhere, inside],
+        in_specs=[anywhere, anywhere, pl.BlockSpec(memory_space=pltpu.SMEM)]
+        + [anywhere] * len(tables),
+        out_specs=[anywhere, anywhere, inside],
         out_shape=[
             jax.ShapeDtypeStruct(magnet.shape, jnp.float32),
-            jax.ShapeDtypeStruct((16, 128), jnp.float32),
+            jax.ShapeDtypeStruct(magnet.shape, jnp.float32),
+            jax.ShapeDtypeStruct((8, 128), jnp.float32),
         ],
-        scratch_shapes=[pltpu.VMEM(dims, jnp.float32) for dims in scratch]
+        scratch_shapes=[pltpu.VMEM(t.shape, jnp.bfloat16) for t in tables]
+        + [pltpu.VMEM(dims, jnp.float32) for dims in scratch]
+        + [pltpu.VMEM((2, 2, 2 * full_rows, 2 * column_count), jnp.bfloat16)]
         + [signals(dims) for dims in semaphores],
         compiler_params=pltpu.CompilerParams(
             vmem_limit_bytes=67043328, collective_id=0, has_side_effects=True
@@ -1037,16 +1121,12 @@
             flops=4 * dots, bytes_accessed=4 * magnet.size * 4, transcendentals=0
         ),
         name="band_kernel",
-    )(magnet, kernel, ease, *[jnp.asarray(t) for t in tables])
+    )(magnet, kernel, anisotropy, *[jnp.asarray(t) for t in tables])
 
 
 def body(magnet, anisotropy, kernel):
-    cell_count = magnet.shape[2] * magnet.shape[3] * lax.axis_size("space") * magnet.shape[4]
-    band_force, small = band_step(magnet, anisotropy, kernel)
-    move_scale, energy_total = small[0:2, 0], small[8:10, 0]
-    stepped = magnet + lift_axes(move_scale) * band_force
-    updated = stepped / jnp.sqrt(jnp.sum(stepped * stepped, axis=1, keepdims=True))
-    return (updated, band_force, energy_total / cell_count)
+    updated, band_force, small = band_step(magnet, anisotropy, kernel)
+    return (updated, band_force, small[: magnet.shape[0], 0])
 
 
 def solution(mesh):

time: 135 us -> 128 us (0.948)
  other arithmetic: 7.68 us -> 0 us
  local copies, waits for them, and re-layouts: 3.79 us -> 7.03 us
  Pallas kernels: 123 us -> 121 us
    reduce_sum x1 -> x0, other arithmetic: 3.91 us -> none  [body(): jnp.sum(stepped * stepped, axis=1, keepdims=True)]
    div x2 -> x0, other arithmetic: 3.77 us -> none  [the longest x1 2.46 us: body(): stepped / jnp.sqrt(jnp.sum(stepped * stepped, axis=1, keepdims=True))]
    unnamed x5 -> x4, local copies, waits for them, and re-layouts: 2.19 us -> 5.72 us
    pallas_call x1, Pallas kernels: 123 us -> 121 us  [band_step(): pl.pallas_call(entry, in_specs=[anywhere, anywhere, pl.BlockSpec(memory_s...]
    broadcast_in_dim x1 -> x0, local copies, waits for them, and re-layouts: 1.36 us -> none  [band_step(): ease = jnp.broadcast_to(anisotropy[:, None], slab)]
where the time goes in v3:
time: 128 us
  Pallas kernels  121 us (95%)
  local copies, waits for them, and re-layouts  7.03 us (5%)
    pallas_call x1, Pallas kernels, band_step(): pl.pallas_call(entry, in_specs=[anywhere, anywhere, pl.BlockSpec(memory_s...  121 us
    unnamed x4, local copies, waits for them, and re-layouts  5.72 us

profile of v3, /device:TPU:0, one launch (start us, length us, event | category | flops | bytes accessed | tf_op | source)
XLA Modules:
  0.0 128.3 jit_solution(14913367694715131256)
XLA Ops:
  0.6 120.6 %band_kernel.1 = (f32[2,3,8,64,256]{4,3,2,1,0:T(8,128)}, f32[2,3,8,64,256]{4,3,2,1,0:T(8,128)}, f32[8,128]{1,0:T(8,128)}) custom-call(f32[2,3,8,64,256]{4,3,2,1,0:T(8,128)} %magnet_ref.1, f32[6,4,512,512]{3,2,1,0:T(8,128)} %kernel_ref.1, f32[64]{0:T(128)} %anisotropy_ref.1, bf16[2,256,512]{2,1,0:T(8,128)(2,1)} %constant.4.clone.refs_0_, ...), custom_call_target="tpu_custom_call" | custom-call | flops 28991029248 | bytes 12582912 | tf_op jit(solution)/shard_map/band_kernel/pallas_call | solution.py:1103
  121.2 1.3 %slice_reduce_fusion = f32[2]{0:T(128)} fusion(f32[8,128]{1,0:T(8,128)} %get-tuple-element.8), kind=kLoop, calls=%fused_computation | loop fusion | bytes 16 | tf_op jit(solution)/shard_map/slice | solution.py:1129
  122.5 0.0 copy-start
  122.5 4.1 %copy.10 = f32[2,3,8,64,256]{4,3,2,1,0:T(8,128)} copy(f32[2,3,8,64,256]{4,3,2,1,0:T(8,128)} %get-tuple-element.12) | data formatting | bytes 6291456
  126.6 0.0 copy-done
  126.6 1.7 %copy.11 = f32[2,3,8,64,256]{4,3,2,1,0:T(8,128)} copy(f32[2,3,8,64,256]{4,3,2,1,0:T(8,128)S(1)} %copy-done) | data formatting | bytes 6291456
Async XLA Ops:
  122.5 4.1 %copy-start = (f32[2,3,8,64,256]{4,3,2,1,0:T(8,128)S(1)}, f32[2,3,8,64,256]{4,3,2,1,0:T(8,128)}, u32[]{:S(2)}) copy-start(f32[2,3,8,64,256]{4,3,2,1,0:T(8,128)} %get-tuple-element.13) | copy-start | bytes 9437188

commit v4 on v3

--- a/solution.py
+++ b/solution.py
@@ -52,7 +52,9 @@
     even_part = np.cos(turn * (position * slot % (2 * count)))
     odd_part = np.sin(turn * (position * slot % (2 * count)))
     odd_part[:, 0] = np.cos(turn * (position[:, 0] * count % (2 * count)))
-    return np.concatenate([even_part, odd_part], axis=1)
+    table = np.concatenate([even_part, odd_part], axis=1)
+    table[:, [0, count]] *= math.sqrt(0.5)
+    return table
 
 
 def half_table(count):
@@ -94,10 +96,16 @@
             [(1.0, layers[0]), (cosine[half, k], layers[half])]
             + [(cosine[z, k], near[z]) for z in range(1, half)]
         )
-        im = weighted(
-            [(-sine[half, k], layers[half])] + [(-sine[z, k], far[z]) for z in range(1, half)]
-        )
-        spectrum.append((re, jnp.zeros_like(re) if im is None else im))
+        if k == 0:
+            im = weighted(
+                [(1.0, layers[0]), ((-1.0) ** half, layers[half])]
+                + [((-1.0) ** z, near[z]) for z in range(1, half)]
+            )
+        else:
+            im = weighted(
+                [(-sine[half, k], layers[half])] + [(-sine[z, k], far[z]) for z in range(1, half)]
+            )
+        spectrum.append((re, im))
     return spectrum
 
 
@@ -107,15 +115,16 @@
     cosine, sine = half_table(count)
     layers = [None] * count
     evens, odds = range(2, count, 2), range(1, count, 2)
-    layers[0] = weighted([(1.0, spectrum[0][0])] + [(2.0, spectrum[k][0]) for k in range(1, count)])
+    ground = [spectrum[0][0] + spectrum[0][1], spectrum[0][0] - spectrum[0][1]]
+    layers[0] = weighted([(1.0, ground[0])] + [(2.0, spectrum[k][0]) for k in range(1, count)])
     layers[half] = weighted(
-        [(1.0, spectrum[0][0])]
+        [(1.0, ground[half % 2])]
         + [(2.0 * cosine[half, k], spectrum[k][0]) for k in range(1, count)]
         + [(-2.0 * sine[half, k], spectrum[k][1]) for k in range(1, count)]
     )
     for z in range(1, half):
         even_re = weighted(
-            [(1.0, spectrum[0][0])] + [(2.0 * cosine[z, k], spectrum[k][0]) for k in evens]
+            [(1.0, ground[z % 2])] + [(2.0 * cosine[z, k], spectrum[k][0]) for k in evens]
         )
         odd_re = weighted([(2.0 * cosine[z, k], spectrum[k][0]) for k in odds])
         even_im = weighted([(2.0 * sine[z, k], spectrum[k][1]) for k in evens])
@@ -134,7 +143,7 @@
     return jnp.concatenate([upper, lower, upper], axis=axis)
 
 
-def tensor_part(c, spec_ref, kernel_ref, out_ref):
+def tensor_part(c, spec_ref, kernel_refs, out_ref):
     rows_full, columns_full = out_ref.shape[2] // 2, out_ref.shape[3] // 2
     lane = 128
     sub = 16
@@ -147,7 +156,8 @@
         edge_columns = slice(columns_full, columns_full + lane)
         first_column = start == 0
 
-        def loaded(component):
+        def loaded(component, part=0):
+            kernel_ref = kernel_refs[part]
             body = kernel_ref[component, rows, columns]
             side = kernel_ref[component, rows, edge_columns] if first_column else None
             if not first_row:
@@ -167,8 +177,8 @@
                 mixed = jnp.where(top, far, mixed)
             return mixed
 
-        own = loaded(c)
-        k_xy = pick(loaded(3), 0, 0) if c < 2 else None
+        own = [loaded(c, part) for part in range(2)]
+        k_xy = [pick(loaded(3, part), 0, 0) if c < 2 else None for part in range(2)]
         k_xz = loaded(4) if c != 1 else None
         k_yz = loaded(5) if c != 0 else None
 
@@ -182,7 +192,7 @@
 
         for px in range(2):
             for py in range(2):
-                own_here = pick(own, px, py)
+                own_here = [pick(own[part], px, py) for part in range(2)]
                 xz_here = pick(k_xz, 0, py) if c != 1 else None
                 yz_here = pick(k_yz, px, 0) if c != 0 else None
                 for part in range(2):
@@ -190,9 +200,9 @@
                     sx = turn if px else -turn
                     sy = turn if py else -turn
                     other = 1 - part
-                    total = own_here * spec(px, py, 2 * c + part)
+                    total = own_here[part] * spec(px, py, 2 * c + part)
                     if c < 2:
-                        across = k_xy * spec(1 - px, 1 - py, 2 * (1 - c) + part)
+                        across = k_xy[part] * spec(1 - px, 1 - py, 2 * (1 - c) + part)
                         total = total - across if px == py else total + across
                     if c == 0:
                         third = xz_here * spec(1 - px, py, 4 + other)
@@ -205,10 +215,6 @@
                         total = total + third if sx > 0 else total - third
                         third = yz_here * spec(px, 1 - py, 2 + other)
                         total = total + third if sy > 0 else total - third
-                    if first_row:
-                        total = jnp.where(top, 0.5 * total, total)
-                    if first_column:
-                        total = jnp.where(left, 0.5 * total, total)
                     upper, lower = split_limbs(total)
                     at_rows, at_columns = place(px, py)
                     out_ref[part, 0, at_rows, at_columns] = upper
@@ -250,15 +256,13 @@
     kernel_ref,
     anisotropy_ref,
     source_tables,
-    updated_ref,
     force_ref,
     small_ref,
     tables,
     cells_ref,
     film_ref,
-    stage_ref,
-    pair_ref,
-    extra_ref,
+    edge_out_ref,
+    edge_ref,
     send_ref,
     back_ref,
     held_ref,
@@ -281,14 +285,12 @@
     tensor_sem,
     film_send,
     film_recv,
-    pair_send,
-    pair_recv,
+    swap_plane_send,
+    swap_plane_recv,
     plane_send,
     plane_recv,
     back_send,
     back_recv,
-    extra_send,
-    extra_recv,
     last_send,
     last_recv,
     image_send,
@@ -300,7 +302,6 @@
     peak_send,
     peak_recv,
     force_sem,
-    update_sem,
     table_sem,
 ):
     fy_ref, fx_ref = tables[:2]
@@ -363,7 +364,7 @@
     def tensor_copy(q):
         return pltpu.make_async_copy(
             kernel_ref.at[:, q, pl.ds(0, rows_full + 8), pl.ds(0, columns_full + 128)],
-            tensor_ref.at[q],
+            tensor_ref.at[pl.ds(6 * q, 6)],
             tensor_sem.at[q],
         )
 
@@ -372,14 +373,45 @@
             magnet_ref.at[1 - half, c], film_ref.at[c], film_send.at[c], film_recv.at[c], partner
         )
 
-    def pair_copy(side, source):
-        return remote(
-            stage_ref.at[side],
-            pair_ref.at[source],
-            pair_send.at[side],
-            pair_recv.at[source],
-            side * parts,
-        )
+    def kernel_copies():
+        body = (pl.ds(0, rows_full), pl.ds(0, columns_full))
+        far = (pl.ds(rows_full, 8), pl.ds(0, columns_full + 128))
+        pieces = [
+            (kernel_ref.at[pl.ds(0, 4), 0, *body], tensor_ref.at[pl.ds(6 * local_planes, 4), *body]),
+            (kernel_ref.at[pl.ds(0, 3), 0, *far], tensor_ref.at[pl.ds(6 * local_planes, 3), *far]),
+            (edge_out_ref, edge_ref),
+        ]
+        return [
+            remote(src, dst, swap_plane_send.at[n], swap_plane_recv.at[n], partner)
+            for n, (src, dst) in enumerate(pieces)
+        ]
+
+    def pack_edges():
+        lane_pos = lax.broadcasted_iota(jnp.int32, (row_step, 128), 1)
+        columns = pl.ds(columns_full, 128)
+
+        def step(i, carry):
+            rows = pl.ds(pl.multiple_of(i * row_step, row_step), row_step)
+            edges = [tensor_ref[c, rows, columns] for c in range(3)]
+            edge = jnp.where(lane_pos == 1, pltpu.roll(edges[1], 1, 1), edges[0])
+            edge_out_ref[rows, :] = jnp.where(lane_pos == 2, pltpu.roll(edges[2], 2, 1), edge)
+            return carry
+
+        lax.fori_loop(0, rows_full // row_step, step, 0)
+
+    def unpack_edges():
+        columns = pl.ds(columns_full, 128)
+
+        def step(i, carry):
+            rows = pl.ds(pl.multiple_of(i * row_step, row_step), row_step)
+            edge = edge_ref[rows, :]
+            for c in range(3):
+                tensor_ref[6 * local_planes + c, rows, columns] = (
+                    pltpu.roll(edge, 128 - c, 1) if c else edge
+                )
+            return carry
+
+        lax.fori_loop(0, rows_full // row_step, step, 0)
 
     def place_of(seat_index, kind):
         return lax.rem((half + kind) * parts + seat_index, groups)
@@ -424,25 +456,6 @@
             half * parts + source,
         )
 
-    def extra_copy(c, step):
-        target = lax.rem(me + step, groups)
-        return remote(
-            held_ref.at[c, target, 0, 1],
-            extra_ref.at[half, c],
-            extra_send.at[c, step],
-            extra_recv.at[half, c],
-            target,
-        )
-
-    def extra_arrival(side, c):
-        return remote(
-            held_ref.at[c, 0, 0, 1],
-            extra_ref.at[side, c],
-            extra_send.at[c, 0],
-            extra_recv.at[side, c],
-            side * parts,
-        )
-
     def last_copy(c):
         return remote(
             film_ref.at[c], arrive_ref.at[c], last_send.at[c], last_recv.at[c], partner
@@ -491,9 +504,6 @@
 
     def table_copy(n):
         return pltpu.make_async_copy(source_tables[n], tables[n], table_sem.at[n])
-
-    def update_copy(i):
-        return pltpu.make_async_copy(cells_ref.at[i], updated_ref.at[i], update_sem.at[i])
 
     def force_copy(i):
         return pltpu.make_async_copy(field_ref.at[i], force_ref.at[i], force_sem.at[i])
@@ -636,13 +646,14 @@
     lane = columns_full
 
     def cell_loop(step, carry):
-        steps = slab // (2 * row_step)
+        unrolled = min(4, slab // row_step)
+        steps = slab // (unrolled * row_step)
 
         def chunk(index, carry):
             z = index // steps
-            start = pl.multiple_of(lax.rem(index, steps) * 2 * row_step, 2 * row_step)
-            for offset in (0, row_step):
-                carry = step(z, pl.multiple_of(start + offset, row_step), carry)
+            start = lax.rem(index, steps) * unrolled * row_step
+            for n in range(unrolled):
+                carry = step(z, pl.multiple_of(start + n * row_step, row_step), carry)
             return carry
 
         return lax.fori_loop(0, layer_count * steps, chunk, carry)
@@ -711,16 +722,13 @@
                 sums_ref[i, k + 1] = totals[k]
 
     def field_sums(i, c, arrived):
-        turn = (2 * i - 1).astype(jnp.float32)
-
         def step(z, start, carry):
             rows = pl.ds(start, row_step)
             place = tangent_rows(z, start)
-            sign = scale * jnp.where(lax.rem(z, 2) == 1, turn, 1.0)
-            field = field_ref[i, c, z, rows, :] + sign * extra_ref[1 - i, c, rows, :]
+            field = field_ref[i, c, z, rows, :]
             if arrived:
                 field = field + arrive_ref[c, z, rows, :]
-            field_ref[i, c, z, rows, :] = field
+                field_ref[i, c, z, rows, :] = field
             values = (
                 cells_ref[i, c, z, rows, :] * field,
                 field * spec_ref[0, 3 * i + c, place, 0:columns_full],
@@ -767,27 +775,14 @@
     for c in range(3):
         own_copy(c).wait()
     fill_rims()
-    for side in range(2):
-
-        def sum_layers(rows):
-            for c in range(3):
-                layers = [cells_ref[1 - side, c, z, rows, :] for z in range(layer_count)]
-                stage_ref[side, c, rows, :] = weighted(
-                    [((-1.0) ** (z * side), layers[z]) for z in range(layer_count)]
-                )
-
-        row_loop(sum_layers)
-
-        @pl.when(me == side * parts)
-        def _():
-            pair_ref[me] = stage_ref[side]
-
-        @pl.when(me != side * parts)
-        def _():
-            pair_copy(side, me).start()
-
     for c in range(1, 3):
         film_copy(c).start()
+
+    @pl.when(seat == 0)
+    def _():
+        for copy in kernel_copies()[:2]:
+            copy.start()
+
     for q in range(local_planes):
         tensor_copy(q).start()
 
@@ -795,6 +790,13 @@
         transform_layers(c, 0)
     for n in range(len(tables)):
         table_copy(n).wait()
+    tensor_copy(0).wait()
+
+    @pl.when(seat == 0)
+    def _():
+        pack_edges()
+        kernel_copies()[2].start()
+
     for c in range(3):
         film_copy(c).wait_recv()
         transform_layers(c, 1)
@@ -803,16 +805,7 @@
                 plane_arrival(c, kind, slot).wait_recv()
 
         def forward(i, carry):
-            q = local_planes - 1 - i
-
-            @pl.when((seat == 0) & (q == 0))
-            def _():
-                if c == 0:
-                    for d in range(1, groups):
-                        pair_copy(0, lax.rem(me + d, groups)).wait_recv()
-                for g in range(groups):
-                    held_ref[c, g, 0, 1] = pair_ref[g, c]
-
+            q = i
             fy = jnp.concatenate([fy_ref[0], fy_ref[0], fy_ref[1]], axis=0)
             fx = jnp.concatenate([fx_ref[0], fx_ref[0], fx_ref[1]], axis=1)
             cells = jnp.concatenate(
@@ -831,13 +824,25 @@
         if c < 2:
             local_fields(c)
 
-    for q in range(local_planes):
+    for q in range(1, local_planes):
         tensor_copy(q).wait()
 
     for c in range(3):
 
-        def backward(q, carry):
-            tensor_part(c, spec_ref.at[q], tensor_ref.at[q], result_ref)
+        def backward(i, carry):
+            q = local_planes - 1 - i
+            twin = (seat == 0) & (q == 0)
+            if c == 0:
+
+                @pl.when(twin)
+                def _():
+                    for copy in kernel_copies():
+                        copy.wait_recv()
+                    unpack_edges()
+
+            second = jnp.where(twin, local_planes, q)
+            kernels = (tensor_ref.at[pl.ds(6 * q, 6)], tensor_ref.at[pl.ds(6 * second, 4)])
+            tensor_part(c, spec_ref.at[q], kernels, result_ref)
             gx = jnp.concatenate([gx_ref[0], gx_ref[0], gx_ref[1]], axis=1)
             gy = jnp.concatenate([gy_ref[0], gy_ref[0], gy_ref[1]], axis=0)
             for part in range(2):
@@ -850,12 +855,6 @@
                 for slot in range(parts - 1):
                     back_copy(c, q, kind, slot).start()
 
-            @pl.when((seat == 0) & (q == 0))
-            def _():
-                extra_ref[half, c] = held_ref[c, me, 0, 1]
-                for step in range(1, groups):
-                    extra_copy(c, step).start()
-
             return carry
 
         lax.fori_loop(0, local_planes, backward, 0)
@@ -869,12 +868,6 @@
 
     neighbour_sums()
     for c in range(3):
-        for side in range(2):
-
-            @pl.when(me != side * parts)
-            def _():
-                extra_arrival(side, c).wait_recv()
-
         field_sums(half, c, False)
     for c in range(3):
         last_copy(c).wait_recv()
@@ -963,27 +956,10 @@
     for g in range(1, groups):
         largest = jnp.maximum(largest, peak_ref[g])
     moves = jnp.minimum(step_limit, rotation_limit / (jnp.sqrt(largest) + epsilon))
-    for i in range(2):
-        move = jnp.broadcast_to(moves[i : i + 1], (row_step, 128))
-        move = jnp.concatenate([move] * (lane // 128), axis=1)
-
-        def step(z, start, carry):
-            rows = pl.ds(start, row_step)
-            moved = [
-                cells_ref[i, c, z, rows, :] + move * field_ref[i, c, z, rows, :] for c in range(3)
-            ]
-            inverse = 1.0 / jnp.sqrt(dot3(moved, moved))
-            for c in range(3):
-                cells_ref[i, c, z, rows, :] = inverse * moved[c]
-            return carry
-
-        cell_loop(step, 0)
-        update_copy(i).start()
-    energy = jnp.concatenate(energies[1:3] + [jnp.zeros((6, 128), jnp.float32)], axis=0)
-    small_ref[...] = energy / cell_count
+    energy = jnp.concatenate(energies[1:3], axis=0) / cell_count
+    small_ref[...] = jnp.concatenate([moves[0:2], energy, jnp.zeros((4, 128), jnp.float32)], axis=0)
     for i in range(2):
         force_copy(i).wait()
-        update_copy(i).wait()
     for d in range(1, groups):
         peak_copy(d, me).wait_send()
     for c in range(3):
@@ -997,9 +973,8 @@
 
     @pl.when(seat == 0)
     def _():
-        for c in range(3):
-            for step in range(1, groups):
-                extra_copy(c, step).wait_send()
+        for copy in kernel_copies():
+            copy.wait_send()
 
     for side in range(2):
         open_side = me != groups - 1 if side == 0 else me != 0
@@ -1007,10 +982,6 @@
         @pl.when(open_side)
         def _():
             rim_copy(side).wait_send()
-
-        @pl.when(me != side * parts)
-        def _():
-            pair_copy(side, me).wait_send()
 
     @pl.when(jnp.logical_not(last))
     def _():
@@ -1034,8 +1005,8 @@
 
     def entry(magnet_ref, kernel_ref, anisotropy_ref, *refs):
         count = len(tables)
-        sources, outs = refs[:count], refs[count : count + 3]
-        held, rest = refs[count + 3 : 2 * count + 3], refs[2 * count + 3 :]
+        sources, outs = refs[:count], refs[count : count + 2]
+        held, rest = refs[count + 2 : 2 * count + 2], refs[2 * count + 2 :]
         scale = -4.0 / padded_cells
         band_kernel(
             scale, magnet_ref, kernel_ref, anisotropy_ref, sources, *outs, held, *rest
@@ -1052,9 +1023,8 @@
     scratch = [
         (2, 3) + film,
         (3,) + film,
-        (2, 3) + slab,
-        (groups, 3) + slab,
-        (2, 3) + slab,
+        (full_rows, 128),
+        (full_rows, 128),
         (3, 2, slots) + block,
         (3, 2, slots) + block,
         (3, groups) + block,
@@ -1071,21 +1041,19 @@
         (16, 128),
         (3, groups, 16, 128),
         (groups, 8, 128),
-        (local_planes, 6, full_rows + 8, column_count + 128),
+        (6 * local_planes + 4, full_rows + 8, column_count + 128),
     ]
     semaphores = [
         (3,),
         (local_planes,),
         (3,),
         (3,),
-        (2,),
-        (groups,),
+        (3,),
+        (3,),
         (3, 2, slots),
         (3, 2, slots),
         (3, local_planes, 2, slots),
         (3, local_planes, 2, slots),
-        (3, groups),
-        (2, 3),
         (3,),
         (3,),
         (2,),
@@ -1097,16 +1065,14 @@
         (groups,),
         (groups,),
         (2,),
-        (2,),
         (len(tables),),
     ]
     return pl.pallas_call(
         entry,
         in_specs=[anywhere, anywhere, pl.BlockSpec(memory_space=pltpu.SMEM)]
         + [anywhere] * len(tables),
-        out_specs=[anywhere, anywhere, inside],
+        out_specs=[anywhere, inside],
         out_shape=[
-            jax.ShapeDtypeStruct(magnet.shape, jnp.float32),
             jax.ShapeDtypeStruct(magnet.shape, jnp.float32),
             jax.ShapeDtypeStruct((8, 128), jnp.float32),
         ],
@@ -1124,9 +1090,59 @@
     )(magnet, kernel, anisotropy, *[jnp.asarray(t) for t in tables])
 
 
+def move_kernel(small_ref, magnet_ref, force_ref, updated_ref, out_ref, energy_ref):
+    i = pl.program_id(0)
+    layers, slab, columns = magnet_ref.shape[2:]
+
+    @pl.when((i == 0) & (pl.program_id(1) == 0))
+    def _():
+        for n in range(2):
+            energy_ref[n] = jnp.max(small_ref[n + 2 : n + 3, :])
+
+    row_step = 8
+    move = jnp.broadcast_to(small_ref[pl.ds(i, 1), :], (row_step, 128))
+    move = jnp.concatenate([move] * (columns // 128), axis=1)
+    unrolled = min(4, slab // row_step)
+
+    def chunk(index, carry):
+        for z in range(layers):
+            for n in range(unrolled):
+                start = (index * unrolled + n) * row_step
+                rows = pl.ds(pl.multiple_of(start, row_step), row_step)
+                force = [force_ref[0, c, z, rows, :] for c in range(3)]
+                moved = [magnet_ref[0, c, z, rows, :] + move * force[c] for c in range(3)]
+                inverse = lax.rsqrt(dot3(moved, moved))
+                for c in range(3):
+                    updated_ref[0, c, z, rows, :] = inverse * moved[c]
+                    out_ref[0, c, z, rows, :] = force[c]
+        return carry
+
+    lax.fori_loop(0, slab // (unrolled * row_step), chunk, 0)
+
+
+def move_images(magnet, force, small):
+    images, _, layer_count, row_count, column_count = magnet.shape
+    layers = max(1, layer_count // 4)
+    block = pl.BlockSpec(
+        (1, 3, layers, row_count, column_count), lambda i, k: (i, 0, k, 0, 0)
+    )
+    return pl.pallas_call(
+        move_kernel,
+        grid=(images, layer_count // layers),
+        in_specs=[pl.BlockSpec((8, 128), lambda i, k: (0, 0)), block, block],
+        out_specs=[block, block, pl.BlockSpec(memory_space=pltpu.SMEM)],
+        out_shape=[
+            jax.ShapeDtypeStruct(magnet.shape, jnp.float32),
+            jax.ShapeDtypeStruct(magnet.shape, jnp.float32),
+            jax.ShapeDtypeStruct((images,), jnp.float32),
+        ],
+        name="move_kernel",
+    )(small, magnet, force)
+
+
 def body(magnet, anisotropy, kernel):
-    updated, band_force, small = band_step(magnet, anisotropy, kernel)
-    return (updated, band_force, small[: magnet.shape[0], 0])
+    force, small = band_step(magnet, anisotropy, kernel)
+    return move_images(magnet, force, small)
 
 
 def solution(mesh):

time: 128 us -> 121 us (0.945)
  local copies, waits for them, and re-layouts: 7.03 us -> 0 us
    pallas_call x1, Pallas kernels: 121 us -> 112 us  [band_step(): pl.pallas_call(entry, in_specs=[anywhere, anywhere, pl.BlockSpec(memory_s...]
    pallas_call x0 -> x1, Pallas kernels: none -> 8.08 us  [move_images(): pl.pallas_call(move_kernel, grid=(images, layer_count // layers), in_spec...]
    unnamed x4 -> x0, local copies, waits for them, and re-layouts: 5.72 us -> none
    slice x1 -> x0, local copies, waits for them, and re-layouts: 1.31 us -> none  [body(): return (updated, band_force, small[:magnet.shape[0], 0])]
where the time goes in v4:
time: 121 us
  Pallas kernels  120 us (99%)
    pallas_call x1, Pallas kernels, band_step(): pl.pallas_call(entry, in_specs=[anywhere, anywhere, pl.BlockSpec(memory_s...  112 us
    pallas_call x1, Pallas kernels, move_images(): pl.pallas_call(move_kernel, grid=(images, layer_count // layers), in_spec...  8.08 us

profile of v4, /device:TPU:0, one launch (start us, length us, event | category | flops | bytes accessed | tf_op | source)
XLA Modules:
  0.0 120.8 jit_solution(16737848137719231607)
XLA Ops:
  0.6 112.0 %band_kernel.1 = (f32[2,3,8,64,256]{4,3,2,1,0:T(8,128)}, f32[8,128]{1,0:T(8,128)}) custom-call(f32[2,3,8,64,256]{4,3,2,1,0:T(8,128)} %magnet_ref.3, f32[6,4,512,512]{3,2,1,0:T(8,128)} %kernel_ref.1, f32[64]{0:T(128)} %anisotropy_ref.1, bf16[2,256,512]{2,1,0:T(8,128)(2,1)} %constant.4.clone.refs_0_, bf16[2,512,256]{2,1,0:T(8,128)(2,1)} %constant.5.clone.refs_1_), custom_call_target="tpu_custom_call" | custom-call | flops 28991029248 | bytes 12582912 | tf_op jit(solution)/shard_map/band_kernel/pallas_call | solution.py:1070
  112.7 8.1 %move_kernel.1 = (f32[2,3,8,64,256]{4,3,2,1,0:T(8,128)}, f32[2,3,8,64,256]{4,3,2,1,0:T(8,128)}, f32[2]{0:T(128)}) custom-call(f32[8,128]{1,0:T(8,128)} %get-tuple-element.5.small_ref, f32[2,3,8,64,256]{4,3,2,1,0:T(8,128)} %magnet_ref.3, f32[2,3,8,64,256]{4,3,2,1,0:T(8,128)} %get-tuple-element.6.force_ref), custom_call_target="tpu_custom_call" | custom-call | tf_op jit(solution)/shard_map/move_kernel/pallas_call | solution.py:1129

commit v5 on v4

--- a/solution.py
+++ b/solution.py
@@ -144,9 +144,9 @@
 
 
 def tensor_part(c, spec_ref, kernel_refs, out_ref):
-    rows_full, columns_full = out_ref.shape[2] // 2, out_ref.shape[3] // 2
+    rows_full, columns_full = out_ref.shape[1] // 2, out_ref.shape[2] // 2
     lane = 128
-    sub = 16
+    sub = 8
     top = lax.broadcasted_iota(jnp.int32, (sub, lane), 0) == 0
     left = lax.broadcasted_iota(jnp.int32, (sub, lane), 1) == 0
 
@@ -215,21 +215,26 @@
                         total = total + third if sx > 0 else total - third
                         third = yz_here * spec(px, 1 - py, 2 + other)
                         total = total + third if sy > 0 else total - third
-                    upper, lower = split_limbs(total)
                     at_rows, at_columns = place(px, py)
-                    out_ref[part, 0, at_rows, at_columns] = upper
-                    out_ref[part, 1, at_rows, at_columns] = lower
+                    out_ref[part, at_rows, at_columns] = total
 
     for start in range(0, columns_full, lane):
         tile(0, True, start)
 
+    unrolled = 3
+    peeled = (rows_full // sub - 1) % unrolled + 1
+    for n in range(1, peeled):
+        for start in range(0, columns_full, lane):
+            tile(n * sub, False, start)
+
     def step(i, carry):
-        row_start = pl.multiple_of(i * sub, sub)
-        for start in range(0, columns_full, lane):
-            tile(row_start, False, start)
+        for n in range(unrolled):
+            row_start = pl.multiple_of((unrolled * i + n + peeled) * sub, sub)
+            for start in range(0, columns_full, lane):
+                tile(row_start, False, start)
         return carry
 
-    lax.fori_loop(1, rows_full // sub, step, 0)
+    lax.fori_loop(0, (rows_full // sub - peeled) // unrolled, step, 0)
 
 
 def arc_angle(sine, cosine):
@@ -285,8 +290,8 @@
     tensor_sem,
     film_send,
     film_recv,
-    swap_plane_send,
-    swap_plane_recv,
+    twin_send,
+    twin_recv,
     plane_send,
     plane_recv,
     back_send,
@@ -376,42 +381,31 @@
     def kernel_copies():
         body = (pl.ds(0, rows_full), pl.ds(0, columns_full))
         far = (pl.ds(rows_full, 8), pl.ds(0, columns_full + 128))
-        pieces = [
-            (kernel_ref.at[pl.ds(0, 4), 0, *body], tensor_ref.at[pl.ds(6 * local_planes, 4), *body]),
-            (kernel_ref.at[pl.ds(0, 3), 0, *far], tensor_ref.at[pl.ds(6 * local_planes, 3), *far]),
+        twin = 6 * local_planes
+        pieces = [(tensor_ref.at[n, *body], tensor_ref.at[twin + n, *body]) for n in (0, 3)]
+        pieces += [
             (edge_out_ref, edge_ref),
+            (tensor_ref.at[pl.ds(0, 3), *far], tensor_ref.at[pl.ds(twin, 3), *far]),
         ]
+        pieces += [(tensor_ref.at[n, *body], tensor_ref.at[twin + n, *body]) for n in (1, 2)]
         return [
-            remote(src, dst, swap_plane_send.at[n], swap_plane_recv.at[n], partner)
+            remote(src, dst, twin_send.at[n], twin_recv.at[n], partner)
             for n, (src, dst) in enumerate(pieces)
         ]
 
     def pack_edges():
-        lane_pos = lax.broadcasted_iota(jnp.int32, (row_step, 128), 1)
-        columns = pl.ds(columns_full, 128)
-
-        def step(i, carry):
-            rows = pl.ds(pl.multiple_of(i * row_step, row_step), row_step)
-            edges = [tensor_ref[c, rows, columns] for c in range(3)]
-            edge = jnp.where(lane_pos == 1, pltpu.roll(edges[1], 1, 1), edges[0])
-            edge_out_ref[rows, :] = jnp.where(lane_pos == 2, pltpu.roll(edges[2], 2, 1), edge)
-            return carry
-
-        lax.fori_loop(0, rows_full // row_step, step, 0)
+        rows, columns = pl.ds(0, rows_full), pl.ds(columns_full, 128)
+        lane_pos = lax.broadcasted_iota(jnp.int32, (rows_full, 128), 1)
+        edge = tensor_ref[0, rows, columns]
+        for c in (1, 2):
+            edge = jnp.where(lane_pos == c, pltpu.roll(tensor_ref[c, rows, columns], c, 1), edge)
+        edge_out_ref[...] = edge
 
     def unpack_edges():
-        columns = pl.ds(columns_full, 128)
-
-        def step(i, carry):
-            rows = pl.ds(pl.multiple_of(i * row_step, row_step), row_step)
-            edge = edge_ref[rows, :]
-            for c in range(3):
-                tensor_ref[6 * local_planes + c, rows, columns] = (
-                    pltpu.roll(edge, 128 - c, 1) if c else edge
-                )
-            return carry
-
-        lax.fori_loop(0, rows_full // row_step, step, 0)
+        rows, columns = pl.ds(0, rows_full), pl.ds(columns_full, 128)
+        edge = edge_ref[...]
+        for c in range(3):
+            tensor_ref[6 * local_planes + c, rows, columns] = pltpu.roll(edge, 128 - c, 1) if c else edge
 
     def place_of(seat_index, kind):
         return lax.rem((half + kind) * parts + seat_index, groups)
@@ -778,11 +772,6 @@
     for c in range(1, 3):
         film_copy(c).start()
 
-    @pl.when(seat == 0)
-    def _():
-        for copy in kernel_copies()[:2]:
-            copy.start()
-
     for q in range(local_planes):
         tensor_copy(q).start()
 
@@ -795,7 +784,8 @@
     @pl.when(seat == 0)
     def _():
         pack_edges()
-        kernel_copies()[2].start()
+        for copy in kernel_copies():
+            copy.start()
 
     for c in range(3):
         film_copy(c).wait_recv()
@@ -832,12 +822,12 @@
         def backward(i, carry):
             q = local_planes - 1 - i
             twin = (seat == 0) & (q == 0)
-            if c == 0:
-
-                @pl.when(twin)
-                def _():
-                    for copy in kernel_copies():
-                        copy.wait_recv()
+
+            @pl.when(twin)
+            def _():
+                for copy in kernel_copies()[:4] if c == 0 else kernel_copies()[c + 3 : c + 4]:
+                    copy.wait_recv()
+                if c == 0:
                     unpack_edges()
 
             second = jnp.where(twin, local_planes, q)
@@ -846,8 +836,7 @@
             gx = jnp.concatenate([gx_ref[0], gx_ref[0], gx_ref[1]], axis=1)
             gy = jnp.concatenate([gy_ref[0], gy_ref[0], gy_ref[1]], axis=0)
             for part in range(2):
-                upper, lower = result_ref[part, 0], result_ref[part, 1]
-                lines = dot32(gx, jnp.concatenate([upper, lower, upper], axis=0))
+                lines = dot32(gx, three_limbs(result_ref[part], 0))
                 cells = dot32(three_limbs(lines, 1), gy)
                 for g in range(groups):
                     held_ref[c, g, q, part] = cells[g * slab : (g + 1) * slab]
@@ -1048,8 +1037,8 @@
         (local_planes,),
         (3,),
         (3,),
-        (3,),
-        (3,),
+        (6,),
+        (6,),
         (3, 2, slots),
         (3, 2, slots),
         (3, local_planes, 2, slots),
@@ -1078,7 +1067,7 @@
         ],
         scratch_shapes=[pltpu.VMEM(t.shape, jnp.bfloat16) for t in tables]
         + [pltpu.VMEM(dims, jnp.float32) for dims in scratch]
-        + [pltpu.VMEM((2, 2, 2 * full_rows, 2 * column_count), jnp.bfloat16)]
+        + [pltpu.VMEM((2, 2 * full_rows, 2 * column_count), jnp.float32)]
         + [signals(dims) for dims in semaphores],
         compiler_params=pltpu.CompilerParams(
             vmem_limit_bytes=67043328, collective_id=0, has_side_effects=True
@@ -1090,52 +1079,87 @@
     )(magnet, kernel, anisotropy, *[jnp.asarray(t) for t in tables])
 
 
-def move_kernel(small_ref, magnet_ref, force_ref, updated_ref, out_ref, energy_ref):
-    i = pl.program_id(0)
-    layers, slab, columns = magnet_ref.shape[2:]
-
-    @pl.when((i == 0) & (pl.program_id(1) == 0))
-    def _():
-        for n in range(2):
-            energy_ref[n] = jnp.max(small_ref[n + 2 : n + 3, :])
-
+def move_kernel(
+    small_ref,
+    magnet_ref,
+    force_ref,
+    updated_ref,
+    out_ref,
+    energy_ref,
+    cells_ref,
+    held_ref,
+    magnet_sem,
+    force_sem,
+    updated_sem,
+    out_sem,
+):
+    images, _, layer_count, slab, columns = magnet_ref.shape
+    pieces = magnet_sem.shape[1]
+    layers = layer_count // pieces
+
+    def copy(src, dst, sem, i, k):
+        part = pl.ds(k * layers, layers)
+        return pltpu.make_async_copy(src.at[i, :, part], dst.at[i, :, part], sem.at[i, k])
+
+    places = [(i, k) for i in range(images) for k in range(pieces)]
+    ahead = 4
+
+    def load(i, k):
+        copy(force_ref, held_ref, force_sem, i, k).start()
+        copy(magnet_ref, cells_ref, magnet_sem, i, k).start()
+
+    for i, k in places[:ahead]:
+        load(i, k)
+    for n in range(images):
+        energy_ref[n] = jnp.max(small_ref[n + 2 : n + 3, :])
     row_step = 8
-    move = jnp.broadcast_to(small_ref[pl.ds(i, 1), :], (row_step, 128))
-    move = jnp.concatenate([move] * (columns // 128), axis=1)
     unrolled = min(4, slab // row_step)
-
-    def chunk(index, carry):
-        for z in range(layers):
+    steps = slab // (unrolled * row_step)
+    for index, (i, k) in enumerate(places):
+        move = jnp.broadcast_to(small_ref[i : i + 1, :], (row_step, 128))
+        move = jnp.concatenate([move] * (columns // 128), axis=1)
+        copy(force_ref, held_ref, force_sem, i, k).wait()
+        copy(held_ref, out_ref, out_sem, i, k).start()
+        copy(magnet_ref, cells_ref, magnet_sem, i, k).wait()
+        for place in places[index + ahead : index + ahead + 1]:
+            load(*place)
+
+        def chunk(index, carry):
+            z = k * layers + index // steps
             for n in range(unrolled):
-                start = (index * unrolled + n) * row_step
+                start = (lax.rem(index, steps) * unrolled + n) * row_step
                 rows = pl.ds(pl.multiple_of(start, row_step), row_step)
-                force = [force_ref[0, c, z, rows, :] for c in range(3)]
-                moved = [magnet_ref[0, c, z, rows, :] + move * force[c] for c in range(3)]
+                moved = [
+                    cells_ref[i, c, z, rows, :] + move * held_ref[i, c, z, rows, :]
+                    for c in range(3)
+                ]
                 inverse = lax.rsqrt(dot3(moved, moved))
                 for c in range(3):
-                    updated_ref[0, c, z, rows, :] = inverse * moved[c]
-                    out_ref[0, c, z, rows, :] = force[c]
-        return carry
-
-    lax.fori_loop(0, slab // (unrolled * row_step), chunk, 0)
+                    cells_ref[i, c, z, rows, :] = inverse * moved[c]
+            return carry
+
+        lax.fori_loop(0, layers * steps, chunk, 0)
+        copy(cells_ref, updated_ref, updated_sem, i, k).start()
+    for i, k in places:
+        copy(held_ref, out_ref, out_sem, i, k).wait()
+        copy(cells_ref, updated_ref, updated_sem, i, k).wait()
 
 
 def move_images(magnet, force, small):
-    images, _, layer_count, row_count, column_count = magnet.shape
-    layers = max(1, layer_count // 4)
-    block = pl.BlockSpec(
-        (1, 3, layers, row_count, column_count), lambda i, k: (i, 0, k, 0, 0)
-    )
+    images, _, layer_count = magnet.shape[:3]
+    pieces = math.gcd(layer_count, 2)
+    anywhere = pl.BlockSpec(memory_space=pl.ANY)
     return pl.pallas_call(
         move_kernel,
-        grid=(images, layer_count // layers),
-        in_specs=[pl.BlockSpec((8, 128), lambda i, k: (0, 0)), block, block],
-        out_specs=[block, block, pl.BlockSpec(memory_space=pltpu.SMEM)],
+        in_specs=[pl.BlockSpec(memory_space=pltpu.VMEM), anywhere, anywhere],
+        out_specs=[anywhere, anywhere, pl.BlockSpec(memory_space=pltpu.SMEM)],
         out_shape=[
             jax.ShapeDtypeStruct(magnet.shape, jnp.float32),
             jax.ShapeDtypeStruct(magnet.shape, jnp.float32),
             jax.ShapeDtypeStruct((images,), jnp.float32),
         ],
+        scratch_shapes=[pltpu.VMEM(magnet.shape, jnp.float32)] * 2
+        + [pltpu.SemaphoreType.DMA((images, pieces))] * 4,
         name="move_kernel",
     )(small, magnet, force)
 

time: 121 us -> 114 us (0.942)
  Pallas kernels: 120 us -> 114 us
    pallas_call x1, Pallas kernels: 112 us -> 107 us  [band_step(): pl.pallas_call(entry, in_specs=[anywhere, anywhere, pl.BlockSpec(memory_s...]
    pallas_call x1, Pallas kernels: 8.08 us -> 6.5 us  [move_images(): pl.pallas_call(move_kernel, in_specs=[pl.BlockSpec(memory_space=pltpu.VME...]
where the time goes in v5:
time: 114 us
  Pallas kernels  114 us (100%)
    pallas_call x1, Pallas kernels, band_step(): pl.pallas_call(entry, in_specs=[anywhere, anywhere, pl.BlockSpec(memory_s...  107 us
    pallas_call x1, Pallas kernels, move_images(): pl.pallas_call(move_kernel, in_specs=[pl.BlockSpec(memory_space=pltpu.VME...  6.5 us

profile of v5, /device:TPU:0, one launch (start us, length us, event | category | flops | bytes accessed | tf_op | source)
XLA Modules:
  0.0 114.2 jit_solution(2092736895888507572)
XLA Ops:
  0.6 107.1 %band_kernel.1 = (f32[2,3,8,64,256]{4,3,2,1,0:T(8,128)}, f32[8,128]{1,0:T(8,128)}) custom-call(f32[2,3,8,64,256]{4,3,2,1,0:T(8,128)} %magnet_ref.3, f32[6,4,512,512]{3,2,1,0:T(8,128)} %kernel_ref.1, f32[64]{0:T(128)} %anisotropy_ref.1, bf16[2,256,512]{2,1,0:T(8,128)(2,1)} %constant.4.clone.refs_0_, bf16[2,512,256]{2,1,0:T(8,128)(2,1)} %constant.5.clone.refs_1_), custom_call_target="tpu_custom_call" | custom-call | flops 28991029248 | bytes 12582912 | tf_op jit(solution)/shard_map/band_kernel/pallas_call | solution.py:1059
  107.7 6.5 %move_kernel.1 = (f32[2,3,8,64,256]{4,3,2,1,0:T(8,128)}, f32[2,3,8,64,256]{4,3,2,1,0:T(8,128)}, f32[2]{0:T(128)}) custom-call(f32[8,128]{1,0:T(8,128)} %get-tuple-element.5.small_ref, f32[2,3,8,64,256]{4,3,2,1,0:T(8,128)} %magnet_ref.3, f32[2,3,8,64,256]{4,3,2,1,0:T(8,128)} %get-tuple-element.6.force_ref), custom_call_target="tpu_custom_call" | custom-call | tf_op jit(solution)/shard_map/move_kernel/pallas_call | solution.py:1152

commit v6 on v5

--- a/solution.py
+++ b/solution.py
@@ -261,7 +261,7 @@
     kernel_ref,
     anisotropy_ref,
     source_tables,
-    force_ref,
+    field_ref,
     small_ref,
     tables,
     cells_ref,
@@ -272,7 +272,6 @@
     back_ref,
     held_ref,
     spec_ref,
-    field_ref,
     arrive_ref,
     next_ref,
     prior_ref,
@@ -306,7 +305,6 @@
     swap_recv,
     peak_send,
     peak_recv,
-    force_sem,
     table_sem,
 ):
     fy_ref, fx_ref = tables[:2]
@@ -413,7 +411,7 @@
     def plane_copy(c, kind, slot):
         target = lax.rem(seat + 1 + slot, parts)
         return remote(
-            send_ref.at[c, kind, slot],
+            send_ref.at[3 if kind else c, slot],
             held_ref.at[c, place_of(seat, kind)],
             plane_send.at[c, kind, slot],
             plane_recv.at[c, kind, parts - 2 - slot],
@@ -423,7 +421,7 @@
     def plane_arrival(c, kind, slot):
         source = lax.rem(seat + 1 + slot, parts)
         return remote(
-            send_ref.at[c, kind, slot],
+            send_ref.at[3 if kind else c, slot],
             held_ref.at[c, place_of(source, kind)],
             plane_send.at[c, kind, slot],
             plane_recv.at[c, kind, slot],
@@ -449,6 +447,84 @@
             back_recv.at[c, q, kind, slot],
             half * parts + source,
         )
+
+    def last_copy(c):
+        return remote(
+            film_ref.at[c], arrive_ref.at[c], last_send.at[c], last_recv.at[c], partner
+        )
+
+    def ahead_copy():
+        return remote(
+            magnet_ref.at[1],
+            prior_ref,
+            image_send.at[0],
+            image_recv.at[0],
+            {"image": lax.rem(image + 1, images)},
+        )
+
+    def behind_copy():
+        return remote(
+            magnet_ref.at[0],
+            next_ref,
+            image_send.at[1],
+            image_recv.at[1],
+            {"image": lax.rem(image + images - 1, images)},
+        )
+
+    def rim_copy(side):
+        return remote(
+            rim_out_ref.at[side],
+            rim_ref.at[side],
+            rim_send.at[side],
+            rim_recv.at[side],
+            lax.rem(me + (1 if side == 0 else groups - 1), groups),
+        )
+
+    def swap_copy(n, shift, d, slot):
+        return remote(
+            tile_ref, swap_ref.at[n, slot], swap_send.at[n, d], swap_recv.at[n, d], target_of(shift, d)
+        )
+
+    def peak_copy(d, slot):
+        return remote(
+            tile_ref.at[pl.ds(0, 8)],
+            peak_ref.at[slot],
+            peak_send.at[d],
+            peak_recv.at[d],
+            lax.rem(me + d, groups),
+        )
+
+    def table_copy(n):
+        return pltpu.make_async_copy(source_tables[n], tables[n], table_sem.at[n])
+
+    def kernel_copies():
+        body = (pl.ds(0, rows_full), pl.ds(0, columns_full))
+        far = (pl.ds(rows_full, 8), pl.ds(0, columns_full + 128))
+        twin = 6 * local_planes
+        pieces = [(tensor_ref.at[n, *body], tensor_ref.at[twin + n, *body]) for n in (0, 3)]
+        pieces += [
+            (edge_out_ref, edge_ref),
+            (tensor_ref.at[pl.ds(0, 3), *far], tensor_ref.at[pl.ds(twin, 3), *far]),
+        ]
+        pieces += [(tensor_ref.at[n, *body], tensor_ref.at[twin + n, *body]) for n in (1, 2)]
+        return [
+            remote(src, dst, twin_send.at[n], twin_recv.at[n], partner)
+            for n, (src, dst) in enumerate(pieces)
+        ]
+
+    def pack_edges():
+        rows, columns = pl.ds(0, rows_full), pl.ds(columns_full, 128)
+        lane_pos = lax.broadcasted_iota(jnp.int32, (rows_full, 128), 1)
+        edge = tensor_ref[0, rows, columns]
+        for c in (1, 2):
+            edge = jnp.where(lane_pos == c, pltpu.roll(tensor_ref[c, rows, columns], c, 1), edge)
+        edge_out_ref[...] = edge
+
+    def unpack_edges():
+        rows, columns = pl.ds(0, rows_full), pl.ds(columns_full, 128)
+        edge = edge_ref[...]
+        for c in range(3):
+            tensor_ref[6 * local_planes + c, rows, columns] = pltpu.roll(edge, 128 - c, 1) if c else edge
 
     def last_copy(c):
         return remote(
@@ -520,7 +596,7 @@
                         if target == here:
                             held_ref[c, place, q, part, rows, :] = spectrum[k][part]
                         else:
-                            send_ref[c, kind, slot, q, part, rows, :] = spectrum[k][part]
+                            send_ref[3 if kind else c, slot, q, part, rows, :] = spectrum[k][part]
 
             row_loop(step)
 
@@ -789,6 +865,9 @@
 
     for c in range(3):
         film_copy(c).wait_recv()
+        if c > 0:
+            for slot in range(parts - 1):
+                plane_copy(c - 1, 1, slot).wait_send()
         transform_layers(c, 1)
         for kind in range(2):
             for slot in range(parts - 1):
@@ -835,11 +914,12 @@
             tensor_part(c, spec_ref.at[q], kernels, result_ref)
             gx = jnp.concatenate([gx_ref[0], gx_ref[0], gx_ref[1]], axis=1)
             gy = jnp.concatenate([gy_ref[0], gy_ref[0], gy_ref[1]], axis=0)
+            lines = [dot32(gx, three_limbs(result_ref[part], 0)) for part in range(2)]
+            cells = dot32(three_limbs(jnp.concatenate(lines, axis=0), 1), gy)
             for part in range(2):
-                lines = dot32(gx, three_limbs(result_ref[part], 0))
-                cells = dot32(three_limbs(lines, 1), gy)
                 for g in range(groups):
-                    held_ref[c, g, q, part] = cells[g * slab : (g + 1) * slab]
+                    start = part * rows_full + g * slab
+                    held_ref[c, g, q, part] = cells[start : start + slab]
             for kind in (1, 0):
                 for slot in range(parts - 1):
                     back_copy(c, q, kind, slot).start()
@@ -932,7 +1012,6 @@
 
         (peak,) = cell_loop(step, zeros(1))
         peaks.append(jnp.max(peak, axis=0, keepdims=True))
-        force_copy(i).start()
     peak = jnp.concatenate(peaks + [jnp.zeros((6, lane), jnp.float32)], axis=0)
     peak = jnp.broadcast_to(jnp.max(peak, axis=1, keepdims=True), (8, 128))
     tile_ref[0:8] = peak
@@ -947,8 +1026,6 @@
     moves = jnp.minimum(step_limit, rotation_limit / (jnp.sqrt(largest) + epsilon))
     energy = jnp.concatenate(energies[1:3], axis=0) / cell_count
     small_ref[...] = jnp.concatenate([moves[0:2], energy, jnp.zeros((4, 128), jnp.float32)], axis=0)
-    for i in range(2):
-        force_copy(i).wait()
     for d in range(1, groups):
         peak_copy(d, me).wait_send()
     for c in range(3):
@@ -956,7 +1033,8 @@
         last_copy(c).wait_send()
         for kind in range(2):
             for slot in range(parts - 1):
-                plane_copy(c, kind, slot).wait_send()
+                if kind == 0 or c == 2:
+                    plane_copy(c, kind, slot).wait_send()
                 for q in range(local_planes):
                     back_copy(c, q, kind, slot).wait_send()
 
@@ -1014,11 +1092,10 @@
         (3,) + film,
         (full_rows, 128),
         (full_rows, 128),
-        (3, 2, slots) + block,
+        (4, slots) + block,
         (3, 2, slots) + block,
         (3, groups) + block,
         (local_planes, 6, 2 * full_rows, 2 * column_count),
-        (2, 3) + film,
         (3,) + film,
         (3,) + film,
         (3,) + film,
@@ -1053,16 +1130,15 @@
         (3, groups),
         (groups,),
         (groups,),
-        (2,),
         (len(tables),),
     ]
     return pl.pallas_call(
         entry,
         in_specs=[anywhere, anywhere, pl.BlockSpec(memory_space=pltpu.SMEM)]
         + [anywhere] * len(tables),
-        out_specs=[anywhere, inside],
+        out_specs=[inside, inside],
         out_shape=[
-            jax.ShapeDtypeStruct(magnet.shape, jnp.float32),
+            pltpu.VMEM(magnet.shape, jnp.float32),
             jax.ShapeDtypeStruct((8, 128), jnp.float32),
         ],
         scratch_shapes=[pltpu.VMEM(t.shape, jnp.bfloat16) for t in tables]
@@ -1070,7 +1146,7 @@
         + [pltpu.VMEM((2, 2 * full_rows, 2 * column_count), jnp.float32)]
         + [signals(dims) for dims in semaphores],
         compiler_params=pltpu.CompilerParams(
-            vmem_limit_bytes=67043328, collective_id=0, has_side_effects=True
+            vmem_limit_bytes=67043328 - 4 * magnet.size, collective_id=0, has_side_effects=True
         ),
         cost_estimate=pl.CostEstimate(
             flops=4 * dots, bytes_accessed=4 * magnet.size * 4, transcendentals=0
@@ -1087,42 +1163,36 @@
     out_ref,
     energy_ref,
     cells_ref,
-    held_ref,
-    magnet_sem,
-    force_sem,
+    cells_sem,
     updated_sem,
     out_sem,
 ):
-    images, _, layer_count, slab, columns = magnet_ref.shape
-    pieces = magnet_sem.shape[1]
+    images, _, layer_count, slab, columns = cells_ref.shape
+    pieces = updated_sem.shape[1]
     layers = layer_count // pieces
 
-    def copy(src, dst, sem, i, k):
+    def piece_copy(src, dst, sem, i, k):
         part = pl.ds(k * layers, layers)
         return pltpu.make_async_copy(src.at[i, :, part], dst.at[i, :, part], sem.at[i, k])
 
+    def out_copy(i):
+        return pltpu.make_async_copy(force_ref.at[i], out_ref.at[i], out_sem.at[i])
+
     places = [(i, k) for i in range(images) for k in range(pieces)]
-    ahead = 4
-
-    def load(i, k):
-        copy(force_ref, held_ref, force_sem, i, k).start()
-        copy(magnet_ref, cells_ref, magnet_sem, i, k).start()
-
-    for i, k in places[:ahead]:
-        load(i, k)
+    for i, k in places:
+        piece_copy(magnet_ref, cells_ref, cells_sem, i, k).start()
+    for i in range(images):
+        out_copy(i).start()
     for n in range(images):
         energy_ref[n] = jnp.max(small_ref[n + 2 : n + 3, :])
     row_step = 8
     unrolled = min(4, slab // row_step)
     steps = slab // (unrolled * row_step)
-    for index, (i, k) in enumerate(places):
+    for i, k in places:
         move = jnp.broadcast_to(small_ref[i : i + 1, :], (row_step, 128))
         move = jnp.concatenate([move] * (columns // 128), axis=1)
-        copy(force_ref, held_ref, force_sem, i, k).wait()
-        copy(held_ref, out_ref, out_sem, i, k).start()
-        copy(magnet_ref, cells_ref, magnet_sem, i, k).wait()
-        for place in places[index + ahead : index + ahead + 1]:
-            load(*place)
+
+        piece_copy(magnet_ref, cells_ref, cells_sem, i, k).wait()
 
         def chunk(index, carry):
             z = k * layers + index // steps
@@ -1130,7 +1200,7 @@
                 start = (lax.rem(index, steps) * unrolled + n) * row_step
                 rows = pl.ds(pl.multiple_of(start, row_step), row_step)
                 moved = [
-                    cells_ref[i, c, z, rows, :] + move * held_ref[i, c, z, rows, :]
+                    cells_ref[i, c, z, rows, :] + move * force_ref[i, c, z, rows, :]
                     for c in range(3)
                 ]
                 inverse = lax.rsqrt(dot3(moved, moved))
@@ -1139,29 +1209,35 @@
             return carry
 
         lax.fori_loop(0, layers * steps, chunk, 0)
-        copy(cells_ref, updated_ref, updated_sem, i, k).start()
+        piece_copy(cells_ref, updated_ref, updated_sem, i, k).start()
+    for i in range(images):
+        out_copy(i).wait()
     for i, k in places:
-        copy(held_ref, out_ref, out_sem, i, k).wait()
-        copy(cells_ref, updated_ref, updated_sem, i, k).wait()
+        piece_copy(cells_ref, updated_ref, updated_sem, i, k).wait()
 
 
 def move_images(magnet, force, small):
     images, _, layer_count = magnet.shape[:3]
-    pieces = math.gcd(layer_count, 2)
+    pieces = math.gcd(layer_count, 4)
+    inside = pl.BlockSpec(memory_space=pltpu.VMEM)
     anywhere = pl.BlockSpec(memory_space=pl.ANY)
     return pl.pallas_call(
         move_kernel,
-        in_specs=[pl.BlockSpec(memory_space=pltpu.VMEM), anywhere, anywhere],
+        in_specs=[inside, anywhere, inside],
         out_specs=[anywhere, anywhere, pl.BlockSpec(memory_space=pltpu.SMEM)],
         out_shape=[
             jax.ShapeDtypeStruct(magnet.shape, jnp.float32),
             jax.ShapeDtypeStruct(magnet.shape, jnp.float32),
             jax.ShapeDtypeStruct((images,), jnp.float32),
         ],
-        scratch_shapes=[pltpu.VMEM(magnet.shape, jnp.float32)] * 2
-        + [pltpu.SemaphoreType.DMA((images, pieces))] * 4,
+        scratch_shapes=[
+            pltpu.VMEM(magnet.shape, jnp.float32),
+            pltpu.SemaphoreType.DMA((images, pieces)),
+            pltpu.SemaphoreType.DMA((images, pieces)),
+            pltpu.SemaphoreType.DMA((images,)),
+        ],
         name="move_kernel",
-    )(small, magnet, force)
+    )(small, magnet, pltpu.with_memory_space_constraint(force, pltpu.VMEM))
 
 
 def body(magnet, anisotropy, kernel):

time: 114 us -> 112 us (0.982)
  Pallas kernels: 114 us -> 111 us
    pallas_call x1, Pallas kernels: 107 us -> 105 us  [band_step(): pl.pallas_call(entry, in_specs=[anywhere, anywhere, pl.BlockSpec(memory_s...]
where the time goes in v6:
time: 112 us; the launch traced here: 111 us
  Pallas kernels  111 us (99%)
    pallas_call x1, Pallas kernels, band_step(): pl.pallas_call(entry, in_specs=[anywhere, anywhere, pl.BlockSpec(memory_s...  105 us
    pallas_call x1, Pallas kernels, move_images(): pl.pallas_call(move_kernel, in_specs=[inside, anywhere, inside], out_spec...  5.79 us

profile of v6, /device:TPU:0, one launch (start us, length us, event | category | flops | bytes accessed | tf_op | source)
XLA Modules:
  0.0 111.4 jit_solution(16451885185542100287)
XLA Ops:
  0.6 105.0 %band_kernel.1 = (f32[2,3,8,64,256]{4,3,2,1,0:T(8,128)S(1)}, f32[8,128]{1,0:T(8,128)}) custom-call(f32[2,3,8,64,256]{4,3,2,1,0:T(8,128)} %magnet_ref.3, f32[6,4,512,512]{3,2,1,0:T(8,128)} %kernel_ref.1, f32[64]{0:T(128)} %anisotropy_ref.1, bf16[2,256,512]{2,1,0:T(8,128)(2,1)} %constant.4.clone.refs_0_, bf16[2,512,256]{2,1,0:T(8,128)(2,1)} %constant.5.clone.refs_1_), custom_call_target="tpu_custom_call" | custom-call | flops 28991029248 | bytes 12582912 | tf_op jit(solution)/shard_map/band_kernel/pallas_call | solution.py:1135
  105.6 5.8 %move_kernel.1 = (f32[2,3,8,64,256]{4,3,2,1,0:T(8,128)}, f32[2,3,8,64,256]{4,3,2,1,0:T(8,128)}, f32[2]{0:T(128)}) custom-call(f32[8,128]{1,0:T(8,128)} %get-tuple-element.5.small_ref, f32[2,3,8,64,256]{4,3,2,1,0:T(8,128)} %magnet_ref.3, f32[2,3,8,64,256]{4,3,2,1,0:T(8,128)S(1)} %get-tuple-element.6.force_ref), custom_call_target="tpu_custom_call" | custom-call | tf_op jit(solution)/shard_map/move_kernel/pallas_call | solution.py:1224

commit v7 on v6

--- a/solution.py
+++ b/solution.py
@@ -277,9 +277,6 @@
     prior_ref,
     rim_out_ref,
     rim_ref,
-    present_ref,
-    ease_ref,
-    sums_ref,
     tile_ref,
     swap_ref,
     peak_ref,
@@ -308,6 +305,7 @@
     table_sem,
 ):
     fy_ref, fx_ref = tables[:2]
+    present_ref, ease_ref = [back_ref.at[0, 0, 0, 0, n] for n in range(2)]
     gx_ref, gy_ref = tables[:2] if len(tables) == 2 else tables[2:]
     groups, local_planes = held_ref.shape[1], held_ref.shape[2]
     slab, columns_full = held_ref.shape[4], held_ref.shape[5]
@@ -376,6 +374,98 @@
             magnet_ref.at[1 - half, c], film_ref.at[c], film_send.at[c], film_recv.at[c], partner
         )
 
+    def place_of(seat_index, kind):
+        return lax.rem((half + kind) * parts + seat_index, groups)
+
+    def plane_copy(c, kind, slot):
+        target = lax.rem(seat + 1 + slot, parts)
+        return remote(
+            send_ref.at[3 if kind else c, slot],
+            held_ref.at[c, place_of(seat, kind)],
+            plane_send.at[c, kind, slot],
+            plane_recv.at[c, kind, parts - 2 - slot],
+            half * parts + target,
+        )
+
+    def plane_arrival(c, kind, slot):
+        source = lax.rem(seat + 1 + slot, parts)
+        return remote(
+            send_ref.at[3 if kind else c, slot],
+            held_ref.at[c, place_of(source, kind)],
+            plane_send.at[c, kind, slot],
+            plane_recv.at[c, kind, slot],
+            half * parts + source,
+        )
+
+    def back_copy(c, q, kind, slot):
+        target = lax.rem(seat + 1 + slot, parts)
+        return remote(
+            held_ref.at[c, place_of(target, kind), q],
+            back_ref.at[c, kind, parts - 2 - slot, q],
+            back_send.at[c, q, kind, slot],
+            back_recv.at[c, q, kind, parts - 2 - slot],
+            half * parts + target,
+        )
+
+    def back_arrival(c, q, kind, slot):
+        source = lax.rem(seat + 1 + slot, parts)
+        return remote(
+            held_ref.at[c, place_of(source, kind), q],
+            back_ref.at[c, kind, slot, q],
+            back_send.at[c, q, kind, slot],
+            back_recv.at[c, q, kind, slot],
+            half * parts + source,
+        )
+
+    def last_copy(c):
+        return remote(
+            film_ref.at[c], arrive_ref.at[c], last_send.at[c], last_recv.at[c], partner
+        )
+
+    def ahead_copy():
+        return remote(
+            magnet_ref.at[1],
+            prior_ref,
+            image_send.at[0],
+            image_recv.at[0],
+            {"image": lax.rem(image + 1, images)},
+        )
+
+    def behind_copy():
+        return remote(
+            magnet_ref.at[0],
+            next_ref,
+            image_send.at[1],
+            image_recv.at[1],
+            {"image": lax.rem(image + images - 1, images)},
+        )
+
+    def rim_copy(side):
+        return remote(
+            rim_out_ref.at[side],
+            rim_ref.at[side],
+            rim_send.at[side],
+            rim_recv.at[side],
+            lax.rem(me + (1 if side == 0 else groups - 1), groups),
+        )
+
+    def swap_copy(n, shift, d, slot):
+        return remote(
+            tile_ref, swap_ref.at[n, slot], swap_send.at[n, d], swap_recv.at[n, d], target_of(shift, d)
+        )
+
+    def peak_copy(d, slot):
+        return remote(
+            tile_ref.at[pl.ds(0, 8)],
+            peak_ref.at[slot],
+            peak_send.at[d],
+            peak_recv.at[d],
+            lax.rem(me + d, groups),
+        )
+
+    def table_copy(n):
+        return pltpu.make_async_copy(source_tables[n], tables[n], table_sem.at[n])
+
     def kernel_copies():
         body = (pl.ds(0, rows_full), pl.ds(0, columns_full))
         far = (pl.ds(rows_full, 8), pl.ds(0, columns_full + 128))
@@ -404,179 +494,6 @@
         edge = edge_ref[...]
         for c in range(3):
             tensor_ref[6 * local_planes + c, rows, columns] = pltpu.roll(edge, 128 - c, 1) if c else edge
-
-    def place_of(seat_index, kind):
-        return lax.rem((half + kind) * parts + seat_index, groups)
-
-    def plane_copy(c, kind, slot):
-        target = lax.rem(seat + 1 + slot, parts)
-        return remote(
-            send_ref.at[3 if kind else c, slot],
-            held_ref.at[c, place_of(seat, kind)],
-            plane_send.at[c, kind, slot],
-            plane_recv.at[c, kind, parts - 2 - slot],
-            half * parts + target,
-        )
-
-    def plane_arrival(c, kind, slot):
-        source = lax.rem(seat + 1 + slot, parts)
-        return remote(
-            send_ref.at[3 if kind else c, slot],
-            held_ref.at[c, place_of(source, kind)],
-            plane_send.at[c, kind, slot],
-            plane_recv.at[c, kind, slot],
-            half * parts + source,
-        )
-
-    def back_copy(c, q, kind, slot):
-        target = lax.rem(seat + 1 + slot, parts)
-        return remote(
-            held_ref.at[c, place_of(target, kind), q],
-            back_ref.at[c, kind, parts - 2 - slot, q],
-            back_send.at[c, q, kind, slot],
-            back_recv.at[c, q, kind, parts - 2 - slot],
-            half * parts + target,
-        )
-
-    def back_arrival(c, q, kind, slot):
-        source = lax.rem(seat + 1 + slot, parts)
-        return remote(
-            held_ref.at[c, place_of(source, kind), q],
-            back_ref.at[c, kind, slot, q],
-            back_send.at[c, q, kind, slot],
-            back_recv.at[c, q, kind, slot],
-            half * parts + source,
-        )
-
-    def last_copy(c):
-        return remote(
-            film_ref.at[c], arrive_ref.at[c], last_send.at[c], last_recv.at[c], partner
-        )
-
-    def ahead_copy():
-        return remote(
-            magnet_ref.at[1],
-            prior_ref,
-            image_send.at[0],
-            image_recv.at[0],
-            {"image": lax.rem(image + 1, images)},
-        )
-
-    def behind_copy():
-        return remote(
-            magnet_ref.at[0],
-            next_ref,
-            image_send.at[1],
-            image_recv.at[1],
-            {"image": lax.rem(image + images - 1, images)},
-        )
-
-    def rim_copy(side):
-        return remote(
-            rim_out_ref.at[side],
-            rim_ref.at[side],
-            rim_send.at[side],
-            rim_recv.at[side],
-            lax.rem(me + (1 if side == 0 else groups - 1), groups),
-        )
-
-    def swap_copy(n, shift, d, slot):
-        return remote(
-            tile_ref, swap_ref.at[n, slot], swap_send.at[n, d], swap_recv.at[n, d], target_of(shift, d)
-        )
-
-    def peak_copy(d, slot):
-        return remote(
-            tile_ref.at[pl.ds(0, 8)],
-            peak_ref.at[slot],
-            peak_send.at[d],
-            peak_recv.at[d],
-            lax.rem(me + d, groups),
-        )
-
-    def table_copy(n):
-        return pltpu.make_async_copy(source_tables[n], tables[n], table_sem.at[n])
-
-    def kernel_copies():
-        body = (pl.ds(0, rows_full), pl.ds(0, columns_full))
-        far = (pl.ds(rows_full, 8), pl.ds(0, columns_full + 128))
-        twin = 6 * local_planes
-        pieces = [(tensor_ref.at[n, *body], tensor_ref.at[twin + n, *body]) for n in (0, 3)]
-        pieces += [
-            (edge_out_ref, edge_ref),
-            (tensor_ref.at[pl.ds(0, 3), *far], tensor_ref.at[pl.ds(twin, 3), *far]),
-        ]
-        pieces += [(tensor_ref.at[n, *body], tensor_ref.at[twin + n, *body]) for n in (1, 2)]
-        return [
-            remote(src, dst, twin_send.at[n], twin_recv.at[n], partner)
-            for n, (src, dst) in enumerate(pieces)
-        ]
-
-    def pack_edges():
-        rows, columns = pl.ds(0, rows_full), pl.ds(columns_full, 128)
-        lane_pos = lax.broadcasted_iota(jnp.int32, (rows_full, 128), 1)
-        edge = tensor_ref[0, rows, columns]
-        for c in (1, 2):
-            edge = jnp.where(lane_pos == c, pltpu.roll(tensor_ref[c, rows, columns], c, 1), edge)
-        edge_out_ref[...] = edge
-
-    def unpack_edges():
-        rows, columns = pl.ds(0, rows_full), pl.ds(columns_full, 128)
-        edge = edge_ref[...]
-        for c in range(3):
-            tensor_ref[6 * local_planes + c, rows, columns] = pltpu.roll(edge, 128 - c, 1) if c else edge
-
-    def last_copy(c):
-        return remote(
-            film_ref.at[c], arrive_ref.at[c], last_send.at[c], last_recv.at[c], partner
-        )
-
-    def ahead_copy():
-        return remote(
-            magnet_ref.at[1],
-            prior_ref,
-            image_send.at[0],
-            image_recv.at[0],
-            {"image": lax.rem(image + 1, images)},
-        )
-
-    def behind_copy():
-        return remote(
-            magnet_ref.at[0],
-            next_ref,
-            image_send.at[1],
-            image_recv.at[1],
-            {"image": lax.rem(image + images - 1, images)},
-        )
-
-    def rim_copy(side):
-        return remote(
-            rim_out_ref.at[side],
-            rim_ref.at[side],
-            rim_send.at[side],
-            rim_recv.at[side],
-            lax.rem(me + (1 if side == 0 else groups - 1), groups),
-        )
-
-    def swap_copy(n, shift, d, slot):
-        return remote(
-            tile_ref, swap_ref.at[n, slot], swap_send.at[n, d], swap_recv.at[n, d], target_of(shift, d)
-        )
-
-    def peak_copy(d, slot):
-        return remote(
-            tile_ref.at[pl.ds(0, 8)],
-            peak_ref.at[slot],
-            peak_send.at[d],
-            peak_recv.at[d],
-            lax.rem(me + d, groups),
-        )
-
-    def table_copy(n):
-        return pltpu.make_async_copy(source_tables[n], tables[n], table_sem.at[n])
-
-    def force_copy(i):
-        return pltpu.make_async_copy(field_ref.at[i], force_ref.at[i], force_sem.at[i])
 
     def transform_layers(c, kind):
         place = place_of(seat, kind)
@@ -728,6 +645,12 @@
 
         return lax.fori_loop(0, layer_count * steps, chunk, carry)
 
+    def get_sum(i, k):
+        return result_ref[i, row_step * k : row_step * (k + 1), 0:lane]
+
+    def put_sum(i, k, value):
+        result_ref[i, row_step * k : row_step * (k + 1), 0:lane] = value
+
     def zeros(count):
         return tuple(jnp.zeros((row_step, lane), jnp.float32) for _ in range(count))
 
@@ -789,7 +712,7 @@
 
             totals = cell_loop(step, zeros(4))
             for k in range(4):
-                sums_ref[i, k + 1] = totals[k]
+                put_sum(i, k + 1, totals[k])
 
     def field_sums(i, c, arrived):
         def step(z, start, carry):
@@ -808,7 +731,7 @@
 
         totals = cell_loop(step, zeros(3))
         for k, slot in enumerate((0, 5, 6)):
-            sums_ref[i, slot] = totals[k] if c == 0 else sums_ref[i, slot] + totals[k]
+            put_sum(i, slot, totals[k] if c == 0 else get_sum(i, slot) + totals[k])
 
     barrier = pltpu.get_barrier_semaphore()
     for n, shift, d in routes:
@@ -874,20 +797,21 @@
                 plane_arrival(c, kind, slot).wait_recv()
 
         def forward(i, carry):
-            q = i
             fy = jnp.concatenate([fy_ref[0], fy_ref[0], fy_ref[1]], axis=0)
             fx = jnp.concatenate([fx_ref[0], fx_ref[0], fx_ref[1]], axis=1)
+            places = [(width * i + n, part) for n in range(width) for part in range(2)]
             cells = jnp.concatenate(
-                [held_ref[c, g, q, part] for part in range(2) for g in range(groups)], axis=0
+                [held_ref[c, g, q, part] for q, part in places for g in range(groups)], axis=0
             )
             lines = dot32(three_limbs(cells, 1), fy)
-            for part in range(2):
+            for n, (q, part) in enumerate(places):
                 spec_ref[q, 2 * c + part] = dot32(
-                    fx, three_limbs(lines[part * rows_full : (part + 1) * rows_full], 0)
+                    fx, three_limbs(lines[n * rows_full : (n + 1) * rows_full], 0)
                 )
             return carry
 
-        lax.fori_loop(0, local_planes, forward, 0)
+        width = math.gcd(local_planes, 2)
+        lax.fori_loop(0, local_planes // width, forward, 0)
         if c == 0:
             wait_rims()
         if c < 2:
@@ -943,7 +867,7 @@
         field_sums(1 - half, c, True)
 
     rows = [
-        jnp.sum(sums_ref[i, k], axis=0, keepdims=True) for i in range(2) for k in range(7)
+        jnp.sum(get_sum(i, k), axis=0, keepdims=True) for i in range(2) for k in range(7)
     ] + [jnp.zeros((1, lane), jnp.float32)] * 2
     tile = jnp.sum(jnp.concatenate(rows, axis=0), axis=1, keepdims=True)
     tile_ref[...] = jnp.broadcast_to(tile, tile_ref.shape)
@@ -1101,9 +1025,6 @@
         (3,) + film,
         (2, 2, 3, layer_count, column_count),
         (2, 2, 3, layer_count, column_count),
-        slab,
-        slab,
-        (2, 7, 8, column_count),
         (16, 128),
         (3, groups, 16, 128),
         (groups, 8, 128),

time: 112 us -> 111 us (level)
  no operation moved by 1% of the time
where the time goes in v7:
time: 111 us
  Pallas kernels  110 us (99%)
    pallas_call x1, Pallas kernels, band_step(): pl.pallas_call(entry, in_specs=[anywhere, anywhere, pl.BlockSpec(memory_s...  104 us
    pallas_call x1, Pallas kernels, move_images(): pl.pallas_call(move_kernel, in_specs=[inside, anywhere, inside], out_spec...  5.79 us

profile of v7, /device:TPU:0, one launch (start us, length us, event | category | flops | bytes accessed | tf_op | source)
XLA Modules:
  0.0 110.8 jit_solution(13934974245218119089)
XLA Ops:
  0.6 104.4 %band_kernel.1 = (f32[2,3,8,64,256]{4,3,2,1,0:T(8,128)S(1)}, f32[8,128]{1,0:T(8,128)}) custom-call(f32[2,3,8,64,256]{4,3,2,1,0:T(8,128)} %magnet_ref.3, f32[6,4,512,512]{3,2,1,0:T(8,128)} %kernel_ref.1, f32[64]{0:T(128)} %anisotropy_ref.1, bf16[2,256,512]{2,1,0:T(8,128)(2,1)} %constant.4.clone.refs_0_, bf16[2,512,256]{2,1,0:T(8,128)(2,1)} %constant.5.clone.refs_1_), custom_call_target="tpu_custom_call" | custom-call | flops 28991029248 | bytes 12582912 | tf_op jit(solution)/shard_map/band_kernel/pallas_call | solution.py:1056
  105.0 5.8 %move_kernel.1 = (f32[2,3,8,64,256]{4,3,2,1,0:T(8,128)}, f32[2,3,8,64,256]{4,3,2,1,0:T(8,128)}, f32[2]{0:T(128)}) custom-call(f32[8,128]{1,0:T(8,128)} %get-tuple-element.5.small_ref, f32[2,3,8,64,256]{4,3,2,1,0:T(8,128)} %magnet_ref.3, f32[2,3,8,64,256]{4,3,2,1,0:T(8,128)S(1)} %get-tuple-element.6.force_ref), custom_call_target="tpu_custom_call" | custom-call | tf_op jit(solution)/shard_map/move_kernel/pallas_call | solution.py:1145
